TPU v7x, 128 devices: a whole 4x4x4 slice. The times are simulated.
128 devices in a mesh: tp: 2 (over core), cp: 64 (over z, y, x).
Axes of the slice: x: 4, y: 4, z: 4, core: 2. Of those that a mesh axis runs over, the one named last changes fastest.
Arguments:
- hidden: bfloat16 [2, 8192, 2048], P(None, 'cp')
- grad_out: bfloat16 [2, 8192, 2048], P(None, 'cp')
- w_query: bfloat16 [2048, 16, 128], P(None, 'tp')
- w_key: bfloat16 [2048, 128], replicated
- w_value: bfloat16 [2048, 128], replicated
- w_out: bfloat16 [16, 128, 2048], P('tp')
Outputs:
- output 1: bfloat16 [2, 8192, 2048], P(None, 'cp')
- output 2: bfloat16 [2, 8192, 2048], P(None, 'cp')
- output 3: float32 [2048, 16, 128], P(None, 'tp')
- output 4: float32 [2048, 128], replicated
- output 5: float32 [2048, 128], replicated
- output 6: float32 [16, 128, 2048], P('tp')
All inputs are finite; a program needn't handle non-finite values.
Results may differ from a plain program's by a relative error of at most 0.0101215.
Values are sent between devices in bfloat16 or wider.
A program may use at most 1 GiB of HBM per device.

v0:
```python
import jax
import jax.numpy as jnp
from jax import lax
from jax.sharding import PartitionSpec as P

ROPE_BASE = 10000.0


def rope_tables(positions, head_dim):
    half_dim = head_dim // 2
    inv_freq = 1.0 / jnp.power(ROPE_BASE, jnp.arange(half_dim, dtype=jnp.float32) * (2.0 / head_dim))
    angles = positions.astype(jnp.float32)[:, None] * inv_freq[None, :]
    return jnp.cos(angles), jnp.sin(angles)


def rotate(rot_in, cos_tab, sin_tab):
    half_dim = rot_in.shape[-1] // 2
    low_half = rot_in[..., :half_dim]
    high_half = rot_in[..., half_dim:]
    return jnp.concatenate([low_half * cos_tab - high_half * sin_tab, high_half * cos_tab + low_half * sin_tab], axis=-1)


def unrotate(rot_in, cos_tab, sin_tab):
    half_dim = rot_in.shape[-1] // 2
    low_half = rot_in[..., :half_dim]
    high_half = rot_in[..., half_dim:]
    return jnp.concatenate([low_half * cos_tab + high_half * sin_tab, high_half * cos_tab - low_half * sin_tab], axis=-1)


def pair_scores(queries, key_blk, q_start, k_start):
    scores = jnp.einsum("bhqe,bke->bhqk", queries, key_blk, preferred_element_type=jnp.float32)
    q_pos = q_start + jnp.arange(queries.shape[2])
    k_pos = k_start + jnp.arange(key_blk.shape[1])
    allowed = k_pos[None, :] <= q_pos[:, None]
    return jnp.where(allowed, scores, -jnp.inf)


def forward_update(queries, kv_blk, q_start, k_start, soft_stats):
    run_max, run_sum, run_acc = soft_stats
    scores = pair_scores(queries, kv_blk[:, 0], q_start, k_start)
    new_max = jnp.maximum(run_max, jnp.max(scores, axis=-1))
    rescale = jnp.exp(run_max - new_max)
    weights = jnp.exp(scores - new_max[..., None])
    new_sum = run_sum * rescale + jnp.sum(weights, axis=-1)
    new_acc = run_acc * rescale[..., None] + jnp.einsum("bhqk,bke->bhqe", weights.astype(jnp.bfloat16), kv_blk[:, 1], preferred_element_type=jnp.float32)
    return new_max, new_sum, new_acc


def backward_update(queries, d_out, row_lse, row_delta, kv_blk, q_start, k_start):
    scores = pair_scores(queries, kv_blk[:, 0], q_start, k_start)
    prob_blk = jnp.exp(scores - row_lse[..., None])
    d_prob = jnp.einsum("bhqe,bke->bhqk", d_out, kv_blk[:, 1], preferred_element_type=jnp.float32)
    d_score = (prob_blk * (d_prob - row_delta[..., None])).astype(jnp.bfloat16)
    dq_part = jnp.einsum("bhqk,bke->bhqe", d_score, kv_blk[:, 0], preferred_element_type=jnp.float32)
    dk_part = jnp.einsum("bhqk,bhqe->bke", d_score, queries, preferred_element_type=jnp.float32)
    dv_part = jnp.einsum("bhqk,bhqe->bke", prob_blk.astype(jnp.bfloat16), d_out, preferred_element_type=jnp.float32)
    return dq_part, jnp.stack([dk_part, dv_part], axis=1)


def solution(mesh):
    cp_size = mesh.shape["cp"]
    shift_pairs = [(src_idx, (src_idx + 1) % cp_size) for src_idx in range(cp_size)]

    def local_program(hidden, grad_out, w_query, w_key, w_value, w_out):
        n_batch, block_len = hidden.shape[0], hidden.shape[1]
        n_local = w_query.shape[1]
        head_dim = w_key.shape[1]
        q_scale = head_dim ** -0.5
        cp_idx = lax.axis_index("cp")
        q_start = cp_idx * block_len
        cos_tab, sin_tab = rope_tables(q_start + jnp.arange(block_len), head_dim)
        q_pre = jnp.einsum("bsd,dhe->bhse", hidden, w_query, preferred_element_type=jnp.float32)
        queries = (rotate(q_pre, cos_tab, sin_tab) * q_scale).astype(jnp.bfloat16)
        key_pre = jnp.einsum("bsd,de->bse", hidden, w_key, preferred_element_type=jnp.float32)
        key_loc = rotate(key_pre, cos_tab, sin_tab).astype(jnp.bfloat16)
        val_loc = jnp.einsum("bsd,de->bse", hidden, w_value, preferred_element_type=jnp.float32).astype(jnp.bfloat16)
        kv_loc = jnp.stack([key_loc, val_loc], axis=1)

        def fwd_compute(step_idx, kv_blk, soft_stats):
            k_start = ((cp_idx - step_idx) % cp_size) * block_len
            return lax.cond(step_idx <= cp_idx, lambda stats_in: forward_update(queries, kv_blk, q_start, k_start, stats_in), lambda stats_in: stats_in, soft_stats)

        def fwd_body(step_idx, loop_state):
            kv_blk, soft_stats = loop_state
            soft_stats = fwd_compute(step_idx, kv_blk, soft_stats)
            return lax.ppermute(kv_blk, "cp", shift_pairs), soft_stats

        stats_init = (jnp.full((n_batch, n_local, block_len), -jnp.inf, jnp.float32), jnp.zeros((n_batch, n_local, block_len), jnp.float32), jnp.zeros((n_batch, n_local, block_len, head_dim), jnp.float32))
        kv_blk, soft_stats = lax.fori_loop(0, cp_size - 1, fwd_body, (kv_loc, stats_init))
        run_max, run_sum, run_acc = fwd_compute(cp_size - 1, kv_blk, soft_stats)
        attn_heads = (run_acc / run_sum[..., None]).astype(jnp.bfloat16)
        row_lse = run_max + jnp.log(run_sum)
        out_part = jnp.einsum("cirf,ife->cre", attn_heads, w_out, preferred_element_type=jnp.float32)
        attn_out = lax.psum(out_part, "tp").astype(jnp.bfloat16)
        d_out = jnp.einsum("cre,ife->cirf", grad_out, w_out, preferred_element_type=jnp.float32).astype(jnp.bfloat16)
        row_delta = jnp.einsum("bhqe,bhqe->bhq", d_out, attn_heads, preferred_element_type=jnp.float32)

        def bwd_compute(step_idx, kv_blk, dkv_blk, dq_acc):
            k_start = ((cp_idx - step_idx) % cp_size) * block_len

            def active(acc_pair):
                dq_in, dkv_in = acc_pair
                dq_part, dkv_part = backward_update(queries, d_out, row_lse, row_delta, kv_blk, q_start, k_start)
                return dq_in + dq_part, dkv_in + dkv_part

            return lax.cond(step_idx <= cp_idx, active, lambda acc_pair: acc_pair, (dq_acc, dkv_blk))

        def bwd_body(step_idx, loop_state):
            kv_blk, dkv_blk, dq_acc = loop_state
            dq_acc, dkv_blk = bwd_compute(step_idx, kv_blk, dkv_blk, dq_acc)
            kv_blk = lax.ppermute(kv_blk, "cp", shift_pairs)
            dkv_blk = lax.ppermute(dkv_blk, "cp", shift_pairs)
            return kv_blk, dkv_blk, dq_acc

        dkv_init = jnp.zeros((n_batch, 2, block_len, head_dim), jnp.float32)
        dq_init = jnp.zeros((n_batch, n_local, block_len, head_dim), jnp.float32)
        kv_blk, dkv_blk, dq_acc = lax.fori_loop(0, cp_size - 1, bwd_body, (kv_loc, dkv_init, dq_init))
        dq_acc, dkv_blk = bwd_compute(cp_size - 1, kv_blk, dkv_blk, dq_acc)
        dkv_blk = lax.ppermute(dkv_blk, "cp", shift_pairs)
        dkv_full = lax.psum(dkv_blk, "tp")
        dq_pre = (unrotate(dq_acc, cos_tab, sin_tab) * q_scale).astype(jnp.bfloat16)
        dk_pre = unrotate(dkv_full[:, 0], cos_tab, sin_tab).astype(jnp.bfloat16)
        dv_pre = dkv_full[:, 1].astype(jnp.bfloat16)
        d_w_query = lax.psum(jnp.einsum("cre,cirf->eif", hidden, dq_pre, preferred_element_type=jnp.float32), "cp")
        d_w_out = lax.psum(jnp.einsum("cirf,cre->ife", attn_heads, grad_out, preferred_element_type=jnp.float32), "cp")
        d_w_key = lax.psum(jnp.einsum("cre,crf->ef", hidden, dk_pre, preferred_element_type=jnp.float32), "cp")
        d_w_value = lax.psum(jnp.einsum("cre,crf->ef", hidden, dv_pre, preferred_element_type=jnp.float32), "cp")
        dh_heads = lax.psum(jnp.einsum("cirf,eif->cre", dq_pre, w_query, preferred_element_type=jnp.float32), "tp")
        dh_kv = jnp.einsum("crf,ef->cre", dk_pre, w_key, preferred_element_type=jnp.float32) + jnp.einsum("crf,ef->cre", dv_pre, w_value, preferred_element_type=jnp.float32)
        d_hidden = (dh_heads + dh_kv).astype(jnp.bfloat16)
        return attn_out, d_hidden, d_w_query, d_w_key, d_w_value, d_w_out

    row_spec = P(None, "cp", None)
    return jax.shard_map(local_program, mesh=mesh, in_specs=(row_spec, row_spec, P(None, "tp", None), P(), P(), P("tp", None, None)), out_specs=(row_spec, row_spec, P(None, "tp", None), P(), P(), P("tp", None, None)), check_vma=False)
```

profile of v0, /device:TPU:1, one launch (start us, length us, event | category | flops | bytes accessed | tf_op | source)
XLA Modules:
  0.0 2025.2 jit_solution(5157676376203793792)
XLA Ops:
  20.9 649.4 %while.40 = (s32[]{:T(128)}, bf16[2,2,128,128]{3,2,0,1:T(8,128)(2,1)S(1)}, f32[2,8,128]{2,1,0:T(8,128)S(1)}, f32[2,8,128]{2,1,0:T(8,128)S(1)}, f32[2,8,128,128]{...) while((s32[]{:T(128)}, ...), condition=%wide.region_5.6_spmd, body=%wide.region_0.5_spmd.sunk | while | flops 136335632 | bytes 6850976 | solution.py:89
  115.3 10.8 collective-permute-done
  218.0 10.8 collective-permute-done
  320.8 10.8 collective-permute-done
  423.5 10.8 collective-permute-done
  526.3 10.8 collective-permute-done
  629.0 10.8 collective-permute-done
  672.8 925.4 %while.41 = (s32[]{:T(128)}, bf16[2,2,128,128]{3,2,0,1:T(8,128)(2,1)}, f32[2,2,128,128]{3,2,0,1:T(8,128)S(1)}, f32[2,8,128,128]{3,2,1,0:T(8,128)S(1)}, s32[]{:T(...) while((s32[]{:T(128)}, ...), condition=%wide.region_14.15_spmd, body=%wide.region_11.14_spmd.sunk | while | flops 337527040 | bytes 12569040 | solution.py:117
  675.9 12.3 collective-permute-done.2
  690.5 10.6 collective-permute-done.2
  703.5 10.6 collective-permute-done.2
  716.4 10.6 collective-permute-done.2
  729.4 10.9 collective-permute-done.2
  744.0 10.6 collective-permute-done.2
  757.0 10.6 collective-permute-done.2
  770.0 10.6 collective-permute-done.2
  782.9 10.6 collective-permute-done.2
  795.9 11.1 collective-permute-done.2
  809.3 12.1 collective-permute-done.2
  823.7 12.6 collective-permute-done.2
  838.6 13.3 collective-permute-done.2
  854.2 13.9 collective-permute-done.2
  870.5 13.9 collective-permute-done.2
  887.5 13.8 collective-permute-done.2
  905.0 13.0 collective-permute-done.2
  921.7 11.8 collective-permute-done.2
  937.2 10.6 collective-permute-done.2
  977.4 10.6 collective-permute-done.2
  990.4 10.6 collective-permute-done.2
  1016.3 11.8 collective-permute-done.2
  1030.4 12.1 collective-permute-done.2
  1044.8 12.6 collective-permute-done.2
  1059.7 13.3 collective-permute-done.2
  1075.2 13.9 collective-permute-done.2
  1091.5 13.9 collective-permute-done.2
  1108.5 13.8 collective-permute-done.2
  1126.0 13.0 collective-permute-done.2
  1142.7 11.8 collective-permute-done.2
  1158.3 10.6 collective-permute-done.2
  1172.6 10.6 collective-permute-done.2
  1185.6 10.6 collective-permute-done.2
  1237.4 11.7 collective-permute-done.2
  1251.5 12.0 collective-permute-done.2
  1265.8 12.5 collective-permute-done.2
  1280.6 13.2 collective-permute-done.2
  1296.1 13.8 collective-permute-done.2
  1312.4 13.9 collective-permute-done.2
  1329.3 13.9 collective-permute-done.2
  1346.8 13.1 collective-permute-done.2
  1363.6 11.9 collective-permute-done.2
  1379.3 10.6 collective-permute-done.2
  1419.6 10.6 collective-permute-done.2
  1432.6 10.6 collective-permute-done.2
  1458.5 11.7 collective-permute-done.2
  1472.5 11.9 collective-permute-done.2
  1486.7 12.3 collective-permute-done.2
  1501.4 12.9 collective-permute-done.2
  1516.6 13.5 collective-permute-done.2
  1532.6 13.9 collective-permute-done.2
  1549.2 13.9 collective-permute-done.2
  1566.4 13.3 collective-permute-done.2
  1583.4 12.1 collective-permute-done.2
  1621.5 144.2 %all-reduce.8.cloned.1.call-done = (f32[2,128,2048]{2,1,0:T(8,128)}, f32[2,2,128,128]{2,3,0,1:T(8,128)}) async-done(((f32[2,128,2048]{2,1,0:T(8,128)}, f32[2,2,128,128]{2,3,0,1:T(8,128)}), (f32[2,128,2048]{2,1,0:T(8,128)}, f32[2,2,128,128]{2,3,0,1:T(8,128)})) %all-reduce.8.cloned.1.call-update) | async-done | bytes 2359312 | tf_op jit(solution)/shard_map/psum | solution.py:128
  1788.6 209.8 %all-reduce.6.cloned.1.call-done = (f32[2048,8,128]{0,2,1:T(8,128)}, f32[2048,128]{0,1:T(8,128)}, f32[2048,128]{0,1:T(8,128)}, f32[8,128,2048]{2,1,0:T(8,128)}) async-done(((f32[2048,8,128]{0,2,1:T(8,128)}, f32[2048,128]{0,1:T(8,128)}, f32[2048,128]{0,1:T(8,128)}, f32[8,128,2048]{2,1,0:T(8,128)}), (f32[2048,8,128]{0,2,1:T(8,128)}, f32[2048,128]{0,1:T(8,128)}, f32[2048,128]{0,1:T(8,128)}, ...) | async-done | bytes 18874384 | tf_op jit(solution)/shard_map/psum | solution.py:124
  (733 shorter events, 941.7 us)
Async XLA Ops:
  7.2 1758.5 %all-reduce.8.cloned.1.call-start = ((), (), s32[]{:S(2)}) async-start(), calls=%async_computation.1 | async-start | bytes 4718592 | tf_op jit(solution)/shard_map/psum | solution.py:128
  675.8 13.8 collective-permute-start.1
  729.4 13.8 collective-permute-start.1
  809.3 13.5 collective-permute-start.1
  823.7 12.6 collective-permute-start.2
  823.7 14.0 collective-permute-start.1
  838.6 13.3 collective-permute-start.2
  838.6 14.7 collective-permute-start.1
  854.2 13.9 collective-permute-start.2
  854.2 15.4 collective-permute-start.1
  870.5 13.9 collective-permute-start.2
  870.5 16.1 collective-permute-start.1
  887.5 13.8 collective-permute-start.2
  887.5 16.6 collective-permute-start.1
  905.0 13.0 collective-permute-start.2
  905.0 15.8 collective-permute-start.1
  921.7 14.6 collective-permute-start.1
  937.2 13.4 collective-permute-start.1
  1016.3 13.2 collective-permute-start.1
  1030.4 13.5 collective-permute-start.1
  1044.8 12.6 collective-permute-start.2
  1044.8 14.0 collective-permute-start.1
  1059.6 13.3 collective-permute-start.2
  1059.6 14.7 collective-permute-start.1
  1075.2 13.9 collective-permute-start.2
  1075.2 15.4 collective-permute-start.1
  1091.5 13.9 collective-permute-start.2
  1091.5 16.1 collective-permute-start.1
  1108.5 13.8 collective-permute-start.2
  1108.5 16.6 collective-permute-start.1
  1126.0 13.0 collective-permute-start.2
  1126.0 15.8 collective-permute-start.1
  1142.7 14.6 collective-permute-start.1
  1158.3 13.4 collective-permute-start.1
  1237.4 13.1 collective-permute-start.1
  1251.5 13.4 collective-permute-start.1
  1265.8 13.9 collective-permute-start.1
  1280.6 13.2 collective-permute-start.2
  1280.6 14.6 collective-permute-start.1
  1296.1 13.8 collective-permute-start.2
  1296.1 15.3 collective-permute-start.1
  1312.3 13.9 collective-permute-start.2
  1312.4 16.0 collective-permute-start.1
  1329.3 13.9 collective-permute-start.2
  1329.3 16.6 collective-permute-start.1
  1346.8 13.1 collective-permute-start.2
  1346.8 15.9 collective-permute-start.1
  1363.6 14.7 collective-permute-start.1
  1379.3 13.5 collective-permute-start.1
  1458.5 13.1 collective-permute-start.1
  1472.5 13.3 collective-permute-start.1
  1486.7 13.7 collective-permute-start.1
  1501.4 12.9 collective-permute-start.2
  1501.4 14.3 collective-permute-start.1
  1516.6 13.5 collective-permute-start.2
  1516.6 15.0 collective-permute-start.1
  1532.6 13.9 collective-permute-start.2
  1532.6 15.7 collective-permute-start.1
  1549.2 13.9 collective-permute-start.2
  1549.2 16.3 collective-permute-start.1
  1566.4 13.3 collective-permute-start.2
  1566.4 16.1 collective-permute-start.1
  1583.4 14.9 collective-permute-start.1
  1612.0 386.4 %all-reduce.6.cloned.1.call-start = ((), (), s32[]{:S(2)}) async-start(), calls=%async_computation | async-start | bytes 37748736 | tf_op jit(solution)/shard_map/psum | solution.py:124
  (144 other events, 1452.0 us)
Sparse Core Ops, SparseCore 0:
  1612.1 153.4 all-reduce.7
  1772.5 225.8 all-reduce.5
where the time goes:
time: 2040 us; the launch traced here: 2030 us
  waiting for transfers between devices  1770 us (87%)
  local copies, waits for them, and re-layouts  185 us (9%)
  matrix products  39.8 us (2%)
    ppermute x63, waiting for transfers between devices, bwd_body(): dkv_blk = lax.ppermute(dkv_blk, 'cp', shift_pairs)  752 us
    ppermute x63, waiting for transfers between devices, fwd_body(): return (lax.ppermute(kv_blk, 'cp', shift_pairs), soft_stats)  603 us
    psum x1, waiting for transfers between devices, local_program(): lax.psum(jnp.einsum('cre,cirf->eif', hidden, dq_pre, preferred_element_ty...  210 us
    psum x1, waiting for transfers between devices, local_program(): lax.psum(jnp.einsum('cirf,eif->cre', dq_pre, w_query, preferred_element_t...  144 us
    another operation x129, local copies, waits for them, and re-layouts  98.8 us
    while x63, local copies, waits for them, and re-layouts  59.9 us
    ppermute x63, waiting for transfers between devices, bwd_body(): kv_blk = lax.ppermute(kv_blk, 'cp', shift_pairs)  53.8 us
  transfers between devices with their start and end apart: 192, of which 192 were waited for; matrix products, arithmetic and copies ran while one was open for 4% of the time, Pallas kernels for 0%

commit v1 on v0

v1 whole, which is shorter than its diff:
```python
import jax
import jax.numpy as jnp
from jax import lax
from jax.experimental import pallas as pl
from jax.experimental.pallas import tpu as pltpu
from jax.sharding import PartitionSpec as P

ROPE_BASE = 10000.0
BLK = 128
TILE = 512
COLS = 256
F32 = jnp.float32
BF16 = jnp.bfloat16


def rope_tables(positions, head_dim):
    half_dim = head_dim // 2
    inv_freq = 1.0 / jnp.power(ROPE_BASE, jnp.arange(half_dim, dtype=F32) * (2.0 / head_dim))
    angles = positions.astype(F32)[:, None] * inv_freq[None, :]
    return jnp.cos(angles), jnp.sin(angles)


def rotate(rot_in, cos_tab, sin_tab):
    half_dim = rot_in.shape[-1] // 2
    low_half = rot_in[..., :half_dim]
    high_half = rot_in[..., half_dim:]
    return jnp.concatenate([low_half * cos_tab - high_half * sin_tab, high_half * cos_tab + low_half * sin_tab], axis=-1)


def unrotate(rot_in, cos_tab, sin_tab):
    return rotate(rot_in, cos_tab, -sin_tab)


def dot(a, b):
    return jnp.dot(a, b, preferred_element_type=F32)


def dot_ta(a, b):
    return lax.dot_general(a, b, (((0,), (0,)), ((), ())), preferred_element_type=F32)


def causal_mask(k_start, q_start, cols):
    k_pos = k_start + lax.broadcasted_iota(jnp.int32, (TILE, cols), 0)
    q_pos = q_start + lax.broadcasted_iota(jnp.int32, (TILE, cols), 1) % BLK
    return k_pos <= q_pos


def fwd_kernel(piece_ref, kv_ref, q_ref, o_ref, lse_ref, qt_scr, acc_scr, m_scr, l_scr):
    n_groups, n_cols, e_dim = q_ref.shape
    per_tile = TILE // BLK
    for grp in range(n_groups):
        piece = piece_ref[grp]
        qt_scr[...] = q_ref[grp].T
        acc_scr[...] = jnp.zeros_like(acc_scr)
        m_scr[...] = jnp.full_like(m_scr, -jnp.inf)
        l_scr[...] = jnp.zeros_like(l_scr)

        def tile_step(tile_idx, masked):
            row0 = pl.multiple_of(tile_idx * TILE, TILE)
            k_t = kv_ref[pl.ds(row0, TILE), :e_dim]
            v_t = kv_ref[pl.ds(row0, TILE), e_dim:]
            for c0 in range(0, n_cols, COLS):
                cs = slice(c0, c0 + COLS)
                s = dot(k_t, qt_scr[:, cs])
                if masked:
                    s = jnp.where(causal_mask(row0, piece * BLK, COLS), s, -jnp.inf)
                m_old = m_scr[:, cs]
                m_new = jnp.maximum(m_old, jnp.max(s, axis=0, keepdims=True))
                p = jnp.exp(s - m_new)
                alpha = jnp.exp(m_old - m_new)
                m_scr[:, cs] = m_new
                l_scr[:, cs] = l_scr[:, cs] * alpha + jnp.sum(p, axis=0, keepdims=True)
                acc_scr[:, cs] = acc_scr[:, cs] * alpha + dot_ta(v_t, p.astype(BF16))

        n_full = piece // per_tile

        def body(tile_idx, carry):
            tile_step(tile_idx, False)
            return carry

        lax.fori_loop(0, n_full, body, 0)
        tile_step(n_full, True)
        o_ref[grp] = (acc_scr[...] / l_scr[...]).T.astype(BF16)
        lse_ref[grp] = m_scr[...] + jnp.log(l_scr[...])


def bwd_kernel(piece_ref, kv_ref, q_ref, do_ref, o_ref, lse_ref, dq_ref, dkv_ref, qt_scr, dot_scr, dqt_scr, p_scr, ds_scr):
    n_groups, n_cols, e_dim = q_ref.shape
    per_tile = TILE // BLK
    dkv_ref[...] = jnp.zeros_like(dkv_ref)
    for grp in range(n_groups):
        piece = piece_ref[grp]
        qt_scr[...] = q_ref[grp].T
        dot_scr[...] = do_ref[grp].T
        dqt_scr[...] = jnp.zeros_like(dqt_scr)
        delta = jnp.sum(dot_scr[...].astype(F32) * o_ref[grp].T.astype(F32), axis=0, keepdims=True)

        def tile_step(tile_idx, masked):
            row0 = pl.multiple_of(tile_idx * TILE, TILE)
            k_t = kv_ref[pl.ds(row0, TILE), :e_dim]
            v_t = kv_ref[pl.ds(row0, TILE), e_dim:]
            for c0 in range(0, n_cols, COLS):
                cs = slice(c0, c0 + COLS)
                s = dot(k_t, qt_scr[:, cs])
                p = jnp.exp(s - lse_ref[grp, :, cs])
                if masked:
                    p = jnp.where(causal_mask(row0, piece * BLK, COLS), p, 0.0)
                d_p = dot(v_t, dot_scr[:, cs])
                p_scr[:, cs] = p.astype(BF16)
                ds_scr[:, cs] = (p * (d_p - delta[:, cs])).astype(BF16)
            rows = pl.ds(row0, TILE)
            dkv_ref[rows, :e_dim] += dot(ds_scr[...], q_ref[grp])
            dkv_ref[rows, e_dim:] += dot(p_scr[...], do_ref[grp])
            dqt_scr[...] += dot_ta(k_t, ds_scr[...])

        n_full = piece // per_tile

        def body(tile_idx, carry):
            tile_step(tile_idx, False)
            return carry

        lax.fori_loop(0, n_full, body, 0)
        tile_step(n_full, True)
        dq_ref[grp] = dqt_scr[...].T


def attention_forward(pieces, kv_all, q_grp):
    n_groups, n_cols, e_dim = q_grp.shape
    seq = kv_all.shape[0]
    vmem = pl.BlockSpec(memory_space=pltpu.VMEM)
    work = n_groups * n_cols * seq // 2
    return pl.pallas_call(
        fwd_kernel,
        out_shape=(jax.ShapeDtypeStruct(q_grp.shape, BF16), jax.ShapeDtypeStruct((n_groups, 1, n_cols), F32)),
        in_specs=[pl.BlockSpec(memory_space=pltpu.SMEM), vmem, vmem],
        out_specs=(vmem, vmem),
        scratch_shapes=[
            pltpu.VMEM((e_dim, n_cols), BF16),
            pltpu.VMEM((e_dim, n_cols), F32),
            pltpu.VMEM((1, n_cols), F32),
            pltpu.VMEM((1, n_cols), F32),
        ],
        compiler_params=pltpu.CompilerParams(vmem_limit_bytes=40 << 20),
        cost_estimate=pl.CostEstimate(flops=4 * work * e_dim, bytes_accessed=kv_all.size * 2, transcendentals=work),
        name="attn_fwd",
    )(pieces, kv_all, q_grp)


def attention_backward(pieces, kv_all, q_grp, do_grp, o_grp, lse):
    n_groups, n_cols, e_dim = q_grp.shape
    seq = kv_all.shape[0]
    vmem = pl.BlockSpec(memory_space=pltpu.VMEM)
    work = n_groups * n_cols * seq // 2
    return pl.pallas_call(
        bwd_kernel,
        out_shape=(jax.ShapeDtypeStruct(q_grp.shape, F32), jax.ShapeDtypeStruct((seq, 2 * e_dim), F32)),
        in_specs=[pl.BlockSpec(memory_space=pltpu.SMEM)] + [vmem] * 5,
        out_specs=(vmem, vmem),
        scratch_shapes=[
            pltpu.VMEM((e_dim, n_cols), BF16),
            pltpu.VMEM((e_dim, n_cols), BF16),
            pltpu.VMEM((e_dim, n_cols), F32),
            pltpu.VMEM((TILE, n_cols), BF16),
            pltpu.VMEM((TILE, n_cols), BF16),
        ],
        compiler_params=pltpu.CompilerParams(vmem_limit_bytes=48 << 20),
        cost_estimate=pl.CostEstimate(flops=10 * work * e_dim, bytes_accessed=kv_all.size * 6, transcendentals=work),
        name="attn_bwd",
    )(pieces, kv_all, q_grp, do_grp, o_grp, lse)


RING = 4
AXIS_STRIDE = (RING * RING, RING, 1)
ORDERS = ((0, 1, 2), (1, 2, 0), (2, 0, 1))
MESH = pl.DeviceIdType.MESH


def ring_of(axis):
    cp, tp = lax.axis_index("cp"), lax.axis_index("tp")
    stride = AXIS_STRIDE[axis]
    pos = (cp // stride) % RING
    right = cp + ((pos + 1) % RING - pos) * stride
    left = cp + ((pos + RING - 1) % RING - pos) * stride
    return pos, (tp, right), (tp, left)


def enter(with_partner=False):
    barrier = pltpu.get_barrier_semaphore()
    peers = []
    for axis in range(3):
        _, right, left = ring_of(axis)
        peers += [right, left]
    if with_partner:
        peers.append((1 - lax.axis_index("tp"), lax.axis_index("cp")))
    for peer in peers:
        pl.semaphore_signal(barrier, inc=1, device_id=peer, device_id_type=MESH)
    pl.semaphore_wait(barrier, len(peers))


def remote(src, dst, sems, idx, device):
    return pltpu.make_async_remote_copy(src_ref=src, dst_ref=dst, send_sem=sems[0].at[idx], recv_sem=sems[1].at[idx], device_id=device, device_id_type=MESH)


def add_rows(dst, dst0, srcs, n_rows, lanes):
    strip = next(s for s in (64, 48, 40, 32, 24, 16, 8) if n_rows % s == 0)
    if lanes[1] > 256:
        strip = next(s for s in (16, 8) if n_rows % s == 0)

    def body(i, carry):
        off = pl.multiple_of(dst0 + i * strip, 8)
        total = dst[pl.ds(off, strip), pl.ds(*lanes)]
        for ref, start in srcs:
            total = total + ref[pl.ds(pl.multiple_of(start + i * strip, 8), strip), :]
        dst[pl.ds(off, strip), pl.ds(*lanes)] = total
        return carry

    lax.fori_loop(0, n_rows // strip, body, 0)


class Part:
    def __init__(self, order, rb, sems, x=None, y=None, recv=None, row0=0, lanes=None, align=8):
        self.order, self.rb, self.sems, self.x, self.y, self.recv = order, rb, sems, x, y, recv
        self.row0, self.lanes, self.align = row0, lanes, align
        self.sent = []

    def view(self, ref, start, n_rows):
        return ref.at[pl.ds(pl.multiple_of(start, self.align), n_rows), pl.ds(*self.lanes)]

    def place(self, phase):
        base = self.row0
        for j in range(phase):
            base = base + ring_of(self.order[j])[0] * (self.rb * RING ** (2 - j))
        slab = self.rb * RING ** (2 - phase)
        h0 = -(-slab // (2 * self.align)) * self.align
        pos, right, left = ring_of(self.order[phase])
        starts = [base + ((pos + d) % RING) * slab for d in range(RING)]
        return slab, h0, slab - h0, starts, right, left

    def go(self, copy):
        copy.start()
        self.sent.append(copy)
        return copy

    def rs_start(self, phase):
        slab, h0, h1, (own, rgt, opp, lft), right, left = self.place(phase)
        buf, k = self.recv[phase], 10 * phase
        self.c = [
            self.go(remote(self.view(self.x, opp, h0), buf.at[pl.ds(0, h0)], self.sems, k, right)),
            self.go(remote(self.view(self.x, opp + h0, h1), buf.at[pl.ds(h0, h1)], self.sems, k + 1, left)),
            self.go(remote(self.view(self.x, rgt + h0, h1), buf.at[pl.ds(slab + h0, h1)], self.sems, k + 2, right)),
            self.go(remote(self.view(self.x, lft, h0), buf.at[pl.ds(2 * slab, h0)], self.sems, k + 3, left)),
        ]

    def rs_mid(self, phase):
        slab, h0, h1, (own, rgt, opp, lft), right, left = self.place(phase)
        buf, k = self.recv[phase], 10 * phase
        self.c[0].wait_recv()
        add_rows(self.x, rgt, [(buf, 0)], h0, self.lanes)
        self.c.append(self.go(remote(self.view(self.x, rgt, h0), buf.at[pl.ds(slab, h0)], self.sems, k + 4, right)))
        self.c[1].wait_recv()
        add_rows(self.x, lft + h0, [(buf, h0)], h1, self.lanes)
        self.c.append(self.go(remote(self.view(self.x, lft + h0, h1), buf.at[pl.ds(2 * slab + h0, h1)], self.sems, k + 5, left)))

    def rs_end(self, phase):
        slab, h0, h1, (own, rgt, opp, lft), right, left = self.place(phase)
        for copy in self.c[2:]:
            copy.wait_recv()
        buf = self.recv[phase]
        add_rows(self.x, own, [(buf, slab), (buf, 2 * slab)], slab, self.lanes)

    def ag_start(self, phase):
        slab, h0, h1, (own, rgt, opp, lft), right, left = self.place(phase)
        mine, k = self.view(self.y, own, slab), 10 * phase
        self.g = [
            self.go(remote(mine, mine, self.sems, k + 6, right)),
            self.go(remote(mine, mine, self.sems, k + 7, left)),
        ]

    def ag_mid(self, phase):
        slab, h0, h1, (own, rgt, opp, lft), right, left = self.place(phase)
        k = 10 * phase
        self.g[0].wait_recv()
        fwd = self.view(self.y, lft, h0)
        self.g.append(self.go(remote(fwd, fwd, self.sems, k + 8, right)))
        self.g[1].wait_recv()
        fwd = self.view(self.y, rgt + h0, h1)
        self.g.append(self.go(remote(fwd, fwd, self.sems, k + 9, left)))

    def ag_end(self, phase):
        self.g[2].wait_recv()
        self.g[3].wait_recv()

    def own_rows(self):
        return self.place(2)[3][0]

    def drain(self):
        for copy in self.sent:
            copy.wait_send()


def reduce_scatter(parts):
    for phase in range(3):
        for stage in ("rs_start", "rs_mid", "rs_end"):
            for part in parts:
                getattr(part, stage)(phase)


def all_gather(parts):
    for phase in (2, 1, 0):
        for stage in ("ag_start", "ag_mid", "ag_end"):
            for part in parts:
                getattr(part, stage)(phase)


def slab_rows(rb):
    return [3 * rb * RING ** (2 - phase) for phase in range(3)]


def place_in_order(block, order):
    digit = [(block // s) % RING for s in AXIS_STRIDE]
    return (digit[order[0]] * RING + digit[order[1]]) * RING + digit[order[2]]


def by_rows(n_rows, align):
    unit = n_rows // align
    counts = [(unit + 2 - c) // 3 for c in range(3)]
    starts = [sum(counts[:c]) * align for c in range(3)]
    return [(starts[c], counts[c] * align) for c in range(3)]


def pair(n):
    return [pltpu.SemaphoreType.DMA((n,)), pltpu.SemaphoreType.DMA((n,))]


def kv_gather_kernel(own_ref, all_ref, y0, y1, y2, s0, r0, s1, r1, s2, r2, out_sem):
    rows, lanes = own_ref.shape
    n_blk = RING ** 3
    split = by_rows(rows, 16)
    parts = []
    for c, (y, s, r) in enumerate(((y0, s0, r0), (y1, s1, r1), (y2, s2, r2))):
        part = Part(ORDERS[c], split[c][1], (s, r), y=y, lanes=(0, lanes), align=16)
        y[pl.ds(pl.multiple_of(part.own_rows(), 16), split[c][1]), :] = own_ref[pl.ds(*split[c]), :]
        parts.append(part)
    enter()
    all_gather(parts)

    def body(blk, carry):
        for c, y in enumerate((y0, y1, y2)):
            at, rb = split[c]
            src = y.at[pl.ds(pl.multiple_of(place_in_order(blk, ORDERS[c]) * rb, 16), rb)]
            pltpu.make_async_copy(src, all_ref.at[pl.ds(pl.multiple_of(blk * rows + at, 16), rb)], out_sem.at[c]).start()
        return carry

    lax.fori_loop(0, n_blk, body, 0)
    for c, y in enumerate((y0, y1, y2)):
        pltpu.make_async_copy(y, all_ref.at[pl.ds(0, n_blk * split[c][1])], out_sem.at[c]).wait()
    for part in parts:
        part.drain()


def kv_gather(own):
    rows, lanes = own.shape
    n_blk = RING ** 3
    split = by_rows(rows, 16)
    return pl.pallas_call(
        kv_gather_kernel,
        out_shape=jax.ShapeDtypeStruct((n_blk * rows, lanes), own.dtype),
        in_specs=[pl.BlockSpec(memory_space=pltpu.VMEM)],
        out_specs=pl.BlockSpec(memory_space=pl.ANY),
        scratch_shapes=[pltpu.VMEM((n_blk * rb, lanes), own.dtype) for _, rb in split] + pair(30) * 3 + [pltpu.SemaphoreType.DMA((3,))],
        compiler_params=pltpu.CompilerParams(collective_id=1, has_side_effects=True, vmem_limit_bytes=16 << 20),
        name="kv_gather",
    )(own)


def dkv_scatter_kernel(dkv_ref, out_ref, x0, x1, x2, *rest):
    recv, sems, in_sem = rest[:9], rest[9:15], rest[15]
    rows, lanes = out_ref.shape
    n_blk = RING ** 3
    split = by_rows(rows, 8)
    xs = (x0, x1, x2)
    parts = [Part(ORDERS[c], split[c][1], sems[2 * c:2 * c + 2], x=xs[c], recv=recv[3 * c:3 * c + 3], lanes=(0, lanes)) for c in range(3)]

    def body(blk, carry):
        for c in range(3):
            at, rb = split[c]
            dst = xs[c].at[pl.ds(pl.multiple_of(place_in_order(blk, ORDERS[c]) * rb, 8), rb)]
            pltpu.make_async_copy(dkv_ref.at[pl.ds(pl.multiple_of(blk * rows + at, 8), rb)], dst, in_sem.at[c]).start()
        return carry

    lax.fori_loop(0, n_blk, body, 0)
    enter()
    for c in range(3):
        pltpu.make_async_copy(dkv_ref.at[pl.ds(0, n_blk * split[c][1])], xs[c], in_sem.at[c]).wait()
    reduce_scatter(parts)
    for c in range(3):
        out_ref[pl.ds(*split[c]), :] = xs[c][pl.ds(pl.multiple_of(parts[c].own_rows(), 8), split[c][1]), :]
    for part in parts:
        part.drain()


def dkv_scatter(dkv):
    n_blk = RING ** 3
    rows, lanes = dkv.shape[0] // n_blk, dkv.shape[1]
    split = by_rows(rows, 8)
    return pl.pallas_call(
        dkv_scatter_kernel,
        out_shape=jax.ShapeDtypeStruct((rows, lanes), F32),
        in_specs=[pl.BlockSpec(memory_space=pl.ANY)],
        out_specs=pl.BlockSpec(memory_space=pltpu.VMEM),
        scratch_shapes=[pltpu.VMEM((n_blk * rb, lanes), F32) for _, rb in split]
        + [pltpu.VMEM((n, lanes), F32) for _, rb in split for n in slab_rows(rb)]
        + pair(30) * 3
        + [pltpu.SemaphoreType.DMA((3,))],
        compiler_params=pltpu.CompilerParams(collective_id=2, has_side_effects=True, vmem_limit_bytes=32 << 20),
        name="dkv_scatter",
    )(dkv)


def grad_sum_layout(d_model, n_local):
    n_blk = RING ** 3
    q_tiles = d_model * n_local // 8 // n_blk
    o_tiles = d_model // 128
    q_count = [q_tiles * 13 // 32, q_tiles * 11 // 32]
    q_count.append(q_tiles - sum(q_count))
    o_count = [o_tiles * 5 // 16, o_tiles * 6 // 16]
    o_count.append(o_tiles - sum(o_count))
    q_rows = [8 * n for n in q_count]
    q_first = [n_blk * sum(q_rows[:c]) for c in range(3)]
    o_lanes = [(128 * sum(o_count[:c]), 128 * o_count[c]) for c in range(3)]
    return q_rows, q_first, o_lanes


def grad_sum_kernel(hid_ref, grad_ref, dq_ref, o_ref, dkv_ref, gq_ref, go_ref, gk_ref, gv_ref, xq, xo, xk, yq, yo, yk, yp, tok_scr, *rest):
    n_parts = 7
    recv, sems, out_sem, swap_s, swap_r = rest[:3 * n_parts], rest[3 * n_parts:5 * n_parts], rest[-3], rest[-2], rest[-1]
    n_blk = RING ** 3
    n_tok, d_model = hid_ref.shape
    n_batch, n_local, block_len, head_dim = dq_ref.shape
    n_cols = n_local * head_dim
    q_rows, q_first, o_lanes = grad_sum_layout(d_model, n_local)
    parts = []
    for c in range(3):
        i = len(parts)
        parts.append(Part(ORDERS[c], q_rows[c], sems[2 * i:2 * i + 2], x=xq, y=yq, recv=recv[3 * i:3 * i + 3], row0=q_first[c], lanes=(0, 128)))
        i += 1
        parts.append(Part(ORDERS[c], n_cols // n_blk, sems[2 * i:2 * i + 2], x=xo, y=yo, recv=recv[3 * i:3 * i + 3], lanes=o_lanes[c]))
    i = 6
    parts.append(Part(ORDERS[2], d_model // n_blk, sems[2 * i:2 * i + 2], x=xk, y=yk, recv=recv[3 * i:3 * i + 3], lanes=(0, 128)))

    for b in range(n_batch):
        for h in range(n_local):
            tok_scr[pl.ds(b * block_len, block_len), pl.ds(h * head_dim, head_dim)] = dq_ref[b, h]
    d_tile = 256

    def q_body(i, carry):
        cols = pl.ds(pl.multiple_of(i * d_tile, d_tile), d_tile)
        hid_t = hid_ref[:, cols]
        res = dot_ta(hid_t, tok_scr[...])
        for h in range(n_local):
            xq[pl.ds(i * d_tile * n_local + h, d_tile, stride=n_local), :] = res[:, h * head_dim:(h + 1) * head_dim]
        xk[cols, :] = dot_ta(hid_t, dkv_ref[...])
        return carry

    lax.fori_loop(0, d_model // d_tile, q_body, 0)
    for b in range(n_batch):
        for h in range(n_local):
            tok_scr[pl.ds(b * block_len, block_len), pl.ds(h * head_dim, head_dim)] = o_ref[b, h]

    def o_body(i, carry):
        cols = pl.ds(pl.multiple_of(i * d_tile, d_tile), d_tile)
        xo[:, cols] = dot_ta(tok_scr[...], grad_ref[:, cols])
        return carry

    lax.fori_loop(0, d_model // d_tile, o_body, 0)

    enter(with_partner=True)
    reduce_scatter(parts)
    for part in parts:
        rows = pl.ds(pl.multiple_of(part.own_rows(), 8), part.rb)
        part.y[rows, pl.ds(*part.lanes)] = part.x[rows, pl.ds(*part.lanes)]
    all_gather(parts)
    partner = (1 - lax.axis_index("tp"), lax.axis_index("cp"))
    swap = pltpu.make_async_remote_copy(src_ref=yk, dst_ref=yp, send_sem=swap_s, recv_sem=swap_r, device_id=partner, device_id_type=MESH)
    swap.start()
    outs = [pltpu.make_async_copy(yq, gq_ref, out_sem.at[0]), pltpu.make_async_copy(yo, go_ref, out_sem.at[1])]
    for copy in outs:
        copy.start()
    swap.wait()
    first = lax.axis_index("tp") == 0

    @pl.when(first)
    def _():
        outs_k = [pltpu.make_async_copy(yk, gk_ref, out_sem.at[2]), pltpu.make_async_copy(yp, gv_ref, out_sem.at[3])]
        for copy in outs_k:
            copy.start()
        for copy in outs_k:
            copy.wait()

    @pl.when(jnp.logical_not(first))
    def _():
        outs_k = [pltpu.make_async_copy(yp, gk_ref, out_sem.at[2]), pltpu.make_async_copy(yk, gv_ref, out_sem.at[3])]
        for copy in outs_k:
            copy.start()
        for copy in outs_k:
            copy.wait()

    for copy in outs:
        copy.wait()
    for part in parts:
        part.drain()


def grad_sum(hid, grad, dq, o, dkv):
    n_tok, d_model = hid.shape
    n_batch, n_local, block_len, head_dim = dq.shape
    n_cols = n_local * head_dim
    n_blk = RING ** 3
    q_rows, _, o_lanes = grad_sum_layout(d_model, n_local)
    recv = []
    for c in range(3):
        recv += [pltpu.VMEM((n, 128), F32) for n in slab_rows(q_rows[c])]
        recv += [pltpu.VMEM((n, o_lanes[c][1]), F32) for n in slab_rows(n_cols // n_blk)]
    recv += [pltpu.VMEM((n, 128), F32) for n in slab_rows(d_model // n_blk)]
    vmem, anyspace = pl.BlockSpec(memory_space=pltpu.VMEM), pl.BlockSpec(memory_space=pl.ANY)
    xq, xo, xk = (pltpu.VMEM(s, F32) for s in ((d_model * n_local, 128), (n_cols, d_model), (d_model, 128)))
    return pl.pallas_call(
        grad_sum_kernel,
        out_shape=(
            jax.ShapeDtypeStruct((d_model * n_local, 128), F32),
            jax.ShapeDtypeStruct((n_cols, d_model), F32),
            jax.ShapeDtypeStruct((d_model, 128), F32),
            jax.ShapeDtypeStruct((d_model, 128), F32),
        ),
        in_specs=[vmem] * 5,
        out_specs=(anyspace,) * 4,
        scratch_shapes=[xq, xo, xk, xq, xo, xk, xk, pltpu.VMEM((n_tok, n_cols), BF16)] + recv + pair(30) * 7 + [pltpu.SemaphoreType.DMA((4,)), pltpu.SemaphoreType.DMA, pltpu.SemaphoreType.DMA],
        compiler_params=pltpu.CompilerParams(collective_id=3, has_side_effects=True, vmem_limit_bytes=67000000),
        name="grad_sum",
    )(hid, grad, dq, o, dkv)


def solution(mesh):
    cp_size = mesh.shape["cp"]
    half = cp_size // 2
    axes = ("tp", "cp")

    def flat(tp, cp):
        return tp * cp_size + cp

    route_a, route_b = [], []
    for cp in range(cp_size):
        mine, mirror = int(cp >= half), cp_size - 1 - cp
        route_b.append((flat(mine, cp), flat(1 - mine, cp)))
        route_b.append((flat(1 - mine, cp), flat(1 - mine, mirror)))
        route_a.append((flat(1 - mine, cp), flat(mine, mirror)))
    back_a = [(dst, src) for src, dst in route_a]
    back_b = [(dst, src) for src, dst in route_b]
    partner = [(0, 1), (1, 0)]

    def exchange(own_of, is_mine, plan_a, plan_b, send_a, send_b):
        got_a = lax.ppermute(send_a, axes, plan_a)
        got_b = lax.ppermute(send_b, axes, plan_b)
        return jnp.where(is_mine, own_of, got_b), jnp.where(is_mine, got_b, got_a)

    def local_program(hidden, grad_out, w_query, w_key, w_value, w_out):
        block_len = hidden.shape[1]
        n_local = w_query.shape[1]
        head_dim = w_key.shape[1]
        q_scale = head_dim ** -0.5
        cp_idx = lax.axis_index("cp")
        tp_idx = lax.axis_index("tp")
        is_mine = tp_idx == (cp_idx >= half).astype(jnp.int32)
        mirror_idx = cp_size - 1 - cp_idx
        pieces = jnp.stack([cp_idx, mirror_idx]).astype(jnp.int32)
        cos_tab, sin_tab = rope_tables(cp_idx * block_len + jnp.arange(block_len), head_dim)
        cos_mir, sin_mir = rope_tables(mirror_idx * block_len + jnp.arange(block_len), head_dim)
        cos_grp = jnp.stack([cos_tab, cos_mir])[:, None]
        sin_grp = jnp.stack([sin_tab, sin_mir])[:, None]

        def pick(pair, idx):
            return lax.dynamic_index_in_dim(pair, idx, 0, keepdims=False)

        def to_workers(x):
            own, other = pick(x, tp_idx), pick(x, 1 - tp_idx)
            return exchange(own, is_mine, route_a, route_b, other, jnp.where(is_mine, other, own))

        def to_homes(own_piece, mir_piece):
            mine, other = exchange(own_piece, is_mine, back_a, back_b, mir_piece, jnp.where(is_mine, mir_piece, own_piece))
            first = tp_idx == 0
            return jnp.stack([jnp.where(first, mine, other), jnp.where(first, other, mine)])

        def sum_over_tp(part, extra=None):
            total = pick(part, tp_idx) + lax.ppermute(pick(part, 1 - tp_idx), "tp", partner)
            if extra is not None:
                total = total + extra
            mine = total.astype(BF16)
            other = lax.ppermute(mine, "tp", partner)
            first = tp_idx == 0
            return jnp.stack([jnp.where(first, mine, other), jnp.where(first, other, mine)])

        hid_b = pick(hidden, tp_idx)
        key_loc = rotate(dot(hid_b, w_key), cos_tab, sin_tab).astype(BF16)
        val_loc = dot(hid_b, w_value).astype(BF16)
        kv_all = kv_gather(jnp.concatenate([key_loc, val_loc], axis=1))

        q_pre = jnp.einsum("bsd,dhe->bhse", hidden, w_query, preferred_element_type=F32)
        queries = (rotate(q_pre, cos_tab, sin_tab) * q_scale).astype(BF16)
        d_out = jnp.einsum("bsd,hed->bhse", grad_out, w_out, preferred_element_type=F32).astype(BF16)
        own_qd, mir_qd = to_workers(jnp.stack([queries, d_out], axis=1))
        grp_shape = (2, n_local * block_len, head_dim)
        q_grp = jnp.stack([own_qd[0], mir_qd[0]]).reshape(grp_shape)
        do_grp = jnp.stack([own_qd[1], mir_qd[1]]).reshape(grp_shape)

        o_grp, lse = attention_forward(pieces, kv_all, q_grp)
        o_split = o_grp.reshape(2, n_local, block_len, head_dim)
        attn_heads = to_homes(o_split[0], o_split[1])
        attn_out = sum_over_tp(jnp.einsum("cirf,ife->cre", attn_heads, w_out, preferred_element_type=F32))

        dq_grp, dkv = attention_backward(pieces, kv_all, q_grp, do_grp, o_grp, lse)
        dkv_loc = dkv_scatter(dkv)
        dq_rot = (unrotate(dq_grp.reshape(2, n_local, block_len, head_dim), cos_grp, sin_grp) * q_scale).astype(BF16)
        dq_pre = to_homes(dq_rot[0], dq_rot[1])
        dk_pre = unrotate(dkv_loc[:, :head_dim], cos_tab, sin_tab).astype(BF16)
        dv_pre = dkv_loc[:, head_dim:].astype(BF16)
        first = tp_idx == 0
        mine_kv = jnp.where(first, dk_pre, dv_pre)
        other_kv = lax.ppermute(jnp.where(first, dv_pre, dk_pre), "tp", partner)
        dkv_pair = jnp.concatenate([jnp.where(first, mine_kv, other_kv), jnp.where(first, other_kv, mine_kv)], axis=0)
        grad_q, grad_o, d_w_key, d_w_value = grad_sum(hidden.reshape(-1, hidden.shape[-1]), grad_out.reshape(-1, hidden.shape[-1]), dq_pre, attn_heads, dkv_pair)
        d_w_query = grad_q.reshape(w_query.shape)
        d_w_out = grad_o.reshape(w_out.shape)
        dh_kv = dot(dk_pre, w_key.T) + dot(dv_pre, w_value.T)
        d_hidden = sum_over_tp(jnp.einsum("cirf,eif->cre", dq_pre, w_query, preferred_element_type=F32), dh_kv)
        return attn_out, d_hidden, d_w_query, d_w_key, d_w_value, d_w_out

    row_spec = P(None, "cp", None)
    return jax.shard_map(local_program, mesh=mesh, in_specs=(row_spec, row_spec, P(None, "tp", None), P(), P(), P("tp", None, None)), out_specs=(row_spec, row_spec, P(None, "tp", None), P(), P(), P("tp", None, None)), check_vma=False)
```

time: 2040 us -> 411 us (0.20)
  waiting for transfers between devices: 1770 us -> 6.75 us
  Pallas kernels: 0 us -> 321 us
  local copies, waits for them, and re-layouts: 185 us -> 17.3 us
  starting transfers between devices: 2.83 us -> 39.4 us
  matrix products: 39.8 us -> 12.3 us
    ppermute x190 -> x11, waiting for transfers between devices: 1410 us -> 6.75 us  [the longest x3 4.52 us: exchange(): got_b = lax.ppermute(send_b, axes, plan_b)]
    psum x2 -> x0, waiting for transfers between devices: 354 us -> none  [the longest x1 210 us: local_program(): lax.psum(jnp.einsum('cre,cirf->eif', hidden, dq_pre, preferred_element_ty...]
    pallas_call x0 -> x5, Pallas kernels: none -> 321 us  [the longest x1 165 us: grad_sum(): pl.pallas_call(grad_sum_kernel, out_shape=(jax.ShapeDtypeStruct((d_model...]
    another operation x129 -> x0, local copies, waits for them, and re-layouts: 98.8 us -> none
    while x66 -> x0, local copies, waits for them, and re-layouts: 61.2 us -> none
    ppermute x190 -> x11, starting transfers between devices: 2.76 us -> 39.4 us  [the longest x3 13.5 us: exchange(): got_a = lax.ppermute(send_a, axes, plan_a)]
    dot_general x19 -> x8, matrix products: 39.8 us -> 12.3 us  [the longest x1 3.93 us: local_program(): jnp.einsum('bsd,dhe->bhse', hidden, w_query, preferred_element_type=F32)]
  transfers between devices with their start and end apart: 192 -> 11, of which waited for: 192 -> 2; matrix products, arithmetic and copies ran while one was open for 4% -> 3% of each run, Pallas kernels for 0% -> 51%
where the time goes in v1:
time: 411 us
  Pallas kernels  321 us (78%)
  starting transfers between devices  39.4 us (10%)
  local copies, waits for them, and re-layouts  17.3 us (4%)
  other arithmetic  13.2 us (3%)
  matrix products  12.3 us (3%)
  waiting for transfers between devices  6.75 us (2%)
    pallas_call x1, Pallas kernels, grad_sum(): pl.pallas_call(grad_sum_kernel, out_shape=(jax.ShapeDtypeStruct((d_model...  165 us
    pallas_call x1, Pallas kernels, dkv_scatter(): pl.pallas_call(dkv_scatter_kernel, out_shape=jax.ShapeDtypeStruct((rows,...  52.1 us
    pallas_call x1, Pallas kernels, kv_gather(): pl.pallas_call(kv_gather_kernel, out_shape=jax.ShapeDtypeStruct((n_blk *...  42.6 us
    pallas_call x1, Pallas kernels, attention_forward(): pl.pallas_call(fwd_kernel, out_shape=(jax.ShapeDtypeStruct(q_grp.shape, B...  30.5 us
    pallas_call x1, Pallas kernels, attention_backward(): pl.pallas_call(bwd_kernel, out_shape=(jax.ShapeDtypeStruct(q_grp.shape, F...  30.1 us
    unnamed x34, local copies, waits for them, and re-layouts  15.2 us
    ppermute x3, starting transfers between devices, exchange(): got_a = lax.ppermute(send_a, axes, plan_a)  13.5 us
    ppermute x1, starting transfers between devices, local_program(): other_kv = lax.ppermute(jnp.where(first, dv_pre, dk_pre), 'tp', partner)  11 us
  transfers between devices with their start and end apart: 11, of which 2 were waited for; matrix products, arithmetic and copies ran while one was open for 3% of the time, Pallas kernels for 51%

profile of v1, /device:TPU:1, one launch (start us, length us, event | category | flops | bytes accessed | tf_op | source)
XLA Modules:
  0.0 410.9 jit_solution(7350576381317183279)
XLA Ops:
  0.7 1.5 fusion.34
  2.2 0.3 multiply_cosine_fusion.2
  2.5 0.1 copy.35
  2.6 0.1 copy.36
  2.7 3.9 fusion.15
  6.6 0.2 subtract_bitcast_fusion
  6.8 0.1 fusion.24
  6.9 3.5 fusion.21
  10.4 0.1 fusion.31
  10.6 0.3 copy.38
  10.8 0.3 copy.39
  11.1 0.1 bitcast_select_fusion.1
  11.2 9.3 %collective-permute-start = (bf16[2,8,128,128]{3,2,1,0:T(8,128)(2,1)S(1)}, bf16[2,8,128,128]{3,2,1,0:T(8,128)(2,1)}, u32[]{:S(2)}, u32[]{:S(2)}) collective-permute-start(bf16[2,8,128,128]{3,2,1,0:T(8,128)(2,1)S(1)} %bitcast_select_fusion.1), channel_id=1, source_target_pairs={{0,64},{64,127},{1,65},{65,126},{2,66},{66,125},{3,67},{67,124},{4... | collective-permute-start | bytes 1572872 | tf_op jit(solution)/shard_map/ppermute | solution.py:563
  20.5 2.5 collective-permute-start.1
  23.0 0.3 convolution_convert_fusion
  23.3 0.1 pad_maximum_fusion.7.own_ref
  23.4 42.6 %kv_gather.1.kv_ref = bf16[8192,256]{1,0:T(8,128)(2,1)S(1)} custom-call(bf16[128,256]{1,0:T(8,128)(2,1)S(1)} %pad_maximum_fusion.7.own_ref), custom_call_target="tpu_custom_call" | custom-call | tf_op jit(solution)/shard_map/kv_gather/pallas_call | solution.py:365
  66.1 2.0 copy-done.1
  68.1 0.1 pad_add_fusion.piece_ref
  68.1 0.5 multiply_cosine_fusion.1
  68.7 1.6 bitcast_select_fusion
  70.4 0.1 fusion.57
  70.5 0.1 pad_maximum_fusion.4
  70.6 30.5 %attn_fwd.1 = (bf16[2,1024,128]{2,1,0:T(8,128)(2,1)S(1)}, f32[2,1,1024]{2,1,0:T(1,128)S(1)}) custom-call(s32[2]{0:T(128)S(1)} %pad_add_fusion.piece_ref, bf16[8192,256]{1,0:T(8,128)(2,1)S(1)} %copy-done.2, bf16[2,1024,128]{2,1,0:T(8,128)(2,1)S(1)} %bitcast.114), custom_call_target="tpu_custom_call" | custom-call | flops 4294967296 | bytes 4194304 | tf_op jit(solution)/shard_map/attn_fwd/pallas_call | solution.py:132
  101.1 30.1 %attn_bwd.1 = (f32[2,1024,128]{2,1,0:T(8,128)S(1)}, f32[8192,256]{1,0:T(8,128)}) custom-call(s32[2]{0:T(128)S(1)} %pad_add_fusion.piece_ref, bf16[8192,256]{1,0:T(8,128)(2,1)} %copy-done.1, bf16[2,1024,128]{2,1,0:T(8,128)(2,1)S(1)} %bitcast.115, bf16[2,1024,128]{2,1,0:T(8,128)(2,1)S(1)} %bitcast.113, bf16[2,1024,128]{2,1,0:T(8,128)(2,1)S(1)} %get-tuple-element.14.o_ref, ...), custom_call_target="tpu_custom_call" | custom-call | flops 10737418240 | bytes 12582912 | tf_op jit(solution)/shard_map/attn_bwd/pallas_call | solution.py:154
  131.3 0.5 multiply_subtract_fusion
  131.8 0.3 fusion.25
  132.3 2.4 copy-done
  134.6 52.1 %dkv_scatter.1 = f32[128,256]{1,0:T(8,128)S(1)} custom-call(f32[8192,256]{1,0:T(8,128)S(1)} %copy-done), custom_call_target="tpu_custom_call" | custom-call | tf_op jit(solution)/shard_map/dkv_scatter/pallas_call | solution.py:406
  186.8 0.3 fusion.48
  187.1 0.1 broadcast_select_fusion.9
  187.2 11.0 %collective-permute-start.10 = (bf16[128,128]{1,0:T(8,128)(2,1)S(1)}, bf16[128,128]{1,0:T(8,128)(2,1)S(1)}, u32[]{:S(2)}, u32[]{:S(2)}) collective-permute-start(bf16[128,128]{1,0:T(8,128)(2,1)S(1)} %get-tuple-element.22), channel_id=1, source_target_pairs={{0,64},{64,0},{1,65},{65,1},{2,66},{66,2},{3,67},{67,3},{4,68},{68... | collective-permute-start | bytes 98312 | tf_op jit(solution)/shard_map/ppermute | solution.py:628
  198.2 0.1 collective-permute-start.6
  198.3 5.5 %collective-permute-start.7 = (bf16[8,128,128]{2,1,0:T(8,128)(2,1)S(1)}, bf16[8,128,128]{2,1,0:T(8,128)(2,1)S(1)}, u32[]{:S(2)}, u32[]{:S(2)}) collective-permute-start(bf16[8,128,128]{2,1,0:T(8,128)(2,1)S(1)} %slice_bitcast_fusion), channel_id=1, source_target_pairs={{63,64},{62,65},{61,66},{60,67},{59,68},{58,69},{57,70},{56,71},{5... | collective-permute-start | bytes 786440 | tf_op jit(solution)/shard_map/ppermute | solution.py:562
  203.7 5.5 %collective-permute-start.3 = (bf16[8,128,128]{2,1,0:T(8,128)(2,1)S(1)}, bf16[8,128,128]{2,1,0:T(8,128)(2,1)S(1)}, u32[]{:S(2)}, u32[]{:S(2)}) collective-permute-start(bf16[8,128,128]{2,1,0:T(8,128)(2,1)S(1)} %bitcast.125), channel_id=1, source_target_pairs={{63,64},{62,65},{61,66},{60,67},{59,68},{58,69},{57,70},{56,71},{5... | collective-permute-start | bytes 786440 | tf_op jit(solution)/shard_map/ppermute | solution.py:562
  209.3 0.3 collective-permute-start.2
  209.6 0.3 fusion.60
  209.9 0.3 convolution_add_fusion
  210.3 2.2 collective-permute-done.7
  212.5 0.1 select_bitcast_fusion.5
  212.6 1.3 fusion.12
  213.9 0.1 dynamic-slice_bitcast_fusion
  213.9 1.8 collective-permute-start.8
  215.8 4.5 %collective-permute-done.2 = bf16[8,128,128]{2,1,0:T(8,128)(2,1)S(1)} collective-permute-done((bf16[8,128,128]{2,1,0:T(8,128)(2,1)S(1)}, bf16[8,128,128]{2,1,0:T(8,128)(2,1)S(1)}, u32[]{:S(2)}, u32[]{:S(2)}) %collective-permute-start.2) | collective-permute-done | bytes 262176 | tf_op jit(solution)/shard_map/ppermute | solution.py:563
  220.3 0.1 select_bitcast_fusion.7
  220.4 1.3 fusion.9
  221.6 1.1 dynamic-slice_bitcast_fusion.1
  222.8 0.6 pad_maximum_fusion.8.dkv_ref
  223.4 0.8 pad_maximum_fusion.5.dq_ref
  224.3 1.0 fusion.27
  225.3 0.5 collective-permute-start.9
  225.8 0.8 pad_maximum_fusion.3.o_ref
  226.6 165.4 %grad_sum.1 = (f32[16384,128]{1,0:T(8,128)}, f32[1024,2048]{1,0:T(8,128)}, f32[2048,128]{1,0:T(8,128)}, f32[2048,128]{1,0:T(8,128)}) custom-call(bf16[256,2048]{1,0:T(8,128)(2,1)} %bitcast.120, bf16[256,2048]{1,0:T(8,128)(2,1)} %bitcast.124, bf16[2,8,128,128]{3,2,1,0:T(8,128)(2,1)} %pad_maximum_fusion.5.dq_ref, ...), custom_call_target="tpu_custom_call" | custom-call | tf_op jit(solution)/shard_map/grad_sum/pallas_call | solution.py:527
  392.1 1.7 fusion.28
  393.7 2.9 collective-permute-start.5
  396.7 1.3 select_bitcast_fusion.1
  397.9 1.1 pad_maximum_fusion.1
  399.0 0.1 select_bitcast_fusion.3
  399.1 1.1 pad_maximum_fusion
  400.2 4.3 %copy.64 = f32[2048,8,128]{2,1,0:T(8,128)} copy(f32[2048,8,128]{2,1,0:T(8,128)S(1)} %bitcast.119) | data formatting | bytes 16777216
  404.4 1.0 copy.65
  405.4 1.0 copy.66
  406.4 1.1 slice-done.1
  407.5 3.4 copy.67
  (48 shorter events, 0.3 us)
Async XLA Ops:
  2.6 4.3 %copy-start.8 = (bf16[2,128,2048]{2,1,0:T(8,128)(2,1)S(1)}, bf16[2,128,2048]{2,1,0:T(8,128)(2,1)}, u32[]{:S(2)}) copy-start(bf16[2,128,2048]{2,1,0:T(8,128)(2,1)} %param.7) | copy-start | bytes 3145732
  10.4 12.6 %copy-start.4 = (bf16[2,128,2048]{2,1,0:T(8,128)(2,1)S(1)}, bf16[2,128,2048]{2,1,0:T(8,128)(2,1)}, u32[]{:S(2)}) copy-start(bf16[2,128,2048]{2,1,0:T(8,128)(2,1)} %param.6) | copy-start | bytes 3145732
  10.4 12.6 %copy-start.7 = (bf16[2048,128]{1,0:T(8,128)(2,1)S(1)}, bf16[2048,128]{1,0:T(8,128)(2,1)}, u32[]{:S(2)}) copy-start(bf16[2048,128]{1,0:T(8,128)(2,1)} %param.10) | copy-start | bytes 1572868
  11.2 57.5 %collective-permute-start = (bf16[2,8,128,128]{3,2,1,0:T(8,128)(2,1)S(1)}, bf16[2,8,128,128]{3,2,1,0:T(8,128)(2,1)}, u32[]{:S(2)}, u32[]{:S(2)}) collective-permute-start(bf16[2,8,128,128]{3,2,1,0:T(8,128)(2,1)S(1)} %bitcast_select_fusion.1), channel_id=1, source_target_pairs={{0,64},{64,127},{1,65},{65,126},{2,66},{66,125},{3,67},{67,124},{4... | collective-permute-start | bytes 1572872 | tf_op jit(solution)/shard_map/ppermute | solution.py:563
  20.5 48.2 %collective-permute-start.1 = (bf16[2,8,128,128]{3,2,1,0:T(8,128)(2,1)S(1)}, bf16[2,8,128,128]{3,2,1,0:T(8,128)(2,1)}, u32[]{:S(2)}, u32[]{:S(2)}) collective-permute-start(bf16[2,8,128,128]{3,2,1,0:T(8,128)(2,1)S(1)} %bitcast.123), channel_id=1, source_target_pairs={{64,63},{65,62},{66,61},{67,60},{68,59},{69,58},{70,57},{71,56},{7... | collective-permute-start | bytes 1572872 | tf_op jit(solution)/shard_map/ppermute | solution.py:562
  66.1 2.0 copy-start.1
  68.1 2.5 copy-start.2
  131.2 3.4 copy-start
  134.6 75.0 %copy-start.5 = (bf16[2048,128]{1,0:T(8,128)(2,1)S(1)}, bf16[2048,128]{1,0:T(8,128)(2,1)}, u32[]{:S(2)}) copy-start(bf16[2048,128]{1,0:T(8,128)(2,1)} %param.9) | copy-start | bytes 1572868
  186.8 25.8 %copy-start.11 = (bf16[2048,8,128]{2,1,0:T(8,128)(2,1)S(1)}, bf16[2048,8,128]{2,1,0:T(8,128)(2,1)}, u32[]{:S(2)}) copy-start(bf16[2048,8,128]{2,1,0:T(8,128)(2,1)} %param.8) | copy-start | bytes 12582916
  187.2 35.6 %collective-permute-start.10 = (bf16[128,128]{1,0:T(8,128)(2,1)S(1)}, bf16[128,128]{1,0:T(8,128)(2,1)S(1)}, u32[]{:S(2)}, u32[]{:S(2)}) collective-permute-start(bf16[128,128]{1,0:T(8,128)(2,1)S(1)} %get-tuple-element.22), channel_id=1, source_target_pairs={{0,64},{64,0},{1,65},{65,1},{2,66},{66,2},{3,67},{67,3},{4,68},{68... | collective-permute-start | bytes 98312 | tf_op jit(solution)/shard_map/ppermute | solution.py:628
  198.2 12.1 %collective-permute-start.6 = (bf16[8,128,128]{2,1,0:T(8,128)(2,1)S(1)}, bf16[8,128,128]{2,1,0:T(8,128)(2,1)S(1)}, u32[]{:S(2)}, u32[]{:S(2)}) collective-permute-start(bf16[8,128,128]{2,1,0:T(8,128)(2,1)S(1)} %broadcast_select_fusion.3), channel_id=1, source_target_pairs={{64,0},{127,64},{65,1},{126,65},{66,2},{125,66},{67,3},{124,67},{6... | collective-permute-start | bytes 786440 | tf_op jit(solution)/shard_map/ppermute | solution.py:563
  198.3 14.2 %collective-permute-start.7 = (bf16[8,128,128]{2,1,0:T(8,128)(2,1)S(1)}, bf16[8,128,128]{2,1,0:T(8,128)(2,1)S(1)}, u32[]{:S(2)}, u32[]{:S(2)}) collective-permute-start(bf16[8,128,128]{2,1,0:T(8,128)(2,1)S(1)} %slice_bitcast_fusion), channel_id=1, source_target_pairs={{63,64},{62,65},{61,66},{60,67},{59,68},{58,69},{57,70},{56,71},{5... | collective-permute-start | bytes 786440 | tf_op jit(solution)/shard_map/ppermute | solution.py:562
  203.7 16.5 %collective-permute-start.3 = (bf16[8,128,128]{2,1,0:T(8,128)(2,1)S(1)}, bf16[8,128,128]{2,1,0:T(8,128)(2,1)S(1)}, u32[]{:S(2)}, u32[]{:S(2)}) collective-permute-start(bf16[8,128,128]{2,1,0:T(8,128)(2,1)S(1)} %bitcast.125), channel_id=1, source_target_pairs={{63,64},{62,65},{61,66},{60,67},{59,68},{58,69},{57,70},{56,71},{5... | collective-permute-start | bytes 786440 | tf_op jit(solution)/shard_map/ppermute | solution.py:562
  209.3 11.0 %collective-permute-start.2 = (bf16[8,128,128]{2,1,0:T(8,128)(2,1)S(1)}, bf16[8,128,128]{2,1,0:T(8,128)(2,1)S(1)}, u32[]{:S(2)}, u32[]{:S(2)}) collective-permute-start(bf16[8,128,128]{2,1,0:T(8,128)(2,1)S(1)} %broadcast_select_fusion.6), channel_id=1, source_target_pairs={{64,0},{127,64},{65,1},{126,65},{66,2},{125,66},{67,3},{124,67},{6... | collective-permute-start | bytes 786440 | tf_op jit(solution)/shard_map/ppermute | solution.py:563
  212.6 7.8 %copy-start.12 = (bf16[8,128,2048]{2,1,0:T(8,128)(2,1)S(1)}, bf16[8,128,2048]{2,1,0:T(8,128)(2,1)}, u32[]{:S(2)}) copy-start(bf16[8,128,2048]{2,1,0:T(8,128)(2,1)} %param.11) | copy-start | bytes 12582916
  213.9 10.3 %collective-permute-start.8 = (f32[128,2048]{1,0:T(8,128)S(1)}, f32[128,2048]{1,0:T(8,128)S(1)}, u32[]{:S(2)}, u32[]{:S(2)}) collective-permute-start(f32[128,2048]{1,0:T(8,128)S(1)} %dynamic-slice_bitcast_fusion), channel_id=1, source_target_pairs={{0,64},{64,0},{1,65},{65,1},{2,66},{66,2},{3,67},{67,3},{4,68},{68... | collective-permute-start | bytes 3145736 | tf_op jit(solution)/shard_map/ppermute | solution.py:594
  221.6 3.7 copy-start.6
  222.8 169.3 %collective-permute-start.4 = (f32[128,2048]{1,0:T(8,128)}, f32[128,2048]{1,0:T(8,128)}, u32[]{:S(2)}, u32[]{:S(2)}) collective-permute-start(f32[128,2048]{1,0:T(8,128)} %dynamic-slice_bitcast_fusion.1), channel_id=1, source_target_pairs={{0,64},{64,0},{1,65},{65,1},{2,66},{66,2},{3,67},{67,3},{4,68},{68... | collective-permute-start | bytes 3145736 | tf_op jit(solution)/shard_map/ppermute | solution.py:594
  225.3 171.4 %collective-permute-start.9 = (bf16[128,2048]{1,0:T(8,128)(2,1)}, bf16[128,2048]{1,0:T(8,128)(2,1)}, u32[]{:S(2)}, u32[]{:S(2)}) collective-permute-start(bf16[128,2048]{1,0:T(8,128)(2,1)} %fusion.27), channel_id=1, source_target_pairs={{0,64},{64,0},{1,65},{65,1},{2,66},{66,2},{3,67},{67,3},{4,68},{68... | collective-permute-start | bytes 1572872 | tf_op jit(solution)/shard_map/ppermute | solution.py:598
  393.7 6.4 %copy-start.3 = (f32[16384,128]{1,0:T(8,128)S(1)}, f32[16384,128]{1,0:T(8,128)}, u32[]{:S(2)}) copy-start(f32[16384,128]{1,0:T(8,128)} %get-tuple-element.18) | copy-start | bytes 25165828
  393.7 5.3 %collective-permute-start.5 = (bf16[128,2048]{1,0:T(8,128)(2,1)S(1)}, bf16[128,2048]{1,0:T(8,128)(2,1)S(1)}, u32[]{:S(2)}, u32[]{:S(2)}) collective-permute-start(bf16[128,2048]{1,0:T(8,128)(2,1)S(1)} %fusion.28), channel_id=1, source_target_pairs={{0,64},{64,0},{1,65},{65,1},{2,66},{66,2},{3,67},{67,3},{4,68},{68... | collective-permute-start | bytes 1572872 | tf_op jit(solution)/shard_map/ppermute | solution.py:598
  399.1 7.3 %slice-start = ((s8[8388608]{0:T(1024)(128)(4,1)}), s8[4194304]{0:T(1024)(128)(4,1)S(1)}, s32[]{:S(2)}) async-start(s8[8388608]{0:T(1024)(128)(4,1)} %bitcast.116), calls=%async_computation | async-start | bytes 8388608
  400.2 4.3 %copy-start.10 = (f32[2048,128]{1,0:T(8,128)S(1)}, f32[2048,128]{1,0:T(8,128)}, u32[]{:S(2)}) copy-start(f32[2048,128]{1,0:T(8,128)} %get-tuple-element.76) | copy-start | bytes 3145732
  400.2 5.2 %copy-start.9 = (f32[2048,128]{1,0:T(8,128)S(1)}, f32[2048,128]{1,0:T(8,128)}, u32[]{:S(2)}) copy-start(f32[2048,128]{1,0:T(8,128)} %get-tuple-element.77) | copy-start | bytes 3145732
  400.2 7.4 %slice-start.1 = ((s8[8388608]{0:T(1024)(128)(4,1)}), s8[4194304]{0:T(1024)(128)(4,1)S(1)}, s32[]{:S(2)}) async-start(s8[8388608]{0:T(1024)(128)(4,1)} %bitcast.116), calls=%async_computation.1 | async-start | bytes 8388608

commit v2 on v1

v2 whole, which is shorter than its diff:
```python
import jax
import jax.numpy as jnp
from jax import lax
from jax.experimental import pallas as pl
from jax.experimental.pallas import tpu as pltpu
from jax.sharding import PartitionSpec as P

ROPE_BASE = 10000.0
BLK = 128
TILE = 512
COLS = 256
F32 = jnp.float32
BF16 = jnp.bfloat16


def rope_tables(positions, head_dim):
    half_dim = head_dim // 2
    inv_freq = 1.0 / jnp.power(ROPE_BASE, jnp.arange(half_dim, dtype=F32) * (2.0 / head_dim))
    angles = positions.astype(F32)[:, None] * inv_freq[None, :]
    return jnp.cos(angles), jnp.sin(angles)


def rotate(rot_in, cos_tab, sin_tab):
    half_dim = rot_in.shape[-1] // 2
    low_half = rot_in[..., :half_dim]
    high_half = rot_in[..., half_dim:]
    return jnp.concatenate([low_half * cos_tab - high_half * sin_tab, high_half * cos_tab + low_half * sin_tab], axis=-1)


def unrotate(rot_in, cos_tab, sin_tab):
    return rotate(rot_in, cos_tab, -sin_tab)


def dot(a, b):
    return jnp.dot(a, b, preferred_element_type=F32)


def dot_ta(a, b):
    return lax.dot_general(a, b, (((0,), (0,)), ((), ())), preferred_element_type=F32)


def causal_mask(k_start, q_start, cols):
    k_pos = k_start + lax.broadcasted_iota(jnp.int32, (TILE, cols), 0)
    q_pos = q_start + lax.broadcasted_iota(jnp.int32, (TILE, cols), 1) % BLK
    return k_pos <= q_pos


def fwd_kernel(piece_ref, kv_ref, q_ref, o_ref, lse_ref, qt_scr, acc_scr, m_scr, l_scr):
    n_groups, n_cols, e_dim = q_ref.shape
    per_tile = TILE // BLK
    for grp in range(n_groups):
        piece = piece_ref[grp]
        qt_scr[...] = q_ref[grp].T
        acc_scr[...] = jnp.zeros_like(acc_scr)
        m_scr[...] = jnp.full_like(m_scr, -jnp.inf)
        l_scr[...] = jnp.zeros_like(l_scr)

        def tile_step(tile_idx, masked):
            row0 = pl.multiple_of(tile_idx * TILE, TILE)
            k_t = kv_ref[pl.ds(row0, TILE), :e_dim]
            v_t = kv_ref[pl.ds(row0, TILE), e_dim:]
            for c0 in range(0, n_cols, COLS):
                cs = slice(c0, c0 + COLS)
                s = dot(k_t, qt_scr[:, cs])
                if masked:
                    s = jnp.where(causal_mask(row0, piece * BLK, COLS), s, -jnp.inf)
                m_old = m_scr[:, cs]
                m_new = jnp.maximum(m_old, jnp.max(s, axis=0, keepdims=True))
                p = jnp.exp(s - m_new)
                alpha = jnp.exp(m_old - m_new)
                m_scr[:, cs] = m_new
                l_scr[:, cs] = l_scr[:, cs] * alpha + jnp.sum(p, axis=0, keepdims=True)
                acc_scr[:, cs] = acc_scr[:, cs] * alpha + dot_ta(v_t, p.astype(BF16))

        n_full = piece // per_tile

        def body(tile_idx, carry):
            tile_step(tile_idx, False)
            return carry

        lax.fori_loop(0, n_full, body, 0)
        tile_step(n_full, True)
        o_ref[grp] = (acc_scr[...] / l_scr[...]).T.astype(BF16)
        lse_ref[grp] = m_scr[...] + jnp.log(l_scr[...])


def attention_forward(pieces, kv_all, q_grp):
    n_groups, n_cols, e_dim = q_grp.shape
    seq = kv_all.shape[0]
    vmem = pl.BlockSpec(memory_space=pltpu.VMEM)
    work = n_groups * n_cols * seq // 2
    return pl.pallas_call(
        fwd_kernel,
        out_shape=(jax.ShapeDtypeStruct(q_grp.shape, BF16), jax.ShapeDtypeStruct((n_groups, 1, n_cols), F32)),
        in_specs=[pl.BlockSpec(memory_space=pltpu.SMEM), vmem, vmem],
        out_specs=(vmem, vmem),
        scratch_shapes=[
            pltpu.VMEM((e_dim, n_cols), BF16),
            pltpu.VMEM((e_dim, n_cols), F32),
            pltpu.VMEM((1, n_cols), F32),
            pltpu.VMEM((1, n_cols), F32),
        ],
        compiler_params=pltpu.CompilerParams(vmem_limit_bytes=40 << 20),
        cost_estimate=pl.CostEstimate(flops=4 * work * e_dim, bytes_accessed=kv_all.size * 2, transcendentals=work),
        name="attn_fwd",
    )(pieces, kv_all, q_grp)


RING = 4
AXIS_STRIDE = (RING * RING, RING, 1)
ORDERS = ((0, 1, 2), (1, 2, 0), (2, 0, 1))
MESH = pl.DeviceIdType.MESH


def ring_of(axis):
    cp, tp = lax.axis_index("cp"), lax.axis_index("tp")
    stride = AXIS_STRIDE[axis]
    pos = (cp // stride) % RING
    right = cp + ((pos + 1) % RING - pos) * stride
    left = cp + ((pos + RING - 1) % RING - pos) * stride
    return pos, (tp, right), (tp, left)


def enter(rings, with_partner=False, with_mirror=False):
    barrier = pltpu.get_barrier_semaphore()
    peers = []
    for _, right, left in rings:
        peers += [right, left]
    if with_partner:
        peers.append((1 - lax.axis_index("tp"), lax.axis_index("cp")))
    if with_mirror:
        mirror = RING ** 3 - 1 - lax.axis_index("cp")
        peers += [(0, mirror), (1, mirror)]
    for peer in peers:
        pl.semaphore_signal(barrier, inc=1, device_id=peer, device_id_type=MESH)
    pl.semaphore_wait(barrier, len(peers))


def remote(src, dst, sems, idx, device):
    return pltpu.make_async_remote_copy(src_ref=src, dst_ref=dst, send_sem=sems[0].at[idx], recv_sem=sems[1].at[idx], device_id=device, device_id_type=MESH)


def add_rows(dst, dst0, srcs, n_rows, lanes):
    strip = next(s for s in (64, 48, 40, 32, 24, 16, 8) if n_rows % s == 0)
    if lanes[1] > 256:
        strip = next(s for s in (16, 8) if n_rows % s == 0)

    def body(i, carry):
        off = pl.multiple_of(dst0 + i * strip, 8)
        total = dst[pl.ds(off, strip), pl.ds(*lanes)]
        for ref, start in srcs:
            total = total + ref[pl.ds(pl.multiple_of(start + i * strip, 8), strip), :]
        dst[pl.ds(off, strip), pl.ds(*lanes)] = total
        return carry

    lax.fori_loop(0, n_rows // strip, body, 0)


class Part:
    def __init__(self, rings, order, rb, sems, x=None, y=None, recv=None, row0=0, lanes=None, align=8):
        self.rb, self.sems, self.x, self.y, self.recv = rb, sems, x, y, recv
        self.row0, self.lanes, self.align = row0, lanes, align
        self.places = []
        base = row0
        for phase in range(3):
            slab = rb * RING ** (2 - phase)
            h0 = -(-slab // (2 * align)) * align
            pos, right, left = rings[order[phase]]
            starts = [base + ((pos + d) % RING) * slab for d in range(RING)]
            self.places.append((slab, h0, slab - h0, starts, right, left))
            base = starts[0]

    def view(self, ref, start, n_rows):
        return ref.at[pl.ds(pl.multiple_of(start, self.align), n_rows), pl.ds(*self.lanes)]

    def place(self, phase):
        return self.places[phase]

    def hop(self, phase, i):
        slab, h0, h1, (own, rgt, opp, lft), right, left = self.place(phase)
        if i < 6:
            start, n_rows, at, device = (
                (opp, h0, 0, right),
                (opp + h0, h1, h0, left),
                (rgt + h0, h1, slab + h0, right),
                (lft, h0, 2 * slab, left),
                (rgt, h0, slab, right),
                (lft + h0, h1, 2 * slab + h0, left),
            )[i]
            src, dst = self.view(self.x, start, n_rows), self.recv[phase].at[pl.ds(at, n_rows)]
        else:
            start, n_rows, device = ((own, slab, right), (own, slab, left), (lft, h0, right), (rgt + h0, h1, left))[i - 6]
            src = dst = self.view(self.y, start, n_rows)
        return remote(src, dst, self.sems, 10 * phase + i, device)

    def rs_start(self, phase):
        for i in range(4):
            self.hop(phase, i).start()

    def rs_mid(self, phase):
        slab, h0, h1, (own, rgt, opp, lft), _, _ = self.place(phase)
        buf = self.recv[phase]
        self.hop(phase, 0).wait_recv()
        add_rows(self.x, rgt, [(buf, 0)], h0, self.lanes)
        self.hop(phase, 4).start()
        self.hop(phase, 1).wait_recv()
        add_rows(self.x, lft + h0, [(buf, h0)], h1, self.lanes)
        self.hop(phase, 5).start()

    def rs_end(self, phase):
        slab, _, _, (own, _, _, _), _, _ = self.place(phase)
        for i in range(2, 6):
            self.hop(phase, i).wait_recv()
        buf = self.recv[phase]
        add_rows(self.x, own, [(buf, slab), (buf, 2 * slab)], slab, self.lanes)

    def ag_start(self, phase):
        self.hop(phase, 6).start()
        self.hop(phase, 7).start()

    def ag_mid(self, phase):
        self.hop(phase, 6).wait_recv()
        self.hop(phase, 8).start()
        self.hop(phase, 7).wait_recv()
        self.hop(phase, 9).start()

    def ag_end(self, phase):
        self.hop(phase, 8).wait_recv()
        self.hop(phase, 9).wait_recv()

    def own_rows(self):
        return self.place(2)[3][0]

    def drain(self, first=0, last=10):
        for phase in range(3):
            for i in range(first, last):
                self.hop(phase, i).wait_send()


def stage(parts, name, phase):
    for part in parts:
        getattr(part, name)(phase)


def reduce_scatter(parts):
    for phase in range(3):
        for name in ("rs_start", "rs_mid", "rs_end"):
            stage(parts, name, phase)


def all_gather(parts):
    for phase in (2, 1, 0):
        for name in ("ag_start", "ag_mid", "ag_end"):
            stage(parts, name, phase)


def slab_rows(rb):
    return [3 * rb * RING ** (2 - phase) for phase in range(3)]


def place_in_order(block, order):
    digit = [(block // s) % RING for s in AXIS_STRIDE]
    return (digit[order[0]] * RING + digit[order[1]]) * RING + digit[order[2]]


def by_rows(n_rows, align):
    unit = n_rows // align
    counts = [(unit + 2 - c) // 3 for c in range(3)]
    starts = [sum(counts[:c]) * align for c in range(3)]
    return [(starts[c], counts[c] * align) for c in range(3)]


def pair(n):
    return [pltpu.SemaphoreType.DMA((n,)), pltpu.SemaphoreType.DMA((n,))]


def kv_gather_kernel(own_ref, all_ref, y0, y1, y2, s0, r0, s1, r1, s2, r2, out_sem):
    rows, lanes = own_ref.shape
    n_blk = RING ** 3
    split = by_rows(rows, 16)
    parts = []
    rings = [ring_of(axis) for axis in range(3)]
    for c, (y, s, r) in enumerate(((y0, s0, r0), (y1, s1, r1), (y2, s2, r2))):
        part = Part(rings, ORDERS[c], split[c][1], (s, r), y=y, lanes=(0, lanes), align=16)
        y[pl.ds(pl.multiple_of(part.own_rows(), 16), split[c][1]), :] = own_ref[pl.ds(*split[c]), :]
        parts.append(part)
    enter(rings)
    all_gather(parts)

    def body(blk, carry):
        for c, y in enumerate((y0, y1, y2)):
            at, rb = split[c]
            src = y.at[pl.ds(pl.multiple_of(place_in_order(blk, ORDERS[c]) * rb, 16), rb)]
            pltpu.make_async_copy(src, all_ref.at[pl.ds(pl.multiple_of(blk * rows + at, 16), rb)], out_sem.at[c]).start()
        return carry

    lax.fori_loop(0, n_blk, body, 0)
    for c, y in enumerate((y0, y1, y2)):
        pltpu.make_async_copy(y, all_ref.at[pl.ds(0, n_blk * split[c][1])], out_sem.at[c]).wait()
    for part in parts:
        part.drain(6, 10)


def kv_gather(own):
    rows, lanes = own.shape
    n_blk = RING ** 3
    split = by_rows(rows, 16)
    return pl.pallas_call(
        kv_gather_kernel,
        out_shape=jax.ShapeDtypeStruct((n_blk * rows, lanes), own.dtype),
        in_specs=[pl.BlockSpec(memory_space=pltpu.VMEM)],
        out_specs=pl.BlockSpec(memory_space=pl.ANY),
        scratch_shapes=[pltpu.VMEM((n_blk * rb, lanes), own.dtype) for _, rb in split] + pair(30) * 3 + [pltpu.SemaphoreType.DMA((3,))],
        compiler_params=pltpu.CompilerParams(collective_id=1, has_side_effects=True, vmem_limit_bytes=16 << 20),
        name="kv_gather",
    )(own)


def grad_layout(d_model, n_local):
    n_blk = RING ** 3
    q_tiles = d_model * n_local // 8 // n_blk
    o_tiles = d_model // 128
    q_count = [q_tiles * 13 // 32, q_tiles * 11 // 32]
    q_count.append(q_tiles - sum(q_count))
    o_count = [o_tiles * 5 // 16, o_tiles * 6 // 16]
    o_count.append(o_tiles - sum(o_count))
    q_rows = [8 * n for n in q_count]
    q_first = [n_blk * sum(q_rows[:c]) for c in range(3)]
    o_lanes = [(128 * sum(o_count[:c]), 128 * o_count[c]) for c in range(3)]
    return q_rows, q_first, o_lanes


def place_heads(dst, src):
    n_batch, n_local, block_len, head_dim = src.shape
    for b in range(n_batch):
        for h in range(n_local):
            dst[pl.ds(b * block_len, block_len), pl.ds(h * head_dim, head_dim)] = src[b, h]


D_TILE = 256


def bwd_kernel(kv_ref, q_ref, do_ref, o_ref, lse_ref, home_ref, grad_ref, cos_ref, sin_ref, dq_ref, dkv_ref, red0, red1, red2, qt_scr, dot_scr, dqt_scr, delta_scr, p_scr, ds_scr, xo, tok_scr, rot_scr, dqh_scr, *rest):
    recv, sems, ex_s, ex_r = rest[:9], rest[9:15], rest[15], rest[16]
    n_groups, n_cols, e_dim = q_ref.shape
    per_tile = TILE // BLK
    n_blk = RING ** 3
    d_model = grad_ref.shape[1]
    n_local, block_len = rot_scr.shape[1], rot_scr.shape[2]
    cp, tp = lax.axis_index("cp"), lax.axis_index("tp")
    mirror = n_blk - 1 - cp
    rings = [ring_of(axis) for axis in range(3)]
    group = cp // (n_blk // 2)
    _, _, o_lanes = grad_layout(d_model, n_local)
    parts = [Part(rings, ORDERS[c], n_cols // n_blk, sems[2 * c:2 * c + 2], x=xo, recv=recv[3 * c:3 * c + 3], lanes=o_lanes[c]) for c in range(3)]

    place_heads(tok_scr, home_ref)

    def o_body(i, carry):
        cols = pl.ds(pl.multiple_of(i * D_TILE, D_TILE), D_TILE)
        xo[:, cols] = dot_ta(tok_scr[...], grad_ref[:, cols])
        return carry

    lax.fori_loop(0, d_model // D_TILE, o_body, 0)
    enter(rings, with_partner=True, with_mirror=True)
    stage(parts, "rs_start", 0)

    for grp in range(n_groups):
        qt_scr[grp] = q_ref[grp].T
        dot_scr[grp] = do_ref[grp].T
        delta_scr[grp] = jnp.sum(dot_scr[grp].astype(F32) * o_ref[grp].T.astype(F32), axis=0, keepdims=True)
    dqt_scr[...] = jnp.zeros_like(dqt_scr)
    dkv_ref[...] = jnp.zeros_like(dkv_ref)

    def tile_step(grp, tile_idx, piece, masked):
        row0 = pl.multiple_of(tile_idx * TILE, TILE)
        k_t = kv_ref[pl.ds(row0, TILE), :e_dim]
        v_t = kv_ref[pl.ds(row0, TILE), e_dim:]
        for c0 in range(0, n_cols, COLS):
            cs = slice(c0, c0 + COLS)
            s = dot(k_t, qt_scr[grp, :, cs])
            p = jnp.exp(s - lse_ref[grp, :, cs])
            if masked:
                p = jnp.where(causal_mask(row0, piece * BLK, COLS), p, 0.0)
            d_p = dot(v_t, dot_scr[grp, :, cs])
            p_scr[:, cs] = p.astype(BF16)
            ds_scr[:, cs] = (p * (d_p - delta_scr[grp, :, cs])).astype(BF16)
        rows = pl.ds(row0, TILE)
        dkv_ref[rows, :e_dim] += dot(ds_scr[...], q_ref[grp])
        dkv_ref[rows, e_dim:] += dot(p_scr[...], do_ref[grp])
        dqt_scr[grp] += dot_ta(k_t, ds_scr[...])

    n_first = cp // per_tile + 1
    n_steps = n_blk // per_tile + 1

    def body(t, carry):
        grp = (t - n_first + n_steps) // n_steps
        piece = cp + grp * (mirror - cp)
        tile_idx = t - grp * n_first
        last = tile_idx == piece // per_tile

        @pl.when(jnp.logical_not(last))
        def _():
            tile_step(grp, tile_idx, piece, False)

        @pl.when(last)
        def _():
            tile_step(grp, tile_idx, piece, True)

        @pl.when(t == 5)
        def _():
            stage(parts, "rs_mid", 0)

        @pl.when(t == 13)
        def _():
            stage(parts, "rs_end", 0)
            stage(parts, "rs_start", 1)

        return carry

    lax.fori_loop(0, n_steps, body, 0)
    stage(parts, "rs_mid", 1)

    scale = e_dim ** -0.5
    half_dim = e_dim // 2
    for grp in range(n_groups):
        cos_t, sin_t = cos_ref[grp], sin_ref[grp]
        for h in range(n_local):
            cols = slice(h * block_len, (h + 1) * block_len)
            low, high = dqt_scr[grp, :half_dim, cols], dqt_scr[grp, half_dim:, cols]
            turned = jnp.concatenate([low * cos_t + high * sin_t, high * cos_t - low * sin_t], axis=0) * scale
            rot_scr[grp, h] = turned.T.astype(BF16)
    is_mine = tp == group

    def give(piece_idx, sem, device):
        return pltpu.make_async_remote_copy(src_ref=rot_scr.at[piece_idx], dst_ref=dqh_scr.at[tp], send_sem=ex_s.at[sem], recv_sem=ex_r.at[tp], device_id=device, device_id_type=MESH)

    def take(batch):
        return pltpu.make_async_remote_copy(src_ref=rot_scr.at[0], dst_ref=dqh_scr.at[batch], send_sem=ex_s.at[0], recv_sem=ex_r.at[batch], device_id=(group, mirror), device_id_type=MESH)

    give(1, 1, (group, mirror)).start()

    @pl.when(jnp.logical_not(is_mine))
    def _():
        give(0, 0, (1 - tp, cp)).start()

    @pl.when(is_mine)
    def _():
        dqh_scr[tp] = rot_scr[0]

    stage(parts, "rs_end", 1)
    for name in ("rs_start", "rs_mid", "rs_end"):
        stage(parts, name, 2)
    for part, out, lanes in zip(parts, (red0, red1, red2), o_lanes):
        out[...] = xo[pl.ds(pl.multiple_of(part.own_rows(), 8), part.rb), pl.ds(*lanes)]
    take(1 - tp).wait_recv()

    @pl.when(jnp.logical_not(is_mine))
    def _():
        take(tp).wait_recv()
        give(0, 0, (1 - tp, cp)).wait_send()

    give(1, 1, (group, mirror)).wait_send()
    dq_ref[...] = dqh_scr[...]
    for part in parts:
        part.drain(0, 6)


def attention_backward(kv_all, q_grp, do_grp, o_grp, lse, o_home, grad, cos_t, sin_t):
    n_groups, n_cols, e_dim = q_grp.shape
    n_tok, d_model = grad.shape
    n_blk = RING ** 3
    seq = kv_all.shape[0]
    _, _, o_lanes = grad_layout(d_model, o_home.shape[1])
    rb = n_cols // n_blk
    vmem = pl.BlockSpec(memory_space=pltpu.VMEM)
    return pl.pallas_call(
        bwd_kernel,
        out_shape=(jax.ShapeDtypeStruct(o_home.shape, BF16), jax.ShapeDtypeStruct((seq, 2 * e_dim), F32)) + tuple(jax.ShapeDtypeStruct((rb, n), F32) for _, n in o_lanes),
        in_specs=[vmem] * 9,
        out_specs=(vmem,) * 5,
        scratch_shapes=[
            pltpu.VMEM((n_groups, e_dim, n_cols), BF16),
            pltpu.VMEM((n_groups, e_dim, n_cols), BF16),
            pltpu.VMEM((n_groups, e_dim, n_cols), F32),
            pltpu.VMEM((n_groups, 1, n_cols), F32),
            pltpu.VMEM((TILE, n_cols), BF16),
            pltpu.VMEM((TILE, n_cols), BF16),
            pltpu.VMEM((n_cols, d_model), F32),
            pltpu.VMEM((n_tok, n_cols), BF16),
            pltpu.VMEM(o_home.shape, BF16),
            pltpu.VMEM(o_home.shape, BF16),
        ]
        + [pltpu.VMEM((n, lanes), F32) for _, lanes in o_lanes for n in slab_rows(rb)]
        + pair(30) * 3
        + pair(2),
        compiler_params=pltpu.CompilerParams(collective_id=2, has_side_effects=True, vmem_limit_bytes=60 << 20),
        name="attn_bwd",
    )(kv_all, q_grp, do_grp, o_grp, lse, o_home, grad, cos_t, sin_t)


def grad_kernel(dkv_ref, hid_ref, dqh_ref, red0, red1, red2, cos_ref, sin_ref, gq_ref, go_ref, gk_ref, gv_ref, dkd_ref, x0, x1, x2, xq, xk, yq, yo, yk, yp, tok_scr, mine_scr, give_scr, got_scr, *rest):
    n_parts = 10
    recv, sems, in_sem, out_sem, swap_s, swap_r = rest[:21], rest[21:21 + 2 * n_parts], rest[-4], rest[-3], rest[-2], rest[-1]
    n_blk = RING ** 3
    n_tok, d_model = hid_ref.shape
    n_batch, n_local, block_len, head_dim = dqh_ref.shape
    n_cols = n_local * head_dim
    rows, lanes = block_len, 2 * head_dim
    q_rows, q_first, o_lanes = grad_layout(d_model, n_local)
    split = by_rows(rows, 8)
    tp, cp = lax.axis_index("tp"), lax.axis_index("cp")
    partner = (1 - tp, cp)
    xs = (x0, x1, x2)
    rings = [ring_of(axis) for axis in range(3)]

    def sem(i):
        return sems[2 * i:2 * i + 2]

    p_d = [Part(rings, ORDERS[c], split[c][1], sem(c), x=xs[c], recv=recv[3 * c:3 * c + 3], lanes=(0, lanes)) for c in range(3)]
    p_q = [Part(rings, ORDERS[c], q_rows[c], sem(3 + c), x=xq, y=yq, recv=recv[9 + 3 * c:12 + 3 * c], row0=q_first[c], lanes=(0, 128)) for c in range(3)]
    p_o = [Part(rings, ORDERS[c], n_cols // n_blk, sem(6 + c), y=yo, lanes=o_lanes[c]) for c in range(3)]
    p_k = Part(rings, ORDERS[2], d_model // n_blk, sem(9), x=xk, y=yk, recv=recv[18:21], lanes=(0, 128))
    p_qo = p_q + p_o

    def load(blk, carry):
        for c in range(3):
            at, rb = split[c]
            dst = xs[c].at[pl.ds(pl.multiple_of(place_in_order(blk, ORDERS[c]) * rb, 8), rb)]
            pltpu.make_async_copy(dkv_ref.at[pl.ds(pl.multiple_of(blk * rows + at, 8), rb)], dst, in_sem.at[c]).start()
        return carry

    lax.fori_loop(0, n_blk, load, 0)
    enter(rings, with_partner=True)
    for c in range(3):
        pltpu.make_async_copy(dkv_ref.at[pl.ds(0, n_blk * split[c][1])], xs[c], in_sem.at[c]).wait()
        p_d[c].rs_start(0)

    place_heads(tok_scr, dqh_ref)

    def q_body(i, carry):
        cols = pl.ds(pl.multiple_of(i * D_TILE, D_TILE), D_TILE)
        res = dot_ta(hid_ref[:, cols], tok_scr[...])
        for h in range(n_local):
            xq[pl.ds(i * D_TILE * n_local + h, D_TILE, stride=n_local), :] = res[:, h * head_dim:(h + 1) * head_dim]
        return carry

    lax.fori_loop(0, d_model // D_TILE, q_body, 0)
    stage(p_d, "rs_mid", 0)
    stage(p_q, "rs_start", 0)
    for part, red in zip(p_o, (red0, red1, red2)):
        part.y[pl.ds(pl.multiple_of(part.own_rows(), 8), part.rb), pl.ds(*part.lanes)] = red[...]
    stage(p_d, "rs_end", 0)
    stage(p_d, "rs_start", 1)
    stage(p_q, "rs_mid", 0)
    stage(p_d, "rs_mid", 1)
    stage(p_d, "rs_end", 1)
    stage(p_d, "rs_start", 2)
    stage(p_q, "rs_end", 0)
    stage(p_q, "rs_start", 1)
    stage(p_d, "rs_mid", 2)
    stage(p_d, "rs_end", 2)

    half_dim = head_dim // 2
    first = tp == 0
    for c in range(3):
        at, rb = split[c]
        own = xs[c][pl.ds(pl.multiple_of(p_d[c].own_rows(), 8), rb), :]
        cos_tab, sin_tab = cos_ref[pl.ds(at, rb), :], sin_ref[pl.ds(at, rb), :]
        low, high = own[:, :half_dim], own[:, half_dim:head_dim]
        mine_scr[pl.ds(at, rb), :head_dim] = jnp.concatenate([low * cos_tab + high * sin_tab, high * cos_tab - low * sin_tab], axis=1)
        mine_scr[pl.ds(at, rb), head_dim:] = own[:, head_dim:]
    both = mine_scr[...].astype(BF16)
    dkd_ref[...] = both
    dk_new, dv_new = both[:, :head_dim], both[:, head_dim:]
    give_scr[...] = jnp.where(first, dv_new, dk_new)
    keep = jnp.where(first, dk_new, dv_new)
    swap_small = pltpu.make_async_remote_copy(src_ref=give_scr, dst_ref=got_scr, send_sem=swap_s.at[0], recv_sem=swap_r.at[0], device_id=partner, device_id_type=MESH)
    swap_small.start()
    stage(p_q, "rs_mid", 1)
    swap_small.wait()
    got = got_scr[...]
    kv_tok = jnp.concatenate([jnp.where(first, keep, got), jnp.where(first, got, keep)], axis=0)
    for i in range(d_model // D_TILE):
        xk[pl.ds(i * D_TILE, D_TILE), :] = dot_ta(hid_ref[:, i * D_TILE:(i + 1) * D_TILE], kv_tok)
    p_k.rs_start(0)
    stage(p_q, "rs_end", 1)
    stage(p_q, "rs_start", 2)
    p_k.rs_mid(0)
    stage(p_q, "rs_mid", 2)
    p_k.rs_end(0)
    p_k.rs_start(1)
    stage(p_q, "rs_end", 2)
    for part in p_q:
        own = pl.ds(pl.multiple_of(part.own_rows(), 8), part.rb)
        yq[own, :] = xq[own, :]
    stage(p_qo, "ag_start", 2)
    p_k.rs_mid(1)
    stage(p_qo, "ag_mid", 2)
    p_k.rs_end(1)
    p_k.rs_start(2)
    stage(p_qo, "ag_end", 2)
    stage(p_qo, "ag_start", 1)
    p_k.rs_mid(2)
    stage(p_qo, "ag_mid", 1)
    p_k.rs_end(2)
    own = pl.ds(pl.multiple_of(p_k.own_rows(), 8), p_k.rb)
    yk[own, :] = xk[own, :]
    p_k.ag_start(2)
    stage(p_qo, "ag_end", 1)
    p_k.ag_mid(2)
    p_k.ag_end(2)
    for name in ("ag_start", "ag_mid", "ag_end"):
        getattr(p_k, name)(1)
    p_all = p_qo + [p_k]
    stage(p_all, "ag_start", 0)

    def put(part, which):
        out = gq_ref if part.y is yq else go_ref
        slab, _, _, starts, _, _ = part.place(0)
        src, dst = part.view(part.y, starts[which], slab), part.view(out, starts[which], slab)
        pltpu.make_async_copy(src, dst, out_sem.at[p_qo.index(part)]).start()

    for part in p_qo:
        put(part, 0)
    stage(p_all, "ag_mid", 0)
    for part in p_qo:
        put(part, 1)
        put(part, 3)
    p_k.ag_end(0)
    swap = pltpu.make_async_remote_copy(src_ref=yk, dst_ref=yp, send_sem=swap_s.at[1], recv_sem=swap_r.at[1], device_id=partner, device_id_type=MESH)
    swap.start()
    for part in p_qo:
        part.ag_end(0)
        put(part, 2)
    swap.wait()

    def put_kv(k_src, v_src):
        outs = [pltpu.make_async_copy(k_src, gk_ref, out_sem.at[6]), pltpu.make_async_copy(v_src, gv_ref, out_sem.at[7])]
        for copy in outs:
            copy.start()
        for copy in outs:
            copy.wait()

    @pl.when(first)
    def _():
        put_kv(yk, yp)

    @pl.when(jnp.logical_not(first))
    def _():
        put_kv(yp, yk)

    for i, part in enumerate(p_qo):
        out = gq_ref if part.y is yq else go_ref
        span = n_blk * part.rb
        pltpu.make_async_copy(part.view(part.y, part.row0, span), part.view(out, part.row0, span), out_sem.at[i]).wait()
    for part in p_d:
        part.drain(0, 6)
    for part in p_q + [p_k]:
        part.drain(0, 10)
    for part in p_o:
        part.drain(6, 10)


def grad_sums(dkv, hid, dq_home, reds, cos_tab, sin_tab):
    n_tok, d_model = hid.shape
    n_batch, n_local, block_len, head_dim = dq_home.shape
    n_cols = n_local * head_dim
    n_blk = RING ** 3
    lanes = 2 * head_dim
    q_rows, _, _ = grad_layout(d_model, n_local)
    split = by_rows(block_len, 8)
    recv = [pltpu.VMEM((n, lanes), F32) for _, rb in split for n in slab_rows(rb)]
    recv += [pltpu.VMEM((n, 128), F32) for rb in q_rows for n in slab_rows(rb)]
    recv += [pltpu.VMEM((n, 128), F32) for n in slab_rows(d_model // n_blk)]
    vmem, anyspace = pl.BlockSpec(memory_space=pltpu.VMEM), pl.BlockSpec(memory_space=pl.ANY)
    xq, xo, xk = (pltpu.VMEM(s, F32) for s in ((d_model * n_local, 128), (n_cols, d_model), (d_model, 128)))
    small = pltpu.VMEM((block_len, head_dim), BF16)
    return pl.pallas_call(
        grad_kernel,
        out_shape=(
            jax.ShapeDtypeStruct((d_model * n_local, 128), F32),
            jax.ShapeDtypeStruct((n_cols, d_model), F32),
            jax.ShapeDtypeStruct((d_model, 128), F32),
            jax.ShapeDtypeStruct((d_model, 128), F32),
            jax.ShapeDtypeStruct((block_len, lanes), BF16),
        ),
        in_specs=[anyspace] + [vmem] * 7,
        out_specs=(anyspace,) * 4 + (vmem,),
        scratch_shapes=[pltpu.VMEM((n_blk * rb, lanes), F32) for _, rb in split]
        + [xq, xk, xq, xo, xk, xk, pltpu.VMEM((n_tok, n_cols), BF16), pltpu.VMEM((block_len, lanes), F32), small, small]
        + recv
        + pair(30) * 10
        + [pltpu.SemaphoreType.DMA((3,)), pltpu.SemaphoreType.DMA((8,))]
        + pair(2),
        compiler_params=pltpu.CompilerParams(collective_id=3, has_side_effects=True, vmem_limit_bytes=67000000),
        name="grad_sums",
    )(dkv, hid, dq_home, *reds, cos_tab, sin_tab)


def solution(mesh):
    cp_size = mesh.shape["cp"]
    half = cp_size // 2
    axes = ("tp", "cp")

    def flat(tp, cp):
        return tp * cp_size + cp

    route_a, route_b = [], []
    for cp in range(cp_size):
        mine, mirror = int(cp >= half), cp_size - 1 - cp
        route_b.append((flat(mine, cp), flat(1 - mine, cp)))
        route_b.append((flat(1 - mine, cp), flat(1 - mine, mirror)))
        route_a.append((flat(1 - mine, cp), flat(mine, mirror)))
    back_a = [(dst, src) for src, dst in route_a]
    back_b = [(dst, src) for src, dst in route_b]
    partner = [(0, 1), (1, 0)]

    def exchange(own_of, is_mine, plan_a, plan_b, send_a, send_b):
        got_a = lax.ppermute(send_a, axes, plan_a)
        got_b = lax.ppermute(send_b, axes, plan_b)
        return jnp.where(is_mine, own_of, got_b), jnp.where(is_mine, got_b, got_a)

    def local_program(hidden, grad_out, w_query, w_key, w_value, w_out):
        block_len = hidden.shape[1]
        n_local = w_query.shape[1]
        head_dim = w_key.shape[1]
        q_scale = head_dim ** -0.5
        cp_idx = lax.axis_index("cp")
        tp_idx = lax.axis_index("tp")
        is_mine = tp_idx == (cp_idx >= half).astype(jnp.int32)
        mirror_idx = cp_size - 1 - cp_idx
        pieces = jnp.stack([cp_idx, mirror_idx]).astype(jnp.int32)
        cos_tab, sin_tab = rope_tables(cp_idx * block_len + jnp.arange(block_len), head_dim)
        cos_mir, sin_mir = rope_tables(mirror_idx * block_len + jnp.arange(block_len), head_dim)

        def pick(pair, idx):
            return lax.dynamic_index_in_dim(pair, idx, 0, keepdims=False)

        def to_workers(x):
            own, other = pick(x, tp_idx), pick(x, 1 - tp_idx)
            return exchange(own, is_mine, route_a, route_b, other, jnp.where(is_mine, other, own))

        def to_homes(own_piece, mir_piece):
            mine, other = exchange(own_piece, is_mine, back_a, back_b, mir_piece, jnp.where(is_mine, mir_piece, own_piece))
            first = tp_idx == 0
            return jnp.stack([jnp.where(first, mine, other), jnp.where(first, other, mine)])

        def sum_over_tp(part, extra=None):
            total = pick(part, tp_idx) + lax.ppermute(pick(part, 1 - tp_idx), "tp", partner)
            if extra is not None:
                total = total + extra
            mine = total.astype(BF16)
            other = lax.ppermute(mine, "tp", partner)
            first = tp_idx == 0
            return jnp.stack([jnp.where(first, mine, other), jnp.where(first, other, mine)])

        hid_b = pick(hidden, tp_idx)
        key_loc = rotate(dot(hid_b, w_key), cos_tab, sin_tab).astype(BF16)
        val_loc = dot(hid_b, w_value).astype(BF16)
        kv_all = kv_gather(jnp.concatenate([key_loc, val_loc], axis=1))

        q_pre = jnp.einsum("bsd,dhe->bhse", hidden, w_query, preferred_element_type=F32)
        queries = (rotate(q_pre, cos_tab, sin_tab) * q_scale).astype(BF16)
        d_out = jnp.einsum("bsd,hed->bhse", grad_out, w_out, preferred_element_type=F32).astype(BF16)
        own_qd, mir_qd = to_workers(jnp.stack([queries, d_out], axis=1))
        grp_shape = (2, n_local * block_len, head_dim)
        q_grp = jnp.stack([own_qd[0], mir_qd[0]]).reshape(grp_shape)
        do_grp = jnp.stack([own_qd[1], mir_qd[1]]).reshape(grp_shape)

        o_grp, lse = attention_forward(pieces, kv_all, q_grp)
        o_split = o_grp.reshape(2, n_local, block_len, head_dim)
        attn_heads = to_homes(o_split[0], o_split[1])
        attn_out = sum_over_tp(jnp.einsum("cirf,ife->cre", attn_heads, w_out, preferred_element_type=F32))

        tabs_t = [jnp.stack(pair_t) for pair_t in ((cos_tab.T, cos_mir.T), (sin_tab.T, sin_mir.T))]
        dq_pre, dkv, *reds = attention_backward(kv_all, q_grp, do_grp, o_grp, lse, attn_heads, grad_out.reshape(-1, grad_out.shape[-1]), *tabs_t)
        grad_q, grad_o, d_w_key, d_w_value, dkv_new = grad_sums(dkv, hidden.reshape(-1, hidden.shape[-1]), dq_pre, reds, cos_tab, sin_tab)
        d_w_query = grad_q.reshape(w_query.shape)
        d_w_out = grad_o.reshape(w_out.shape)
        dk_pre, dv_pre = dkv_new[:, :head_dim], dkv_new[:, head_dim:]
        dh_kv = dot(dk_pre, w_key.T) + dot(dv_pre, w_value.T)
        d_hidden = sum_over_tp(jnp.einsum("cirf,eif->cre", dq_pre, w_query, preferred_element_type=F32), dh_kv)
        return attn_out, d_hidden, d_w_query, d_w_key, d_w_value, d_w_out

    row_spec = P(None, "cp", None)
    return jax.shard_map(local_program, mesh=mesh, in_specs=(row_spec, row_spec, P(None, "tp", None), P(), P(), P("tp", None, None)), out_specs=(row_spec, row_spec, P(None, "tp", None), P(), P(), P("tp", None, None)), check_vma=False)
```

time: 411 us -> 394 us (0.959)
  starting transfers between devices: 39.4 us -> 27.1 us
  Pallas kernels: 321 us -> 311 us
  matrix products: 12.3 us -> 18 us
  other arithmetic: 13.2 us -> 8.83 us
    ppermute x1 -> x0, starting transfers between devices: 11 us -> none  [local_program(): other_kv = lax.ppermute(jnp.where(first, dv_pre, dk_pre), 'tp', partner)]
    pallas_call x3 -> x2, Pallas kernels: 248 us -> 238 us  [the longest x1 178 us: grad_sums(): pl.pallas_call(grad_kernel, out_shape=(jax.ShapeDtypeStruct((d_model * n_...]
    ppermute x3 -> x2, waiting for transfers between devices: 4.52 us -> 8.83 us  [exchange(): got_b = lax.ppermute(send_b, axes, plan_b)]
    ppermute x3 -> x2, starting transfers between devices: 13.5 us -> 13.9 us  [exchange(): got_a = lax.ppermute(send_a, axes, plan_a)]
    ppermute x3 -> x2, starting transfers between devices: 9.69 us -> 9.58 us  [exchange(): got_b = lax.ppermute(send_b, axes, plan_b)]
    unnamed x34 -> x44, local copies, waits for them, and re-layouts: 15.2 us -> 15.1 us
  transfers between devices with their start and end apart: 11 -> 8, of which waited for: 2 -> 2; matrix products, arithmetic and copies ran while one was open for 3% -> 3% of each run, Pallas kernels for 51% -> 56%
where the time goes in v2:
time: 394 us
  Pallas kernels  311 us (79%)
  starting transfers between devices  27.1 us (7%)
  local copies, waits for them, and re-layouts  18.2 us (5%)
  matrix products  18 us (5%)
  waiting for transfers between devices  9.24 us (2%)
  other arithmetic  8.83 us (2%)
    pallas_call x1, Pallas kernels, grad_sums(): pl.pallas_call(grad_kernel, out_shape=(jax.ShapeDtypeStruct((d_model * n_...  178 us
    pallas_call x1, Pallas kernels, attention_backward(): pl.pallas_call(bwd_kernel, out_shape=(jax.ShapeDtypeStruct(o_home.shape,...  60 us
    pallas_call x1, Pallas kernels, kv_gather(): pl.pallas_call(kv_gather_kernel, out_shape=jax.ShapeDtypeStruct((n_blk *...  42.6 us
    pallas_call x1, Pallas kernels, attention_forward(): pl.pallas_call(fwd_kernel, out_shape=(jax.ShapeDtypeStruct(q_grp.shape, B...  30.4 us
    unnamed x44, local copies, waits for them, and re-layouts  15.1 us
    ppermute x2, starting transfers between devices, exchange(): got_a = lax.ppermute(send_a, axes, plan_a)  13.9 us
    ppermute x2, starting transfers between devices, exchange(): got_b = lax.ppermute(send_b, axes, plan_b)  9.58 us
    ppermute x2, waiting for transfers between devices, exchange(): got_b = lax.ppermute(send_b, axes, plan_b)  8.83 us
  transfers between devices with their start and end apart: 8, of which 2 were waited for; matrix products, arithmetic and copies ran while one was open for 3% of the time, Pallas kernels for 56%

profile of v2, /device:TPU:1, one launch (start us, length us, event | category | flops | bytes accessed | tf_op | source)
XLA Modules:
  0.0 393.8 jit_solution(5642046113269762287)
XLA Ops:
  0.7 1.5 fusion.33
  2.2 0.3 multiply_cosine_fusion
  2.5 0.1 copy.35
  2.6 0.1 copy.36
  2.7 0.5 copy-done.13
  3.1 0.0 copy-done.14
  3.1 3.9 fusion.15
  7.1 0.2 subtract_bitcast_fusion
  7.2 0.1 fusion.24
  7.4 3.5 fusion.21
  10.9 0.0 copy-start.5
  10.9 0.0 copy-start.9
  10.9 0.1 fusion.30
  11.0 0.3 copy.38
  11.3 0.3 copy.39
  11.6 0.1 bitcast_select_fusion.1
  11.7 9.3 %collective-permute-start = (bf16[2,8,128,128]{3,2,1,0:T(8,128)(2,1)S(1)}, bf16[2,8,128,128]{3,2,1,0:T(8,128)(2,1)}, u32[]{:S(2)}, u32[]{:S(2)}) collective-permute-start(bf16[2,8,128,128]{3,2,1,0:T(8,128)(2,1)S(1)} %bitcast_select_fusion.1), channel_id=1, source_target_pairs={{0,64},{64,127},{1,65},{65,126},{2,66},{66,125},{3,67},{67,124},{4... | collective-permute-start | bytes 1572872 | tf_op jit(solution)/shard_map/ppermute | solution.py:721
  21.0 2.5 collective-permute-start.1
  23.5 0.3 convolution_convert_fusion
  23.8 0.1 pad_maximum_fusion.5.own_ref
  23.9 42.6 %kv_gather.1.kv_ref = bf16[8192,256]{1,0:T(8,128)(2,1)S(1)} custom-call(bf16[128,256]{1,0:T(8,128)(2,1)S(1)} %pad_maximum_fusion.5.own_ref), custom_call_target="tpu_custom_call" | custom-call | tf_op jit(solution)/shard_map/kv_gather/pallas_call | solution.py:308
  66.5 0.0 copy-start
  66.5 2.0 copy-done
  68.6 0.1 pad_add_fusion.piece_ref
  68.6 1.4 bitcast_select_fusion
  70.1 0.1 fusion.44
  70.2 0.1 pad_maximum_fusion.2
  70.2 0.0 copy-start.2
  70.2 0.8 copy-done.1
  71.1 30.4 %attn_fwd.1 = (bf16[2,1024,128]{2,1,0:T(8,128)(2,1)S(1)}, f32[2,1,1024]{2,1,0:T(1,128)S(1)}) custom-call(s32[2]{0:T(128)S(1)} %pad_add_fusion.piece_ref, bf16[8192,256]{1,0:T(8,128)(2,1)S(1)} %copy-done.1, bf16[2,1024,128]{2,1,0:T(8,128)(2,1)S(1)} %bitcast.92), custom_call_target="tpu_custom_call" | custom-call | flops 4294967296 | bytes 4194304 | tf_op jit(solution)/shard_map/attn_fwd/pallas_call | solution.py:92
  101.4 0.6 copy-done.4
  102.1 11.4 %collective-permute-start.3 = (bf16[8,128,128]{2,1,0:T(8,128)(2,1)S(1)}, bf16[8,128,128]{2,1,0:T(8,128)(2,1)S(1)}, u32[]{:S(2)}, u32[]{:S(2)}) collective-permute-start(bf16[8,128,128]{2,1,0:T(8,128)(2,1)S(1)} %bitcast.106), channel_id=1, source_target_pairs={{63,64},{62,65},{61,66},{60,67},{59,68},{58,69},{57,70},{56,71},{5... | collective-permute-start | bytes 786440 | tf_op jit(solution)/shard_map/ppermute | solution.py:720
  113.5 0.3 collective-permute-start.2
  113.7 0.3 multiply_sine_fusion.2
  114.1 0.7 pad_maximum_fusion.6
  114.7 0.8 pad_maximum_fusion.4
  115.6 8.8 %collective-permute-done.2 = bf16[8,128,128]{2,1,0:T(8,128)(2,1)S(1)} collective-permute-done((bf16[8,128,128]{2,1,0:T(8,128)(2,1)S(1)}, bf16[8,128,128]{2,1,0:T(8,128)(2,1)S(1)}, u32[]{:S(2)}, u32[]{:S(2)}) %collective-permute-start.2) | collective-permute-done | bytes 262176 | tf_op jit(solution)/shard_map/ppermute | solution.py:721
  124.4 0.8 pad_maximum_fusion.3.home_ref
  125.3 60.0 %attn_bwd.1 = (bf16[2,8,128,128]{3,2,1,0:T(8,128)(2,1)}, f32[8192,256]{1,0:T(8,128)}, f32[16,640]{1,0:T(8,128)}, f32[16,768]{1,0:T(8,128)}, f32[16,640]{1,0:T(8,128)}) custom-call(bf16[8192,256]{1,0:T(8,128)(2,1)} %copy-done, bf16[2,1024,128]{2,1,0:T(8,128)(2,1)} %bitcast.93, bf16[2,1024,128]{2,1,0:T(8,128)(2,1)} %bitcast.103, ...), custom_call_target="tpu_custom_call" | custom-call | tf_op jit(solution)/shard_map/attn_bwd/pallas_call | solution.py:477
  185.3 0.0 copy-start.15
  185.4 3.8 fusion.12
  189.1 0.0 copy-start.6
  189.2 1.1 dynamic-slice_bitcast_fusion
  190.3 2.9 collective-permute-start.6
  193.2 1.3 fusion.9
  194.6 1.1 dynamic-slice_bitcast_fusion.1
  195.7 0.5 copy-done.7
  196.2 178.3 %grad_sums.1 = (f32[16384,128]{1,0:T(8,128)}, f32[1024,2048]{1,0:T(8,128)}, f32[2048,128]{1,0:T(8,128)}, f32[2048,128]{1,0:T(8,128)}, bf16[128,256]{1,0:T(8,128)(2,1)}) custom-call(f32[8192,256]{1,0:T(8,128)} %get-tuple-element.21.dkv_ref, bf16[256,2048]{1,0:T(8,128)(2,1)} %bitcast.100, bf16[2,8,128,128]{3,2,1,0:T(8,128)(2,1)} %get-tuple-element.20.dqh_ref, ...), custom_call_target="tpu_custom_call" | custom-call | tf_op jit(solution)/shard_map/grad_sums/pallas_call | solution.py:679
  374.6 0.0 copy-start.8
  374.6 1.5 fusion.40
  376.1 2.2 fusion.26
  378.3 0.2 collective-permute-start.7
  378.6 1.4 fusion.27
  380.0 0.4 collective-permute-start.5
  380.4 0.1 select_bitcast_fusion.1
  380.5 1.1 pad_maximum_fusion.1
  381.6 0.4 collective-permute-done.5
  382.0 0.1 select_bitcast_fusion.3
  382.0 1.1 pad_maximum_fusion
  383.1 4.3 %copy.64 = f32[2048,8,128]{2,1,0:T(8,128)} copy(f32[2048,8,128]{2,1,0:T(8,128)S(1)} %bitcast.99) | data formatting | bytes 16777216
  387.4 1.0 copy.65
  388.4 1.0 copy.66
  389.3 1.0 slice-done.1
  390.4 3.4 copy.67
  (41 shorter events, 0.2 us)
Async XLA Ops:
  2.5 0.6 copy-start.13
  2.5 0.6 copy-start.14
  3.1 4.3 %copy-start.12 = (bf16[2,128,2048]{2,1,0:T(8,128)(2,1)S(1)}, bf16[2,128,2048]{2,1,0:T(8,128)(2,1)}, u32[]{:S(2)}) copy-start(bf16[2,128,2048]{2,1,0:T(8,128)(2,1)} %param.7) | copy-start | bytes 3145732
  10.9 12.6 %copy-start.5 = (bf16[2,128,2048]{2,1,0:T(8,128)(2,1)S(1)}, bf16[2,128,2048]{2,1,0:T(8,128)(2,1)}, u32[]{:S(2)}) copy-start(bf16[2,128,2048]{2,1,0:T(8,128)(2,1)} %param.6) | copy-start | bytes 3145732
  10.9 12.6 %copy-start.9 = (bf16[2048,128]{1,0:T(8,128)(2,1)S(1)}, bf16[2048,128]{1,0:T(8,128)(2,1)}, u32[]{:S(2)}) copy-start(bf16[2048,128]{1,0:T(8,128)(2,1)} %param.10) | copy-start | bytes 1572868
  11.7 57.0 %collective-permute-start = (bf16[2,8,128,128]{3,2,1,0:T(8,128)(2,1)S(1)}, bf16[2,8,128,128]{3,2,1,0:T(8,128)(2,1)}, u32[]{:S(2)}, u32[]{:S(2)}) collective-permute-start(bf16[2,8,128,128]{3,2,1,0:T(8,128)(2,1)S(1)} %bitcast_select_fusion.1), channel_id=1, source_target_pairs={{0,64},{64,127},{1,65},{65,126},{2,66},{66,125},{3,67},{67,124},{4... | collective-permute-start | bytes 1572872 | tf_op jit(solution)/shard_map/ppermute | solution.py:721
  21.0 47.7 %collective-permute-start.1 = (bf16[2,8,128,128]{3,2,1,0:T(8,128)(2,1)S(1)}, bf16[2,8,128,128]{3,2,1,0:T(8,128)(2,1)}, u32[]{:S(2)}, u32[]{:S(2)}) collective-permute-start(bf16[2,8,128,128]{3,2,1,0:T(8,128)(2,1)S(1)} %bitcast.104), channel_id=1, source_target_pairs={{64,63},{65,62},{66,61},{67,60},{68,59},{69,58},{70,57},{71,56},{7... | collective-permute-start | bytes 1572872 | tf_op jit(solution)/shard_map/ppermute | solution.py:720
  66.5 2.0 copy-start
  68.6 2.5 copy-start.1
  70.2 31.2 %copy-start.2 = (bf16[2,8,128,128]{3,2,1,0:T(8,128)(2,1)}, bf16[2,8,128,128]{3,2,1,0:T(8,128)(2,1)S(1)}, u32[]{:S(2)}) copy-start(bf16[2,8,128,128]{3,2,1,0:T(8,128)(2,1)S(1)} %pad_maximum_fusion.2) | copy-start | bytes 1572868
  101.4 0.6 copy-start.4
  102.0 23.3 %copy-start.3 = (bf16[2,1024,128]{2,1,0:T(8,128)(2,1)}, bf16[2,1024,128]{2,1,0:T(8,128)(2,1)S(1)}, u32[]{:S(2)}) copy-start(bf16[2,1024,128]{2,1,0:T(8,128)(2,1)S(1)} %get-tuple-element.18.o_ref) | copy-start | bytes 1572868
  102.1 22.3 %collective-permute-start.3 = (bf16[8,128,128]{2,1,0:T(8,128)(2,1)S(1)}, bf16[8,128,128]{2,1,0:T(8,128)(2,1)S(1)}, u32[]{:S(2)}, u32[]{:S(2)}) collective-permute-start(bf16[8,128,128]{2,1,0:T(8,128)(2,1)S(1)} %bitcast.106), channel_id=1, source_target_pairs={{63,64},{62,65},{61,66},{60,67},{59,68},{58,69},{57,70},{56,71},{5... | collective-permute-start | bytes 786440 | tf_op jit(solution)/shard_map/ppermute | solution.py:720
  113.5 10.9 %collective-permute-start.2 = (bf16[8,128,128]{2,1,0:T(8,128)(2,1)S(1)}, bf16[8,128,128]{2,1,0:T(8,128)(2,1)S(1)}, u32[]{:S(2)}, u32[]{:S(2)}) collective-permute-start(bf16[8,128,128]{2,1,0:T(8,128)(2,1)S(1)} %broadcast_select_fusion.3), channel_id=1, source_target_pairs={{64,0},{127,64},{65,1},{126,65},{66,2},{125,66},{67,3},{124,67},{6... | collective-permute-start | bytes 786440 | tf_op jit(solution)/shard_map/ppermute | solution.py:721
  185.3 7.9 %copy-start.15 = (bf16[8,128,2048]{2,1,0:T(8,128)(2,1)S(1)}, bf16[8,128,2048]{2,1,0:T(8,128)(2,1)}, u32[]{:S(2)}) copy-start(bf16[8,128,2048]{2,1,0:T(8,128)(2,1)} %param.11) | copy-start | bytes 12582916
  189.1 5.4 %copy-start.6 = (f32[2,128,2048]{2,1,0:T(8,128)}, f32[2,128,2048]{2,1,0:T(8,128)S(1)}, u32[]{:S(2)}) copy-start(f32[2,128,2048]{2,1,0:T(8,128)S(1)} %fusion.12) | copy-start | bytes 6291460
  190.3 185.8 %collective-permute-start.6 = (f32[128,2048]{1,0:T(8,128)}, f32[128,2048]{1,0:T(8,128)}, u32[]{:S(2)}, u32[]{:S(2)}) collective-permute-start(f32[128,2048]{1,0:T(8,128)} %dynamic-slice_bitcast_fusion), channel_id=1, source_target_pairs={{0,64},{64,0},{1,65},{65,1},{2,66},{66,2},{3,67},{67,3},{4,68},{68... | collective-permute-start | bytes 3145736 | tf_op jit(solution)/shard_map/ppermute | solution.py:750
  194.5 1.7 copy-start.7
  196.2 182.4 %collective-permute-start.4 = (f32[128,2048]{1,0:T(8,128)}, f32[128,2048]{1,0:T(8,128)}, u32[]{:S(2)}, u32[]{:S(2)}) collective-permute-start(f32[128,2048]{1,0:T(8,128)} %dynamic-slice_bitcast_fusion.1), channel_id=1, source_target_pairs={{0,64},{64,0},{1,65},{65,1},{2,66},{66,2},{3,67},{67,3},{4,68},{68... | collective-permute-start | bytes 3145736 | tf_op jit(solution)/shard_map/ppermute | solution.py:750
  374.6 4.0 %copy-start.8 = (f32[2,128,2048]{2,1,0:T(8,128)S(1)}, f32[2,128,2048]{2,1,0:T(8,128)}, u32[]{:S(2)}) copy-start(f32[2,128,2048]{2,1,0:T(8,128)} %copy-done.7) | copy-start | bytes 6291460
  376.1 7.0 %slice-start.2 = ((s8[8388608]{0:T(1024)(128)(4,1)}), s8[4194304]{0:T(1024)(128)(4,1)S(1)}, s32[]{:S(2)}) async-start(s8[8388608]{0:T(1024)(128)(4,1)} %bitcast.97), calls=%async_computation.2 | async-start | bytes 8388608
  378.3 2.1 collective-permute-start.7
  380.0 3.2 slice-start.3
  380.0 2.0 collective-permute-start.5
  382.0 7.3 %slice-start = ((s8[8388608]{0:T(1024)(128)(4,1)}), s8[4194304]{0:T(1024)(128)(4,1)S(1)}, s32[]{:S(2)}) async-start(s8[8388608]{0:T(1024)(128)(4,1)} %bitcast.94), calls=%async_computation | async-start | bytes 8388608
  383.1 4.3 %copy-start.11 = (f32[2048,128]{1,0:T(8,128)S(1)}, f32[2048,128]{1,0:T(8,128)}, u32[]{:S(2)}) copy-start(f32[2048,128]{1,0:T(8,128)} %get-tuple-element.73) | copy-start | bytes 3145732
  383.1 5.3 %copy-start.10 = (f32[2048,128]{1,0:T(8,128)S(1)}, f32[2048,128]{1,0:T(8,128)}, u32[]{:S(2)}) copy-start(f32[2048,128]{1,0:T(8,128)} %get-tuple-element.74) | copy-start | bytes 3145732
  383.1 7.2 %slice-start.1 = ((s8[8388608]{0:T(1024)(128)(4,1)}), s8[4194304]{0:T(1024)(128)(4,1)S(1)}, s32[]{:S(2)}) async-start(s8[8388608]{0:T(1024)(128)(4,1)} %bitcast.94), calls=%async_computation.1 | async-start | bytes 8388608

commit v3 on v0

v3 whole, which is shorter than its diff:
```python
import jax
import jax.numpy as jnp
from jax import lax
from jax.experimental import pallas as pl
from jax.experimental.pallas import tpu as pltpu
from jax.sharding import PartitionSpec as P

ROPE_BASE = 10000.0
BLK = 128
TILE = 512
COLS = 256
F32 = jnp.float32
BF16 = jnp.bfloat16


def rope_tables(positions, head_dim):
    half_dim = head_dim // 2
    inv_freq = 1.0 / jnp.power(ROPE_BASE, jnp.arange(half_dim, dtype=F32) * (2.0 / head_dim))
    angles = positions.astype(F32)[:, None] * inv_freq[None, :]
    return jnp.cos(angles), jnp.sin(angles)


def rotate(rot_in, cos_tab, sin_tab):
    half_dim = rot_in.shape[-1] // 2
    low_half = rot_in[..., :half_dim]
    high_half = rot_in[..., half_dim:]
    return jnp.concatenate([low_half * cos_tab - high_half * sin_tab, high_half * cos_tab + low_half * sin_tab], axis=-1)


def unrotate(rot_in, cos_tab, sin_tab):
    return rotate(rot_in, cos_tab, -sin_tab)


def dot(a, b):
    return jnp.dot(a, b, preferred_element_type=F32)


def dot_ta(a, b):
    return lax.dot_general(a, b, (((0,), (0,)), ((), ())), preferred_element_type=F32)


def causal_mask(k_start, q_start, cols):
    k_pos = k_start + lax.broadcasted_iota(jnp.int32, (TILE, cols), 0)
    q_pos = q_start + lax.broadcasted_iota(jnp.int32, (TILE, cols), 1) % BLK
    return k_pos <= q_pos


RING = 4
AXIS_STRIDE = (RING * RING, RING, 1)
ORDERS = ((0, 1, 2), (1, 2, 0), (2, 0, 1))
MESH = pl.DeviceIdType.MESH


def ring_of(axis):
    cp, tp = lax.axis_index("cp"), lax.axis_index("tp")
    stride = AXIS_STRIDE[axis]
    pos = (cp // stride) % RING
    right = cp + ((pos + 1) % RING - pos) * stride
    left = cp + ((pos + RING - 1) % RING - pos) * stride
    across = cp + ((pos + 2) % RING - pos) * stride
    return pos, (tp, right), (tp, left), (tp, across)


def enter(rings, with_partner=False, with_mirror=False):
    barrier = pltpu.get_barrier_semaphore()
    peers = []
    for _, *others in rings:
        peers += others
    if with_partner:
        peers.append((1 - lax.axis_index("tp"), lax.axis_index("cp")))
    if with_mirror:
        mirror = RING ** 3 - 1 - lax.axis_index("cp")
        peers += [(0, mirror), (1, mirror)]
    for peer in peers:
        pl.semaphore_signal(barrier, inc=1, device_id=peer, device_id_type=MESH)
    pl.semaphore_wait(barrier, len(peers))


def remote(src, dst, sems, idx, device):
    return pltpu.make_async_remote_copy(src_ref=src, dst_ref=dst, send_sem=sems[0].at[idx], recv_sem=sems[1].at[idx], device_id=device, device_id_type=MESH)


def add_rows(dst, dst0, srcs, n_rows, lanes):
    strip = next(s for s in (64, 48, 40, 32, 24, 16, 8) if n_rows % s == 0)
    if lanes[1] > 256:
        strip = next(s for s in (16, 8) if n_rows % s == 0)

    def body(i, carry):
        off = pl.multiple_of(dst0 + i * strip, 8)
        total = dst[pl.ds(off, strip), pl.ds(*lanes)]
        for ref, start in srcs:
            total = total + ref[pl.ds(pl.multiple_of(start + i * strip, 8), strip), :]
        dst[pl.ds(off, strip), pl.ds(*lanes)] = total
        return carry

    lax.fori_loop(0, n_rows // strip, body, 0)


class Part:
    def __init__(self, rings, order, rb, sems, x=None, y=None, recv=None, row0=0, lanes=None, align=8, direct=2):
        self.direct = direct
        self.rb, self.sems, self.x, self.y, self.recv = rb, sems, x, y, recv
        self.row0, self.lanes, self.align = row0, lanes, align
        self.places = []
        base = row0
        for phase in range(3):
            slab = rb * RING ** (2 - phase)
            h0 = -(-slab // (2 * align)) * align
            pos, right, left, across = rings[order[phase]]
            starts = [base + ((pos + d) % RING) * slab for d in range(RING)]
            self.places.append((slab, h0, slab - h0, starts, right, left, across))
            base = starts[0]

    def view(self, ref, start, n_rows):
        return ref.at[pl.ds(pl.multiple_of(start, self.align), n_rows), pl.ds(*self.lanes)]

    def place(self, phase):
        return self.places[phase]

    def hop(self, phase, i):
        slab, h0, h1, (own, rgt, opp, lft), right, left, across = self.place(phase)
        if phase >= self.direct:
            start, n_rows, at, device = {
                0: (opp, slab, 0, across),
                2: (rgt, slab, slab, right),
                3: (lft, slab, 2 * slab, left),
                6: (own, slab, 0, right),
                7: (own, slab, 0, left),
                8: (own, slab, 0, across),
            }[i]
        else:
            start, n_rows, at, device = (
                (opp, h0, 0, right),
                (opp + h0, h1, h0, left),
                (rgt + h0, h1, slab + h0, right),
                (lft, h0, 2 * slab, left),
                (rgt, h0, slab, right),
                (lft + h0, h1, 2 * slab + h0, left),
                (own, slab, 0, right),
                (own, slab, 0, left),
                (lft, h0, 0, right),
                (rgt + h0, h1, 0, left),
            )[i]
        if i < 6:
            src, dst = self.view(self.x, start, n_rows), self.recv[phase].at[pl.ds(at, n_rows)]
        else:
            src = dst = self.view(self.y, start, n_rows)
        return remote(src, dst, self.sems, 10 * phase + i, device)

    def rs_start(self, phase):
        for i in (0, 2, 3) if phase >= self.direct else range(4):
            self.hop(phase, i).start()

    def rs_mid(self, phase):
        if phase >= self.direct:
            return
        slab, h0, h1, (own, rgt, opp, lft), *_ = self.place(phase)
        buf = self.recv[phase]
        self.hop(phase, 0).wait_recv()
        add_rows(self.x, rgt, [(buf, 0)], h0, self.lanes)
        self.hop(phase, 4).start()
        self.hop(phase, 1).wait_recv()
        add_rows(self.x, lft + h0, [(buf, h0)], h1, self.lanes)
        self.hop(phase, 5).start()

    def rs_end(self, phase):
        slab, _, _, (own, _, _, _), *_ = self.place(phase)
        buf = self.recv[phase]
        terms = [(buf, slab), (buf, 2 * slab)]
        if phase >= self.direct:
            terms.append((buf, 0))
        for i in (0, 2, 3) if phase >= self.direct else range(2, 6):
            self.hop(phase, i).wait_recv()
        add_rows(self.x, own, terms, slab, self.lanes)

    def ag_start(self, phase):
        for i in (6, 7, 8) if phase >= self.direct else (6, 7):
            self.hop(phase, i).start()

    def ag_mid(self, phase):
        if phase >= self.direct:
            return
        self.hop(phase, 6).wait_recv()
        self.hop(phase, 8).start()
        self.hop(phase, 7).wait_recv()
        self.hop(phase, 9).start()

    def ag_end(self, phase):
        for i in (6, 7, 8) if phase >= self.direct else (8, 9):
            self.hop(phase, i).wait_recv()

    def own_rows(self):
        return self.place(2)[3][0]

    def drain(self, rs=(), ag=()):
        for phase in rs:
            for i in (0, 2, 3) if phase >= self.direct else range(6):
                self.hop(phase, i).wait_send()
        for phase in ag:
            for i in (6, 7, 8) if phase >= self.direct else range(6, 10):
                self.hop(phase, i).wait_send()


def stage(parts, step):
    for part in parts:
        getattr(part, step[:-1])(int(step[-1]))


def slab_rows(rb):
    return [3 * rb * RING ** (2 - phase) for phase in range(3)]


def place_in_order(block, order):
    digit = [(block // s) % RING for s in AXIS_STRIDE]
    return (digit[order[0]] * RING + digit[order[1]]) * RING + digit[order[2]]


def by_rows(n_rows, align):
    unit = n_rows // align
    counts = [(unit + 2 - c) // 3 for c in range(3)]
    starts = [sum(counts[:c]) * align for c in range(3)]
    return [(starts[c], counts[c] * align) for c in range(3)]


def pair(n):
    return [pltpu.SemaphoreType.DMA((n,)), pltpu.SemaphoreType.DMA((n,))]


def grad_layout(d_model, n_local):
    n_blk = RING ** 3
    q_tiles = d_model * n_local // 8 // n_blk
    o_tiles = d_model // 128
    q_count = [q_tiles * 13 // 32, q_tiles * 11 // 32]
    q_count.append(q_tiles - sum(q_count))
    o_count = [o_tiles * 5 // 16, o_tiles * 6 // 16]
    o_count.append(o_tiles - sum(o_count))
    q_rows = [8 * n for n in q_count]
    q_first = [n_blk * sum(q_rows[:c]) for c in range(3)]
    o_lanes = [(128 * sum(o_count[:c]), 128 * o_count[c]) for c in range(3)]
    return q_rows, q_first, o_lanes


def place_heads(dst, src):
    n_batch, n_rows, head_dim = src.shape
    for b in range(n_batch):
        for h in range(n_rows // BLK):
            dst[pl.ds(b * BLK, BLK), pl.ds(h * head_dim, head_dim)] = src[b, h * BLK:(h + 1) * BLK, :]


D_TILE = 256


class Return:
    def __init__(self, src, dst, sems):
        self.src, self.dst, self.sems = src, dst, sems
        self.cp, self.tp = lax.axis_index("cp"), lax.axis_index("tp")
        self.mirror = RING ** 3 - 1 - self.cp
        self.group = self.cp // (RING ** 3 // 2)
        self.is_mine = self.tp == self.group

    def give(self, piece_idx):
        device = (self.group, self.mirror) if piece_idx else (1 - self.tp, self.cp)
        return pltpu.make_async_remote_copy(src_ref=self.src.at[piece_idx], dst_ref=self.dst.at[self.tp], send_sem=self.sems[0].at[piece_idx], recv_sem=self.sems[1].at[self.tp], device_id=device, device_id_type=MESH)

    def take(self, batch):
        return pltpu.make_async_remote_copy(src_ref=self.src.at[1], dst_ref=self.dst.at[batch], send_sem=self.sems[0].at[1], recv_sem=self.sems[1].at[batch], device_id=(self.group, self.mirror), device_id_type=MESH)

    def start(self):
        self.give(1).start()

        @pl.when(jnp.logical_not(self.is_mine))
        def _():
            self.give(0).start()

        @pl.when(self.is_mine)
        def _():
            self.dst[self.tp] = self.src[0]

    def wait(self):
        self.take(1 - self.tp).wait_recv()

        @pl.when(jnp.logical_not(self.is_mine))
        def _():
            self.take(self.tp).wait_recv()

    def drain(self):
        self.give(1).wait_send()

        @pl.when(jnp.logical_not(self.is_mine))
        def _():
            self.give(0).wait_send()


class Handout:
    def __init__(self, src, dst, sems):
        self.src, self.dst, self.sems = src, dst, sems
        self.cp, self.tp = lax.axis_index("cp"), lax.axis_index("tp")
        self.mirror = RING ** 3 - 1 - self.cp
        self.is_mine = self.tp == self.cp // (RING ** 3 // 2)

    def copy(self, kind, batch, slot, device, sem):
        return pltpu.make_async_remote_copy(src_ref=self.src.at[batch, kind], dst_ref=self.dst.at[slot, kind], send_sem=self.sems[0].at[2 * kind + sem], recv_sem=self.sems[1].at[2 * kind + slot], device_id=device, device_id_type=MESH)

    def near(self, kind):
        return self.copy(kind, 1 - self.tp, 0, (1 - self.tp, self.cp), 0)

    def far(self, kind, batch):
        return self.copy(kind, batch, 1, (batch, self.mirror), batch)

    def start(self, kind):
        @pl.when(self.is_mine)
        def _():
            self.near(kind).start()
            self.dst[0, kind] = self.src[self.tp, kind]

        @pl.when(jnp.logical_not(self.is_mine))
        def _():
            self.far(kind, 0).start()
            self.far(kind, 1).start()

    def wait(self, kind):
        self.far(kind, 0).wait_recv()

        @pl.when(jnp.logical_not(self.is_mine))
        def _():
            self.near(kind).wait_recv()

    def drain(self, kind):
        @pl.when(self.is_mine)
        def _():
            self.near(kind).wait_send()

        @pl.when(jnp.logical_not(self.is_mine))
        def _():
            self.far(kind, 0).wait_send()
            self.far(kind, 1).wait_send()


D_TILE = 256


def attn_kernel(own_ref, qd_ref, grad_ref, cos_ref, sin_ref, oh_ref, dqh_ref, dkv_ref, red0, red1, red2, y0, y1, y2, kv_scr, qd_scr, o_scr, qt_scr, dot_scr, dqt_scr, m_scr, l_scr, delta_scr, p_scr, ds_scr, xo, tok_scr, rot_scr, oh_scr, dqh_scr, *rest):
    recv, k_sems, o_sems = rest[:3], rest[3:9], rest[9:15]
    hand_sems, oh_sems, dqh_sems = rest[15:17], rest[17:19], rest[19:21]
    n_groups, _, n_cols, e_dim = qd_scr.shape
    rows = own_ref.shape[0]
    per_tile = TILE // BLK
    n_blk = RING ** 3
    d_model = grad_ref.shape[1]
    cp = lax.axis_index("cp")
    mirror = n_blk - 1 - cp
    rings = [ring_of(axis) for axis in range(3)]
    _, _, o_lanes = grad_layout(d_model, n_cols // rows)
    ys = (y0, y1, y2)
    split = by_rows(rows, 16)
    p_kv = [Part(rings, ORDERS[c], split[c][1], k_sems[2 * c:2 * c + 2], y=ys[c], lanes=(0, 2 * e_dim), align=16, direct=1) for c in range(3)]
    p_o = [Part(rings, ORDERS[c], n_cols // n_blk, o_sems[2 * c:2 * c + 2], x=xo, recv=[recv[c]], lanes=o_lanes[c]) for c in range(3)]
    hand = Handout(qd_ref, qd_scr, hand_sems)
    o_back = Return(o_scr, oh_scr, oh_sems)
    dq_back = Return(rot_scr, dqh_scr, dqh_sems)

    for c in range(3):
        ys[c][pl.ds(pl.multiple_of(p_kv[c].own_rows(), 16), split[c][1]), :] = own_ref[pl.ds(*split[c]), :]
    enter(rings, with_partner=True, with_mirror=True)
    stage(p_kv, "ag_start2")
    stage(p_kv, "ag_end2")
    stage(p_kv, "ag_start1")
    hand.start(0)
    stage(p_kv, "ag_end1")
    stage(p_kv, "ag_start0")
    dqt_scr[...] = jnp.zeros_like(dqt_scr)
    dkv_ref[...] = jnp.zeros_like(dkv_ref)
    m_scr[...] = jnp.full_like(m_scr, -jnp.inf)
    l_scr[...] = jnp.zeros_like(l_scr)
    hand.wait(0)
    for grp in range(n_groups):
        qt_scr[grp] = qd_scr[grp, 0].T
    stage(p_kv, "ag_mid0")
    hand.start(1)
    stage(p_kv, "ag_end0")

    def place_kv(blk, carry):
        for c in range(3):
            at, rb = split[c]
            src = pl.ds(pl.multiple_of(place_in_order(blk, ORDERS[c]) * rb, 16), rb)
            kv_scr[pl.ds(pl.multiple_of(blk * rows + at, 16), rb), :] = ys[c][src, :]
        return carry

    lax.fori_loop(0, n_blk, place_kv, 0)

    n_first = cp // per_tile + 1
    n_steps = n_blk // per_tile + 1

    def over_tiles(tile_step, extra):
        def body(t, carry):
            grp = (t - n_first + n_steps) // n_steps
            piece = cp + grp * (mirror - cp)
            tile_idx = t - grp * n_first
            last = tile_idx == piece // per_tile

            @pl.when(jnp.logical_not(last))
            def _():
                tile_step(grp, tile_idx, piece, False)

            @pl.when(last)
            def _():
                tile_step(grp, tile_idx, piece, True)

            for when, action in extra:
                pl.when(t == when)(action)
            return carry

        lax.fori_loop(0, n_steps, body, 0)

    def fwd_step(grp, tile_idx, piece, masked):
        row0 = pl.multiple_of(tile_idx * TILE, TILE)
        k_t = kv_scr[pl.ds(row0, TILE), :e_dim]
        v_t = kv_scr[pl.ds(row0, TILE), e_dim:]
        for c0 in range(0, n_cols, COLS):
            cs = slice(c0, c0 + COLS)
            s = dot(k_t, qt_scr[grp, :, cs])
            if masked:
                s = jnp.where(causal_mask(row0, piece * BLK, COLS), s, -jnp.inf)
            m_old = m_scr[grp, :, cs]
            m_new = jnp.maximum(m_old, jnp.max(s, axis=0, keepdims=True))
            p = jnp.exp(s - m_new)
            alpha = jnp.exp(m_old - m_new)
            m_scr[grp, :, cs] = m_new
            l_scr[grp, :, cs] = l_scr[grp, :, cs] * alpha + jnp.sum(p, axis=0, keepdims=True)
            dqt_scr[grp, :, cs] = dqt_scr[grp, :, cs] * alpha + dot_ta(v_t, p.astype(BF16))

    over_tiles(fwd_step, ())
    hand.wait(1)
    for grp in range(n_groups):
        o_t = (dqt_scr[grp] / l_scr[grp]).astype(BF16)
        o_scr[grp] = o_t.T
        dot_scr[grp] = qd_scr[grp, 1].T
        delta_scr[grp] = jnp.sum(dot_scr[grp].astype(F32) * o_t.astype(F32), axis=0, keepdims=True)
    o_back.start()
    m_scr[...] = m_scr[...] + jnp.log(l_scr[...])
    dqt_scr[...] = jnp.zeros_like(dqt_scr)

    def bwd_step(grp, tile_idx, piece, masked):
        row0 = pl.multiple_of(tile_idx * TILE, TILE)
        k_t = kv_scr[pl.ds(row0, TILE), :e_dim]
        v_t = kv_scr[pl.ds(row0, TILE), e_dim:]
        for c0 in range(0, n_cols, COLS):
            cs = slice(c0, c0 + COLS)
            s = dot(k_t, qt_scr[grp, :, cs])
            p = jnp.exp(s - m_scr[grp, :, cs])
            if masked:
                p = jnp.where(causal_mask(row0, piece * BLK, COLS), p, 0.0)
            d_p = dot(v_t, dot_scr[grp, :, cs])
            p_scr[:, cs] = p.astype(BF16)
            ds_scr[:, cs] = (p * (d_p - delta_scr[grp, :, cs])).astype(BF16)
        at = pl.ds(row0, TILE)
        dkv_ref[at, :e_dim] += dot(ds_scr[...], qd_scr[grp, 0])
        dkv_ref[at, e_dim:] += dot(p_scr[...], qd_scr[grp, 1])
        dqt_scr[grp] += dot_ta(k_t, ds_scr[...])

    def sum_wo_start():
        o_back.wait()
        place_heads(tok_scr, oh_scr)

        def o_body(i, carry):
            cols = pl.ds(pl.multiple_of(i * D_TILE, D_TILE), D_TILE)
            xo[:, cols] = dot_ta(tok_scr[...], grad_ref[:, cols])
            return carry

        lax.fori_loop(0, d_model // D_TILE, o_body, 0)
        stage(p_o, "rs_start0")

    over_tiles(bwd_step, ((3, sum_wo_start), (9, lambda: stage(p_o, "rs_mid0"))))

    scale = e_dim ** -0.5
    half_dim = e_dim // 2
    for grp in range(n_groups):
        cos_t, sin_t = cos_ref[grp], sin_ref[grp]
        for h in range(n_cols // rows):
            cols = slice(h * rows, (h + 1) * rows)
            low, high = dqt_scr[grp, :half_dim, cols], dqt_scr[grp, half_dim:, cols]
            turned = jnp.concatenate([low * cos_t + high * sin_t, high * cos_t - low * sin_t], axis=0) * scale
            rot_scr[grp, cols, :] = turned.T.astype(BF16)
    dq_back.start()
    oh_ref[...] = oh_scr[...]
    stage(p_o, "rs_end0")
    for part, out, lanes in zip(p_o, (red0, red1, red2), o_lanes):
        slab, _, _, starts, *_ = part.place(0)
        out[...] = xo[pl.ds(pl.multiple_of(starts[0], 8), slab), pl.ds(*lanes)]
    dq_back.wait()
    dqh_ref[...] = dqh_scr[...]
    for part in p_kv:
        part.drain(ag=range(3))
    for part in p_o:
        part.drain(rs=(0,))
    for kind in range(2):
        hand.drain(kind)
    o_back.drain()
    dq_back.drain()


def attention(own_kv, qd_home, grad, cos_t, sin_t):
    n_batch, _, n_cols, e_dim = qd_home.shape
    rows = own_kv.shape[0]
    n_tok, d_model = grad.shape
    n_blk = RING ** 3
    seq = n_blk * rows
    _, _, o_lanes = grad_layout(d_model, n_cols // rows)
    slab = n_cols // RING
    vmem = pl.BlockSpec(memory_space=pltpu.VMEM)
    heads = (2, n_cols, e_dim)
    work = 2 * n_cols * seq // 2
    return pl.pallas_call(
        attn_kernel,
        out_shape=(jax.ShapeDtypeStruct(heads, BF16), jax.ShapeDtypeStruct(heads, BF16), jax.ShapeDtypeStruct((seq, 2 * e_dim), F32)) + tuple(jax.ShapeDtypeStruct((slab, n), F32) for _, n in o_lanes),
        in_specs=[vmem] * 5,
        out_specs=(vmem,) * 6,
        scratch_shapes=[pltpu.VMEM((n_blk * rb, 2 * e_dim), BF16) for _, rb in by_rows(rows, 16)]
        + [
            pltpu.VMEM((seq, 2 * e_dim), BF16),
            pltpu.VMEM((2, 2, n_cols, e_dim), BF16),
            pltpu.VMEM(heads, BF16),
            pltpu.VMEM((2, e_dim, n_cols), BF16),
            pltpu.VMEM((2, e_dim, n_cols), BF16),
            pltpu.VMEM((2, e_dim, n_cols), F32),
            pltpu.VMEM((2, 1, n_cols), F32),
            pltpu.VMEM((2, 1, n_cols), F32),
            pltpu.VMEM((2, 1, n_cols), F32),
            pltpu.VMEM((TILE, n_cols), BF16),
            pltpu.VMEM((TILE, n_cols), BF16),
            pltpu.VMEM((n_cols, d_model), F32),
            pltpu.VMEM((n_tok, n_cols), BF16),
            pltpu.VMEM(heads, BF16),
            pltpu.VMEM(heads, BF16),
            pltpu.VMEM(heads, BF16),
        ]
        + [pltpu.VMEM((3 * slab, lanes), F32) for _, lanes in o_lanes]
        + pair(30) * 6
        + pair(4)
        + pair(2) * 2,
        compiler_params=pltpu.CompilerParams(collective_id=2, has_side_effects=True, vmem_limit_bytes=64000000),
        cost_estimate=pl.CostEstimate(flops=14 * work * e_dim, bytes_accessed=seq * e_dim * 12, transcendentals=2 * work),
        name="attention",
    )(own_kv, qd_home, grad, cos_t, sin_t)


GRAD_PLAN = (
    "d.rs_start0", "d.rs_mid0", "weights.q", "r.rs_start1", "d.rs_end0", "d.rs_start1", "d.rs_mid1", "r.rs_mid1",
    "d.rs_end1", "d.rs_start2", "r.rs_end1", "q.rs_start0", "d.rs_end2", "weights.prep", "q.rs_mid0", "weights.kv",
    "k.rs_start0", "k.rs_mid0", "r.rs_start2", "q.rs_end0", "k.rs_end0", "k.rs_start1", "q.rs_start1", "k.rs_mid1",
    "q.rs_mid1", "r.rs_end2", "o.ag_start2", "q.rs_end1", "q.rs_start2", "k.rs_end1", "o.ag_end2", "k.rs_start2",
    "o.ag_start1", "q.rs_end2", "k.rs_end2", "q.ag_start2", "k.ag_start2", "o.ag_mid1", "q.ag_end2", "k.ag_end2",
    "k.ag_start1", "q.ag_start1", "k.ag_mid1", "q.ag_mid1", "o.ag_end1", "k.ag_end1", "k.ag_start0", "o.ag_start0",
    "k.ag_mid0", "q.ag_end1", "q.ag_start0", "o.ag_mid0", "q.ag_mid0", "o.ag_end0", "k.ag_end0", "q.ag_end0",
)


def grad_kernel(dkv_ref, hid_ref, dqh_ref, red0, red1, red2, cos_ref, sin_ref, gq_ref, go_ref, gk_ref, gv_ref, dkd_ref, x0, x1, x2, xq, xk, yq, yo, yk, yp, xo0, xo1, xo2, tok_scr, mine_scr, give_scr, got_scr, *rest):
    n_parts = 10
    recv, sems, in_sem, out_sem, swap_s, swap_r = rest[:27], rest[27:27 + 2 * n_parts], rest[-4], rest[-3], rest[-2], rest[-1]
    n_blk = RING ** 3
    n_tok, d_model = hid_ref.shape
    n_batch, _, head_dim = dqh_ref.shape
    rows, lanes = n_tok // n_batch, 2 * head_dim
    n_local = dqh_ref.shape[1] // rows
    n_cols = n_local * head_dim
    q_rows, q_first, o_lanes = grad_layout(d_model, n_local)
    split = by_rows(rows, 8)
    tp, cp = lax.axis_index("tp"), lax.axis_index("cp")
    partner = (1 - tp, cp)
    xs = (x0, x1, x2)
    rings = [ring_of(axis) for axis in range(3)]

    def sem(i):
        return sems[2 * i:2 * i + 2]

    p_d = [Part(rings, ORDERS[c], split[c][1], sem(c), x=xs[c], recv=recv[3 * c:3 * c + 3], lanes=(0, lanes)) for c in range(3)]
    p_q = [Part(rings, ORDERS[c], q_rows[c], sem(3 + c), x=xq, y=yq, recv=recv[9 + 3 * c:12 + 3 * c], row0=q_first[c], lanes=(0, 128)) for c in range(3)]
    p_o = [Part(rings, ORDERS[c], n_cols // n_blk, sem(6 + c), y=yo, lanes=o_lanes[c]) for c in range(3)]
    xos = (xo0, xo1, xo2)
    o_slab = n_cols // RING
    p_r = [Part(rings, ORDERS[c], n_cols // n_blk, sem(6 + c), x=xos[c], recv=[None] + list(recv[21 + 2 * c:23 + 2 * c]), row0=0 - rings[ORDERS[c][0]][0] * o_slab, lanes=(0, o_lanes[c][1])) for c in range(3)]
    p_k = Part(rings, ORDERS[2], d_model // n_blk, sem(9), x=xk, y=yk, recv=recv[18:21], lanes=(0, 128))
    p_qo = p_q + p_o

    def load(blk, carry):
        for c in range(3):
            at, rb = split[c]
            dst = xs[c].at[pl.ds(pl.multiple_of(place_in_order(blk, ORDERS[c]) * rb, 8), rb)]
            pltpu.make_async_copy(dkv_ref.at[pl.ds(pl.multiple_of(blk * rows + at, 8), rb)], dst, in_sem.at[c]).start()
        return carry

    lax.fori_loop(0, n_blk, load, 0)
    for c, red in enumerate((red0, red1, red2)):
        pltpu.make_async_copy(red, xos[c], in_sem.at[3 + c]).start()
    enter(rings, with_partner=True)
    for c, red in enumerate((red0, red1, red2)):
        pltpu.make_async_copy(red, xos[c], in_sem.at[3 + c]).wait()
    for c in range(3):
        pltpu.make_async_copy(dkv_ref.at[pl.ds(0, n_blk * split[c][1])], xs[c], in_sem.at[c]).wait()
    half_dim = head_dim // 2
    first = tp == 0
    swap_small = pltpu.make_async_remote_copy(src_ref=give_scr, dst_ref=got_scr, send_sem=swap_s.at[0], recv_sem=swap_r.at[0], device_id=partner, device_id_type=MESH)
    swap = pltpu.make_async_remote_copy(src_ref=yk, dst_ref=yp, send_sem=swap_s.at[1], recv_sem=swap_r.at[1], device_id=partner, device_id_type=MESH)

    def put(parts, which):
        for part in parts:
            out = gq_ref if part.y is yq else go_ref
            slab, _, _, starts, *_ = part.place(0)
            for i in which:
                src, dst = part.view(part.y, starts[i], slab), part.view(out, starts[i], slab)
                pltpu.make_async_copy(src, dst, out_sem.at[p_qo.index(part)]).start()

    def own_block(parts, sums):
        for part, total in zip(parts, sums):
            at, lanes_y, lanes_x = part.own_rows(), pl.ds(*part.lanes), pl.ds(*total.lanes)
            part.y[pl.ds(pl.multiple_of(at, 8), part.rb), lanes_y] = total.x[pl.ds(pl.multiple_of(total.own_rows(), 8), part.rb), lanes_x]

    def weights_q():
        place_heads(tok_scr, dqh_ref)

        def q_body(i, carry):
            cols = pl.ds(pl.multiple_of(i * D_TILE, D_TILE), D_TILE)
            res = dot_ta(hid_ref[:, cols], tok_scr[...])
            for h in range(n_local):
                xq[pl.ds(i * D_TILE * n_local + h, D_TILE, stride=n_local), :] = res[:, h * head_dim:(h + 1) * head_dim]
            return carry

        lax.fori_loop(0, d_model // D_TILE, q_body, 0)

    def new_dkv():
        dkd_ref[...] = mine_scr[...].astype(BF16)
        return dkd_ref[:, :head_dim], dkd_ref[:, head_dim:]

    def weights_prep():
        for c in range(3):
            at, rb = split[c]
            own = xs[c][pl.ds(pl.multiple_of(p_d[c].own_rows(), 8), rb), :]
            cos_tab, sin_tab = cos_ref[pl.ds(at, rb), :], sin_ref[pl.ds(at, rb), :]
            low, high = own[:, :half_dim], own[:, half_dim:head_dim]
            mine_scr[pl.ds(at, rb), :head_dim] = jnp.concatenate([low * cos_tab + high * sin_tab, high * cos_tab - low * sin_tab], axis=1)
            mine_scr[pl.ds(at, rb), head_dim:] = own[:, head_dim:]
        dk_new, dv_new = new_dkv()
        give_scr[...] = jnp.where(first, dv_new, dk_new)
        swap_small.start()

    def weights_kv():
        swap_small.wait()
        got = got_scr[...]
        keep = jnp.where(first, dkd_ref[:, :head_dim], dkd_ref[:, head_dim:])
        kv_tok = jnp.concatenate([jnp.where(first, keep, got), jnp.where(first, got, keep)], axis=0)
        for i in range(d_model // D_TILE):
            xk[pl.ds(i * D_TILE, D_TILE), :] = dot_ta(hid_ref[:, i * D_TILE:(i + 1) * D_TILE], kv_tok)

    groups = {"d": p_d, "q": p_q, "r": p_r, "o": p_o, "k": [p_k]}
    after = {
        "weights.q": weights_q,
        "weights.prep": weights_prep,
        "weights.kv": weights_kv,
        "r.rs_end2": lambda: own_block(p_o, p_r),
        "q.rs_end2": lambda: own_block(p_q, p_q),
        "k.rs_end2": lambda: own_block([p_k], [p_k]),
        "o.ag_mid0": lambda: put(p_o, (0, 1, 3)),
        "o.ag_end0": lambda: put(p_o, (2,)),
        "q.ag_start0": lambda: put(p_q, (0,)),
        "q.ag_mid0": lambda: put(p_q, (1, 3)),
        "q.ag_end0": lambda: put(p_q, (2,)),
        "k.ag_end0": swap.start,
    }
    for step in GRAD_PLAN:
        who, what = step.split(".")
        if who in groups:
            stage(groups[who], what)
        if step in after:
            after[step]()
    swap.wait()

    def put_kv(k_src, v_src):
        outs = [pltpu.make_async_copy(k_src, gk_ref, out_sem.at[6]), pltpu.make_async_copy(v_src, gv_ref, out_sem.at[7])]
        for copy in outs:
            copy.start()
        for copy in outs:
            copy.wait()

    @pl.when(first)
    def _():
        put_kv(yk, yp)

    @pl.when(jnp.logical_not(first))
    def _():
        put_kv(yp, yk)

    for i, part in enumerate(p_qo):
        out = gq_ref if part.y is yq else go_ref
        span = n_blk * part.rb
        pltpu.make_async_copy(part.view(part.y, part.row0, span), part.view(out, part.row0, span), out_sem.at[i]).wait()
    for part in p_d:
        part.drain(rs=range(3))
    for part in p_q + [p_k]:
        part.drain(rs=range(3), ag=range(3))
    for part, red in zip(p_o, p_r):
        red.drain(rs=(1, 2))
        part.drain(ag=range(3))


def grad_sums(dkv, hid, dq_home, reds, cos_tab, sin_tab):
    n_tok, d_model = hid.shape
    n_batch, _, head_dim = dq_home.shape
    block_len = n_tok // n_batch
    n_local = dq_home.shape[1] // block_len
    n_cols = n_local * head_dim
    n_blk = RING ** 3
    lanes = 2 * head_dim
    q_rows, _, o_lanes = grad_layout(d_model, n_local)
    split = by_rows(block_len, 8)
    recv = [pltpu.VMEM((n, lanes), F32) for _, rb in split for n in slab_rows(rb)]
    recv += [pltpu.VMEM((n, 128), F32) for rb in q_rows for n in slab_rows(rb)]
    recv += [pltpu.VMEM((n, 128), F32) for n in slab_rows(d_model // n_blk)]
    recv += [pltpu.VMEM((n, w), F32) for _, w in o_lanes for n in slab_rows(n_cols // n_blk)[1:]]
    vmem, anyspace = pl.BlockSpec(memory_space=pltpu.VMEM), pl.BlockSpec(memory_space=pl.ANY)
    xq, xo, xk = (pltpu.VMEM(s, F32) for s in ((d_model * n_local, 128), (n_cols, d_model), (d_model, 128)))
    small = pltpu.VMEM((block_len, head_dim), BF16)
    return pl.pallas_call(
        grad_kernel,
        out_shape=(
            jax.ShapeDtypeStruct((d_model * n_local, 128), F32),
            jax.ShapeDtypeStruct((n_cols, d_model), F32),
            jax.ShapeDtypeStruct((d_model, 128), F32),
            jax.ShapeDtypeStruct((d_model, 128), F32),
            jax.ShapeDtypeStruct((block_len, lanes), BF16),
        ),
        in_specs=[anyspace] + [vmem] * 2 + [anyspace] * 3 + [vmem] * 2,
        out_specs=(anyspace,) * 4 + (vmem,),
        scratch_shapes=[pltpu.VMEM((n_blk * rb, lanes), F32) for _, rb in split]
        + [xq, xk, xq, xo, xk, xk]
        + [pltpu.VMEM((n_cols // RING, w), F32) for _, w in o_lanes]
        + [pltpu.VMEM((n_tok, n_cols), BF16), pltpu.VMEM((block_len, lanes), F32), small, small]
        + recv
        + pair(30) * 10
        + [pltpu.SemaphoreType.DMA((6,)), pltpu.SemaphoreType.DMA((8,))]
        + pair(2),
        compiler_params=pltpu.CompilerParams(collective_id=3, has_side_effects=True, vmem_limit_bytes=67000000),
        cost_estimate=pl.CostEstimate(flops=2 * n_tok * d_model * n_cols * 80, bytes_accessed=40 << 20, transcendentals=0),
        name="grad_sums",
    )(dkv, hid, dq_home, *reds, cos_tab, sin_tab)


def solution(mesh):
    cp_size = mesh.shape["cp"]
    partner = [(0, 1), (1, 0)]

    def local_program(hidden, grad_out, w_query, w_key, w_value, w_out):
        block_len = hidden.shape[1]
        n_local = w_query.shape[1]
        head_dim = w_key.shape[1]
        q_scale = head_dim ** -0.5
        cp_idx = lax.axis_index("cp")
        tp_idx = lax.axis_index("tp")
        mirror_idx = cp_size - 1 - cp_idx
        cos_tab, sin_tab = rope_tables(cp_idx * block_len + jnp.arange(block_len), head_dim)
        cos_mir, sin_mir = rope_tables(mirror_idx * block_len + jnp.arange(block_len), head_dim)

        def pick(pair, idx):
            return lax.dynamic_index_in_dim(pair, idx, 0, keepdims=False)

        def sum_over_tp(part, extra=None):
            total = pick(part, tp_idx) + lax.ppermute(pick(part, 1 - tp_idx), "tp", partner)
            if extra is not None:
                total = total + extra
            mine = total.astype(BF16)
            other = lax.ppermute(mine, "tp", partner)
            first = tp_idx == 0
            return jnp.stack([jnp.where(first, mine, other), jnp.where(first, other, mine)])

        hid_b = pick(hidden, tp_idx)
        key_loc = rotate(dot(hid_b, w_key), cos_tab, sin_tab).astype(BF16)
        val_loc = dot(hid_b, w_value).astype(BF16)
        own_kv = jnp.concatenate([key_loc, val_loc], axis=1)

        q_pre = jnp.einsum("bsd,dhe->bhse", hidden, w_query, preferred_element_type=F32)
        queries = (rotate(q_pre, cos_tab, sin_tab) * q_scale).astype(BF16)
        d_out = jnp.einsum("bsd,hed->bhse", grad_out, w_out, preferred_element_type=F32).astype(BF16)
        qd_home = jnp.stack([queries, d_out], axis=1).reshape(2, 2, n_local * block_len, head_dim)
        tabs_t = [jnp.stack(pair_t) for pair_t in ((cos_tab.T, cos_mir.T), (sin_tab.T, sin_mir.T))]
        o_home, dq_home, dkv, *reds = attention(own_kv, qd_home, grad_out.reshape(-1, grad_out.shape[-1]), *tabs_t)
        attn_heads = o_home.reshape(2, n_local, block_len, head_dim)
        dq_pre = dq_home.reshape(2, n_local, block_len, head_dim)
        attn_out = sum_over_tp(jnp.einsum("cirf,ife->cre", attn_heads, w_out, preferred_element_type=F32))
        grad_q, grad_o, d_w_key, d_w_value, dkv_new = grad_sums(dkv, hidden.reshape(-1, hidden.shape[-1]), dq_home, reds, cos_tab, sin_tab)
        d_w_query = grad_q.reshape(w_query.shape)
        d_w_out = grad_o.reshape(w_out.shape)
        dk_pre, dv_pre = dkv_new[:, :head_dim], dkv_new[:, head_dim:]
        dh_kv = dot(dk_pre, w_key.T) + dot(dv_pre, w_value.T)
        d_hidden = sum_over_tp(jnp.einsum("cirf,eif->cre", dq_pre, w_query, preferred_element_type=F32), dh_kv)
        return attn_out, d_hidden, d_w_query, d_w_key, d_w_value, d_w_out

    row_spec = P(None, "cp", None)
    return jax.shard_map(local_program, mesh=mesh, in_specs=(row_spec, row_spec, P(None, "tp", None), P(), P(), P("tp", None, None)), out_specs=(row_spec, row_spec, P(None, "tp", None), P(), P(), P("tp", None, None)), check_vma=False)
```

time: 2040 us -> 340 us (0.17)
  waiting for transfers between devices: 1770 us -> 0.74 us
  Pallas kernels: 0 us -> 291 us
  local copies, waits for them, and re-layouts: 185 us -> 17.3 us
    ppermute x190 -> x4, waiting for transfers between devices: 1410 us -> 0.74 us  [the longest x2 0.73 us: sum_over_tp(): other = lax.ppermute(mine, 'tp', partner)]
    psum x2 -> x0, waiting for transfers between devices: 354 us -> none  [the longest x1 210 us: local_program(): lax.psum(jnp.einsum('cre,cirf->eif', hidden, dq_pre, preferred_element_ty...]
    pallas_call x0 -> x2, Pallas kernels: none -> 291 us  [the longest x1 161 us: grad_sums(): pl.pallas_call(grad_kernel, out_shape=(jax.ShapeDtypeStruct((d_model * n_...]
    another operation x129 -> x0, local copies, waits for them, and re-layouts: 98.8 us -> none
    while x66 -> x0, local copies, waits for them, and re-layouts: 61.2 us -> none
  transfers between devices with their start and end apart: 192 -> 4, of which waited for: 192 -> 2; matrix products, arithmetic and copies ran while one was open for 4% -> 3% of each run, Pallas kernels for 0% -> 47%
where the time goes in v3:
time: 340 us
  Pallas kernels  291 us (86%)
  matrix products  20.2 us (6%)
  local copies, waits for them, and re-layouts  17.3 us (5%)
  other arithmetic  7.17 us (2%)
    pallas_call x1, Pallas kernels, grad_sums(): pl.pallas_call(grad_kernel, out_shape=(jax.ShapeDtypeStruct((d_model * n_...  161 us
    pallas_call x1, Pallas kernels, attention(): pl.pallas_call(attn_kernel, out_shape=(jax.ShapeDtypeStruct(heads, BF16),...  130 us
    unnamed x28, local copies, waits for them, and re-layouts  14.3 us
  transfers between devices with their start and end apart: 4, of which 2 were waited for; matrix products, arithmetic and copies ran while one was open for 3% of the time, Pallas kernels for 47%

profile of v3, /device:TPU:1, one launch (start us, length us, event | category | flops | bytes accessed | tf_op | source)
XLA Modules:
  0.0 340.1 jit_solution(7964178643814018248)
XLA Ops:
  0.7 1.5 fusion.31
  2.2 0.3 multiply_cosine_fusion
  2.5 0.0 copy-start.8
  2.5 0.0 copy-start.9
  2.5 0.1 copy.27
  2.6 0.1 copy.28
  2.7 3.9 %fusion.15 = f32[2,8,128,128]{2,3,0,1:T(8,128)S(1)} fusion(bf16[2048,8,128,1]{2,1,0,3:T(8,128)(2,1)} %bitcast.86, bf16[2,128,2048]{2,1,0:T(8,128)(2,1)} %param.6), kind=kOutput, calls=%fused_computation.12 | convolution fusion | flops 1073741824 | bytes 6291456 | tf_op jit(solution)/shard_map/bsd,dhe->bhse/dot_general | solution.py:780
  6.5 0.0 copy-done.8
  6.5 0.0 copy-done.9
  6.5 0.1 multiply_subtract_fusion
  6.7 0.3 copy.29
  7.0 0.3 copy.30
  7.4 0.0 copy-start.3
  7.4 0.0 copy-start.6
  7.4 3.9 %fusion.21 = bf16[2,8,128,128]{3,2,0,1:T(8,128)(2,1)S(1)} fusion(bf16[8,128,2048]{2,1,0:T(8,128)(2,1)} %param.11, bf16[2,128,2048]{2,1,0:T(8,128)(2,1)} %param.7), kind=kOutput, calls=%fused_computation.14 | convolution fusion | flops 1074003968 | bytes 5767168 | tf_op jit(solution)/shard_map/bsd,hed->bhse/dot_general | solution.py:782
  11.3 0.0 copy-done.3
  11.3 0.0 copy-done.6
  11.4 0.3 convolution_convert_fusion
  11.7 0.3 multiply_sine_fusion.2
  12.0 0.3 fusion.24
  12.3 1.1 pad_maximum_fusion.qd_ref
  13.4 0.7 pad_maximum_fusion.3.own_ref
  14.1 0.7 pad_maximum_fusion.4
  14.8 129.5 %attention.1 = (bf16[2,1024,128]{2,1,0:T(8,128)(2,1)}, bf16[2,1024,128]{2,1,0:T(8,128)(2,1)}, f32[8192,256]{1,0:T(8,128)}, f32[256,640]{1,0:T(8,128)}, f32[256,768]{1,0:T(8,128)}, /*index=5*/f32[256,640]{1,0:T(8,128)}) custom-call(bf16[128,256]{1,0:T(8,128)(2,1)} %pad_maximum_fusion.3.own_ref, bf16[2,2,1024,128]{3,2,1,0:T(8,128)(2,1)} %pad_maximum_fusion.qd_ref, ...), custom_call_target="tpu_custom_call" | custom-call | flops 15032385536 | bytes 12582912 | tf_op jit(solution)/shard_map/attention/pallas_call | solution.py:513
  144.3 0.0 copy-start.7
  144.3 3.7 %fusion.12 = f32[2,128,2048]{2,1,0:T(8,128)S(1)} fusion(bf16[2,8,128,128]{3,2,1,0:T(8,128)(2,1)} %bitcast.88, bf16[2048,8,128]{2,1,0:T(8,128)(2,1)} %param.8), kind=kOutput, calls=%fused_computation.10 | convolution fusion | flops 1073741824 | bytes 6815744 | tf_op jit(solution)/shard_map/cirf,eif->cre/dot_general | solution.py:794
  148.0 0.0 copy-start.2
  148.1 1.1 dynamic-slice_bitcast_fusion
  149.2 0.6 collective-permute-start.2
  149.8 0.0 copy-done.7
  149.8 3.4 %fusion.9 = f32[2,128,2048]{2,1,0:T(8,128)S(1)} fusion(bf16[2,8,128,128]{3,2,1,0:T(8,128)(2,1)S(1)} %bitcast.85, bf16[8,128,2048]{2,1,0:T(8,128)(2,1)} %param.11), kind=kOutput, calls=%fused_computation.9 | convolution fusion | flops 1073741824 | bytes 6815744 | tf_op jit(solution)/shard_map/cirf,ife->cre/dot_general | solution.py:788
  153.2 0.0 copy-done.2
  153.2 0.0 copy-start
  153.2 1.3 copy-done
  154.5 1.0 dynamic-slice_bitcast_fusion.1
  155.6 0.0 collective-permute-start
  155.6 161.1 %grad_sums.1 = (f32[16384,128]{1,0:T(8,128)}, f32[1024,2048]{1,0:T(8,128)}, f32[2048,128]{1,0:T(8,128)}, f32[2048,128]{1,0:T(8,128)}, bf16[128,256]{1,0:T(8,128)(2,1)}) custom-call(f32[8192,256]{1,0:T(8,128)} %get-tuple-element.19.dkv_ref, bf16[256,2048]{1,0:T(8,128)(2,1)} %bitcast.84, bf16[2,1024,128]{2,1,0:T(8,128)(2,1)} %get-tuple-element.18.dqh_ref, ...), custom_call_target="tpu_custom_call" | custom-call | flops 85899345920 | bytes 41943040 | tf_op jit(solution)/shard_map/grad_sums/pallas_call | solution.py:723
  316.7 0.0 copy-start.1
  316.7 1.5 fusion.38
  318.2 0.0 collective-permute-done.2
  318.2 2.1 fusion.26
  320.3 2.4 collective-permute-start.3
  322.7 0.0 collective-permute-done
  322.7 0.0 copy-done.1
  322.7 1.3 fusion.27
  324.0 0.1 collective-permute-start.1
  324.1 0.1 collective-permute-done.3
  324.2 0.1 select_bitcast_fusion.1
  324.3 1.1 pad_maximum_fusion.2
  325.4 0.7 collective-permute-done.1
  326.0 0.1 select_bitcast_fusion.3
  326.1 0.0 slice-start
  326.1 1.1 pad_maximum_fusion.1
  327.2 0.0 copy-start.5
  327.2 0.0 copy-start.4
  327.2 0.0 slice-start.1
  327.2 7.6 %copy.55 = f32[2048,8,128]{2,1,0:T(8,128)} copy(f32[2048,8,128]{2,1,0:T(8,128)} %bitcast.80) | data formatting | bytes 16777216
  334.7 0.0 copy-done.5
  334.7 1.0 copy.56
  335.7 0.0 copy-done.4
  335.7 1.0 copy.57
  336.7 0.0 slice-done
  336.7 0.0 slice-done.1
  336.7 3.4 copy.58
  (5 shorter events, 0.1 us)
Async XLA Ops:
  2.5 4.0 %copy-start.8 = (f32[128,64]{1,0:T(8,128)}, f32[128,64]{1,0:T(8,128)S(1)}, u32[]{:S(2)}) copy-start(f32[128,64]{1,0:T(8,128)S(1)} %get-tuple-element.40.cos_ref) | copy-start | bytes 98308
  2.5 4.0 %copy-start.9 = (f32[128,64]{1,0:T(8,128)}, f32[128,64]{1,0:T(8,128)S(1)}, u32[]{:S(2)}) copy-start(f32[128,64]{1,0:T(8,128)S(1)} %get-tuple-element.41.sin_ref) | copy-start | bytes 98308
  7.4 4.0 %copy-start.3 = (bf16[2048,128]{1,0:T(8,128)(2,1)S(1)}, bf16[2048,128]{1,0:T(8,128)(2,1)}, u32[]{:S(2)}) copy-start(bf16[2048,128]{1,0:T(8,128)(2,1)} %param.10) | copy-start | bytes 1572868
  7.4 4.0 %copy-start.6 = (bf16[2,128,2048]{2,1,0:T(8,128)(2,1)S(1)}, bf16[2,128,2048]{2,1,0:T(8,128)(2,1)}, u32[]{:S(2)}) copy-start(bf16[2,128,2048]{2,1,0:T(8,128)(2,1)} %param.6) | copy-start | bytes 3145732
  144.3 5.4 %copy-start.7 = (bf16[2,1024,128]{2,1,0:T(8,128)(2,1)S(1)}, bf16[2,1024,128]{2,1,0:T(8,128)(2,1)}, u32[]{:S(2)}) copy-start(bf16[2,1024,128]{2,1,0:T(8,128)(2,1)} %get-tuple-element.17) | copy-start | bytes 1572868
  148.0 5.2 %copy-start.2 = (f32[2,128,2048]{2,1,0:T(8,128)}, f32[2,128,2048]{2,1,0:T(8,128)S(1)}, u32[]{:S(2)}) copy-start(f32[2,128,2048]{2,1,0:T(8,128)S(1)} %fusion.12) | copy-start | bytes 6291460
  149.2 169.0 %collective-permute-start.2 = (f32[128,2048]{1,0:T(8,128)}, f32[128,2048]{1,0:T(8,128)}, u32[]{:S(2)}, u32[]{:S(2)}) collective-permute-start(f32[128,2048]{1,0:T(8,128)} %dynamic-slice_bitcast_fusion), channel_id=1, source_target_pairs={{0,64},{64,0},{1,65},{65,1},{2,66},{66,2},{3,67},{67,3},{4,68},{68... | collective-permute-start | bytes 3145736 | tf_op jit(solution)/shard_map/ppermute | solution.py:767
  153.2 1.3 copy-start
  155.6 167.1 %collective-permute-start = (f32[128,2048]{1,0:T(8,128)}, f32[128,2048]{1,0:T(8,128)}, u32[]{:S(2)}, u32[]{:S(2)}) collective-permute-start(f32[128,2048]{1,0:T(8,128)} %dynamic-slice_bitcast_fusion.1), channel_id=1, source_target_pairs={{0,64},{64,0},{1,65},{65,1},{2,66},{66,2},{3,67},{67,3},{4,68},{68... | collective-permute-start | bytes 3145736 | tf_op jit(solution)/shard_map/ppermute | solution.py:767
  316.7 6.0 %copy-start.1 = (f32[2,128,2048]{2,1,0:T(8,128)S(1)}, f32[2,128,2048]{2,1,0:T(8,128)}, u32[]{:S(2)}) copy-start(f32[2,128,2048]{2,1,0:T(8,128)} %copy-done) | copy-start | bytes 6291460
  320.3 4.0 %collective-permute-start.3 = (bf16[128,2048]{1,0:T(8,128)(2,1)S(1)}, bf16[128,2048]{1,0:T(8,128)(2,1)S(1)}, u32[]{:S(2)}, u32[]{:S(2)}) collective-permute-start(bf16[128,2048]{1,0:T(8,128)(2,1)S(1)} %fusion.26), channel_id=1, source_target_pairs={{0,64},{64,0},{1,65},{65,1},{2,66},{66,2},{3,67},{67,3},{4,68},{68... | collective-permute-start | bytes 1572872 | tf_op jit(solution)/shard_map/ppermute | solution.py:771
  324.0 2.0 collective-permute-start.1
  326.1 10.6 %slice-start = ((s8[8388608]{0:T(1024)(128)(4,1)}), s8[4194304]{0:T(1024)(128)(4,1)S(1)}, s32[]{:S(2)}) async-start(s8[8388608]{0:T(1024)(128)(4,1)} %bitcast.77), calls=%async_computation | async-start | bytes 8388608
  327.2 7.6 %copy-start.5 = (f32[2048,128]{1,0:T(8,128)S(1)}, f32[2048,128]{1,0:T(8,128)}, u32[]{:S(2)}) copy-start(f32[2048,128]{1,0:T(8,128)} %get-tuple-element.57) | copy-start | bytes 3145732
  327.2 8.5 %copy-start.4 = (f32[2048,128]{1,0:T(8,128)S(1)}, f32[2048,128]{1,0:T(8,128)}, u32[]{:S(2)}) copy-start(f32[2048,128]{1,0:T(8,128)} %get-tuple-element.58) | copy-start | bytes 3145732
  327.2 9.5 %slice-start.1 = ((s8[8388608]{0:T(1024)(128)(4,1)}), s8[4194304]{0:T(1024)(128)(4,1)S(1)}, s32[]{:S(2)}) async-start(s8[8388608]{0:T(1024)(128)(4,1)} %bitcast.77), calls=%async_computation.1 | async-start | bytes 8388608

commit v4 on v3

--- a/solution.py
+++ b/solution.py
@@ -226,18 +226,23 @@
     return [pltpu.SemaphoreType.DMA((n,)), pltpu.SemaphoreType.DMA((n,))]
 
 
-def grad_layout(d_model, n_local):
-    n_blk = RING ** 3
-    q_tiles = d_model * n_local // 8 // n_blk
-    o_tiles = d_model // 128
-    q_count = [q_tiles * 13 // 32, q_tiles * 11 // 32]
-    q_count.append(q_tiles - sum(q_count))
-    o_count = [o_tiles * 5 // 16, o_tiles * 6 // 16]
-    o_count.append(o_tiles - sum(o_count))
-    q_rows = [8 * n for n in q_count]
-    q_first = [n_blk * sum(q_rows[:c]) for c in range(3)]
-    o_lanes = [(128 * sum(o_count[:c]), 128 * o_count[c]) for c in range(3)]
-    return q_rows, q_first, o_lanes
+def thirds(n, unit):
+    most = n * 3 // 8
+    sizes = (most, most, n - 2 * most)
+    return [(unit * most * c, unit * size) for c, size in enumerate(sizes)]
+
+
+def wide_lanes(d_model):
+    few = d_model // 128 * 5 // 16 * 128
+    sizes = (few, d_model - 2 * few, few)
+    return [(sum(sizes[:c]), size) for c, size in enumerate(sizes)]
+
+
+def spread(ring, src_of, dst, n_rows, sems):
+    pos, right, left, across = ring
+    rows = dst.at[pl.ds(pl.multiple_of(pos * n_rows, n_rows), n_rows)]
+    hops = enumerate((right, across, left))
+    return [remote(src_of((pos + i + 1) % RING), rows, sems, i, device) for i, device in hops]
 
 
 def place_heads(dst, src):
@@ -299,7 +304,7 @@
         self.is_mine = self.tp == self.cp // (RING ** 3 // 2)
 
     def copy(self, kind, batch, slot, device, sem):
-        return pltpu.make_async_remote_copy(src_ref=self.src.at[batch, kind], dst_ref=self.dst.at[slot, kind], send_sem=self.sems[0].at[2 * kind + sem], recv_sem=self.sems[1].at[2 * kind + slot], device_id=device, device_id_type=MESH)
+        return pltpu.make_async_remote_copy(src_ref=self.src[kind].at[batch], dst_ref=self.dst.at[slot, kind], send_sem=self.sems[0].at[2 * kind + sem], recv_sem=self.sems[1].at[2 * kind + slot], device_id=device, device_id_type=MESH)
 
     def near(self, kind):
         return self.copy(kind, 1 - self.tp, 0, (1 - self.tp, self.cp), 0)
@@ -311,7 +316,7 @@
         @pl.when(self.is_mine)
         def _():
             self.near(kind).start()
-            self.dst[0, kind] = self.src[self.tp, kind]
+            self.dst[0, kind] = self.src[kind][self.tp]
 
         @pl.when(jnp.logical_not(self.is_mine))
         def _():
@@ -339,28 +344,36 @@
 D_TILE = 256
 
 
-def attn_kernel(own_ref, qd_ref, grad_ref, cos_ref, sin_ref, oh_ref, dqh_ref, dkv_ref, red0, red1, red2, y0, y1, y2, kv_scr, qd_scr, o_scr, qt_scr, dot_scr, dqt_scr, m_scr, l_scr, delta_scr, p_scr, ds_scr, xo, tok_scr, rot_scr, oh_scr, dqh_scr, *rest):
-    recv, k_sems, o_sems = rest[:3], rest[3:9], rest[9:15]
-    hand_sems, oh_sems, dqh_sems = rest[15:17], rest[17:19], rest[19:21]
+def attn_kernel(k_ref, v_ref, q_ref, hid_ref, grad_ref, wo_ref, cos_ref, sin_ref, oh_ref, dqh_ref, dkv_ref, red0, red1, red2, ho0, ho1, ho2, y0, y1, y2, kv_scr, qd_scr, o_scr, qt_scr, dot_scr, dqt_scr, m_scr, l_scr, delta_scr, p_scr, ds_scr, xo, tok_scr, rot_scr, oh_scr, dqh_scr, do_home, *rest):
+    rest = list(rest)
+
+    def grab(n):
+        return [rest.pop(0) for _ in range(n)]
+
+    recv, hr = grab(3), grab(3)
+    k_sems, o_sems, h_sems = ([grab(2) for _ in range(3)] for _ in range(3))
+    hand_sems, oh_sems, dqh_sems, (h_out,) = grab(2), grab(2), grab(2), rest
     n_groups, _, n_cols, e_dim = qd_scr.shape
-    rows = own_ref.shape[0]
+    rows = k_ref.shape[0]
     per_tile = TILE // BLK
     n_blk = RING ** 3
     d_model = grad_ref.shape[1]
     cp = lax.axis_index("cp")
     mirror = n_blk - 1 - cp
     rings = [ring_of(axis) for axis in range(3)]
-    _, _, o_lanes = grad_layout(d_model, n_cols // rows)
+    o_lanes = wide_lanes(d_model)
     ys = (y0, y1, y2)
     split = by_rows(rows, 16)
-    p_kv = [Part(rings, ORDERS[c], split[c][1], k_sems[2 * c:2 * c + 2], y=ys[c], lanes=(0, 2 * e_dim), align=16, direct=1) for c in range(3)]
-    p_o = [Part(rings, ORDERS[c], n_cols // n_blk, o_sems[2 * c:2 * c + 2], x=xo, recv=[recv[c]], lanes=o_lanes[c]) for c in range(3)]
-    hand = Handout(qd_ref, qd_scr, hand_sems)
+    p_kv = [Part(rings, ORDERS[c], split[c][1], k_sems[c], y=ys[c], lanes=(0, 2 * e_dim), align=16, direct=1) for c in range(3)]
+    p_o = [Part(rings, ORDERS[c], n_cols // n_blk, o_sems[c], x=xo, recv=[recv[c]], lanes=o_lanes[c]) for c in range(3)]
+    hand = Handout((q_ref, do_home), qd_scr, hand_sems)
     o_back = Return(o_scr, oh_scr, oh_sems)
     dq_back = Return(rot_scr, dqh_scr, dqh_sems)
 
     for c in range(3):
-        ys[c][pl.ds(pl.multiple_of(p_kv[c].own_rows(), 16), split[c][1]), :] = own_ref[pl.ds(*split[c]), :]
+        own = pl.ds(pl.multiple_of(p_kv[c].own_rows(), 16), split[c][1])
+        ys[c][own, :e_dim] = k_ref[pl.ds(*split[c]), :]
+        ys[c][own, e_dim:] = v_ref[pl.ds(*split[c]), :]
     enter(rings, with_partner=True, with_mirror=True)
     stage(p_kv, "ag_start2")
     stage(p_kv, "ag_end2")
@@ -368,6 +381,11 @@
     hand.start(0)
     stage(p_kv, "ag_end1")
     stage(p_kv, "ag_start0")
+    for cols in range(0, n_cols, COLS):
+        res = lax.dot_general(grad_ref[...], wo_ref[pl.ds(cols, COLS), :], (((1,), (1,)), ((), ())), preferred_element_type=F32).astype(BF16)
+        for b in range(n_groups):
+            for h in range(COLS // e_dim):
+                do_home[b, pl.ds(cols + h * rows, rows), :] = res[b * rows:(b + 1) * rows, h * e_dim:(h + 1) * e_dim]
     dqt_scr[...] = jnp.zeros_like(dqt_scr)
     dkv_ref[...] = jnp.zeros_like(dkv_ref)
     m_scr[...] = jnp.full_like(m_scr, -jnp.inf)
@@ -386,6 +404,19 @@
             kv_scr[pl.ds(pl.multiple_of(blk * rows + at, 16), rb), :] = ys[c][src, :]
         return carry
 
+    h_slab = d_model // RING
+    n_tok = hid_ref.shape[0]
+
+    def hid_cols(pos):
+        return hid_ref.at[:, pl.ds(pl.multiple_of(pos * h_slab, h_slab), h_slab)]
+
+    h_sent = []
+    for c in range(3):
+        ring = rings[ORDERS[c][0]]
+        h_sent += spread(ring, hid_cols, hr[c], n_tok, h_sems[c])
+        hr[c][pl.ds(pl.multiple_of(ring[0] * n_tok, n_tok), n_tok), :] = hid_cols(ring[0])[...]
+    for copy in h_sent:
+        copy.start()
     lax.fori_loop(0, n_blk, place_kv, 0)
 
     n_first = cp // per_tile + 1
@@ -482,6 +513,11 @@
             turned = jnp.concatenate([low * cos_t + high * sin_t, high * cos_t - low * sin_t], axis=0) * scale
             rot_scr[grp, cols, :] = turned.T.astype(BF16)
     dq_back.start()
+    for copy in h_sent:
+        copy.wait_recv()
+    h_outs = [pltpu.make_async_copy(hr[c], out, h_out.at[c]) for c, out in enumerate((ho0, ho1, ho2))]
+    for copy in h_outs:
+        copy.start()
     oh_ref[...] = oh_scr[...]
     stage(p_o, "rs_end0")
     for part, out, lanes in zip(p_o, (red0, red1, red2), o_lanes):
@@ -495,26 +531,31 @@
         part.drain(rs=(0,))
     for kind in range(2):
         hand.drain(kind)
+    for copy in h_sent:
+        copy.wait_send()
+    for copy in h_outs:
+        copy.wait()
     o_back.drain()
     dq_back.drain()
 
 
-def attention(own_kv, qd_home, grad, cos_t, sin_t):
-    n_batch, _, n_cols, e_dim = qd_home.shape
-    rows = own_kv.shape[0]
+def attention(key_loc, val_loc, q_home, hid, grad, w_out, cos_t, sin_t):
+    n_batch, n_cols, e_dim = q_home.shape
+    rows = key_loc.shape[0]
     n_tok, d_model = grad.shape
     n_blk = RING ** 3
     seq = n_blk * rows
-    _, _, o_lanes = grad_layout(d_model, n_cols // rows)
+    o_lanes = wide_lanes(d_model)
     slab = n_cols // RING
     vmem = pl.BlockSpec(memory_space=pltpu.VMEM)
     heads = (2, n_cols, e_dim)
-    work = 2 * n_cols * seq // 2
+    h_ring = (RING * n_tok, d_model // RING)
+    work = n_cols * seq
     return pl.pallas_call(
         attn_kernel,
-        out_shape=(jax.ShapeDtypeStruct(heads, BF16), jax.ShapeDtypeStruct(heads, BF16), jax.ShapeDtypeStruct((seq, 2 * e_dim), F32)) + tuple(jax.ShapeDtypeStruct((slab, n), F32) for _, n in o_lanes),
-        in_specs=[vmem] * 5,
-        out_specs=(vmem,) * 6,
+        out_shape=(jax.ShapeDtypeStruct(heads, BF16), jax.ShapeDtypeStruct(heads, BF16), jax.ShapeDtypeStruct((seq, 2 * e_dim), F32)) + tuple(jax.ShapeDtypeStruct((slab, n), F32) for _, n in o_lanes) + (jax.ShapeDtypeStruct(h_ring, BF16),) * 3,
+        in_specs=[vmem] * 8,
+        out_specs=(vmem,) * 6 + (pl.BlockSpec(memory_space=pl.ANY),) * 3,
         scratch_shapes=[pltpu.VMEM((n_blk * rb, 2 * e_dim), BF16) for _, rb in by_rows(rows, 16)]
         + [
             pltpu.VMEM((seq, 2 * e_dim), BF16),
@@ -530,58 +571,65 @@
             pltpu.VMEM((TILE, n_cols), BF16),
             pltpu.VMEM((n_cols, d_model), F32),
             pltpu.VMEM((n_tok, n_cols), BF16),
-            pltpu.VMEM(heads, BF16),
-            pltpu.VMEM(heads, BF16),
-            pltpu.VMEM(heads, BF16),
         ]
+        + [pltpu.VMEM(heads, BF16)] * 4
         + [pltpu.VMEM((3 * slab, lanes), F32) for _, lanes in o_lanes]
+        + [pltpu.VMEM(h_ring, BF16)] * 3
         + pair(30) * 6
+        + pair(3) * 3
         + pair(4)
-        + pair(2) * 2,
+        + pair(2) * 2
+        + [pltpu.SemaphoreType.DMA((3,))],
         compiler_params=pltpu.CompilerParams(collective_id=2, has_side_effects=True, vmem_limit_bytes=64000000),
         cost_estimate=pl.CostEstimate(flops=14 * work * e_dim, bytes_accessed=seq * e_dim * 12, transcendentals=2 * work),
         name="attention",
-    )(own_kv, qd_home, grad, cos_t, sin_t)
+    )(key_loc, val_loc, q_home, hid, grad, w_out, cos_t, sin_t)
 
 
 GRAD_PLAN = (
-    "d.rs_start0", "d.rs_mid0", "weights.q", "r.rs_start1", "d.rs_end0", "d.rs_start1", "d.rs_mid1", "r.rs_mid1",
-    "d.rs_end1", "d.rs_start2", "r.rs_end1", "q.rs_start0", "d.rs_end2", "weights.prep", "q.rs_mid0", "weights.kv",
-    "k.rs_start0", "k.rs_mid0", "r.rs_start2", "q.rs_end0", "k.rs_end0", "k.rs_start1", "q.rs_start1", "k.rs_mid1",
-    "q.rs_mid1", "r.rs_end2", "o.ag_start2", "q.rs_end1", "q.rs_start2", "k.rs_end1", "o.ag_end2", "k.rs_start2",
-    "o.ag_start1", "q.rs_end2", "k.rs_end2", "q.ag_start2", "k.ag_start2", "o.ag_mid1", "q.ag_end2", "k.ag_end2",
-    "k.ag_start1", "q.ag_start1", "k.ag_mid1", "q.ag_mid1", "o.ag_end1", "k.ag_end1", "k.ag_start0", "o.ag_start0",
-    "k.ag_mid0", "q.ag_end1", "q.ag_start0", "o.ag_mid0", "q.ag_mid0", "o.ag_end0", "k.ag_end0", "q.ag_end0",
+    "r.rs_start1", "d.rs_start0", "weights.q", "d.rs_mid0", "r.rs_mid1", "s.rs_start1", "d.rs_end0", "d.rs_start1",
+    "r.rs_end1", "s.rs_mid1", "d.rs_mid1", "r.rs_start2", "s.rs_end1", "d.rs_end1", "d.rs_start2", "s.rs_start2",
+    "r.rs_end2", "o.ag_start2", "d.rs_end2", "weights.prep", "weights.kv", "s.rs_end2", "q.ag_start2", "o.ag_end2",
+    "o.ag_start1", "weights.slab", "t.rs_start1", "q.ag_end2", "q.ag_start1", "t.rs_mid1", "o.ag_mid1", "t.rs_end1",
+    "t.rs_start2", "q.ag_mid1", "t.rs_end2", "k.ag_start2", "o.ag_end1", "o.ag_start0", "k.ag_end2", "q.ag_end1",
+    "k.ag_start1", "k.ag_mid1", "q.ag_start0", "k.ag_end1", "k.ag_start0", "o.ag_mid0", "k.ag_mid0", "q.ag_mid0",
+    "k.ag_end0", "o.ag_end0", "q.ag_end0",
 )
 
 
-def grad_kernel(dkv_ref, hid_ref, dqh_ref, red0, red1, red2, cos_ref, sin_ref, gq_ref, go_ref, gk_ref, gv_ref, dkd_ref, x0, x1, x2, xq, xk, yq, yo, yk, yp, xo0, xo1, xo2, tok_scr, mine_scr, give_scr, got_scr, *rest):
-    n_parts = 10
-    recv, sems, in_sem, out_sem, swap_s, swap_r = rest[:27], rest[27:27 + 2 * n_parts], rest[-4], rest[-3], rest[-2], rest[-1]
+def grad_kernel(dkv_ref, dqh_ref, red0, red1, red2, hi0, hi1, hi2, cos_ref, sin_ref, gq_ref, go_ref, gk_ref, gv_ref, dkd_ref, yq, yo, yk, yp, turn_scr, tok_scr, kvt_scr, kvr_scr, mine_scr, give_scr, got_scr, xk, *rest):
+    rest = list(rest)
+
+    def grab(n):
+        return [rest.pop(0) for _ in range(n)]
+
     n_blk = RING ** 3
-    n_tok, d_model = hid_ref.shape
     n_batch, _, head_dim = dqh_ref.shape
+    n_tok, n_cols = tok_scr.shape
+    d_model = yq.shape[0]
     rows, lanes = n_tok // n_batch, 2 * head_dim
-    n_local = dqh_ref.shape[1] // rows
-    n_cols = n_local * head_dim
-    q_rows, q_first, o_lanes = grad_layout(d_model, n_local)
+    n_local = n_cols // head_dim
+    q_lanes, o_lanes = thirds(n_local, head_dim), wide_lanes(d_model)
     split = by_rows(rows, 8)
     tp, cp = lax.axis_index("tp"), lax.axis_index("cp")
     partner = (1 - tp, cp)
-    xs = (x0, x1, x2)
     rings = [ring_of(axis) for axis in range(3)]
-
-    def sem(i):
-        return sems[2 * i:2 * i + 2]
-
-    p_d = [Part(rings, ORDERS[c], split[c][1], sem(c), x=xs[c], recv=recv[3 * c:3 * c + 3], lanes=(0, lanes)) for c in range(3)]
-    p_q = [Part(rings, ORDERS[c], q_rows[c], sem(3 + c), x=xq, y=yq, recv=recv[9 + 3 * c:12 + 3 * c], row0=q_first[c], lanes=(0, 128)) for c in range(3)]
-    p_o = [Part(rings, ORDERS[c], n_cols // n_blk, sem(6 + c), y=yo, lanes=o_lanes[c]) for c in range(3)]
-    xos = (xo0, xo1, xo2)
-    o_slab = n_cols // RING
-    p_r = [Part(rings, ORDERS[c], n_cols // n_blk, sem(6 + c), x=xos[c], recv=[None] + list(recv[21 + 2 * c:23 + 2 * c]), row0=0 - rings[ORDERS[c][0]][0] * o_slab, lanes=(0, o_lanes[c][1])) for c in range(3)]
-    p_k = Part(rings, ORDERS[2], d_model // n_blk, sem(9), x=xk, y=yk, recv=recv[18:21], lanes=(0, 128))
-    p_qo = p_q + p_o
+    colours = range(3)
+
+    def shifted(c, n_rows):
+        return 0 - rings[ORDERS[c][0]][0] * (n_rows // RING)
+
+    xs, xos, xqs, hr, dqr = (grab(3) for _ in range(5))
+    sem_d, sem_q, sem_o, sem_g = ([grab(2) for _ in colours] for _ in range(4))
+    sem_k, sem_kr = grab(2), grab(2)
+    p_d = [Part(rings, ORDERS[c], split[c][1], sem_d[c], x=xs[c], recv=grab(3), lanes=(0, lanes)) for c in colours]
+    p_s = [Part(rings, ORDERS[c], d_model // n_blk, sem_q[c], x=xqs[c], recv=[None] + grab(2), row0=shifted(c, d_model), lanes=(0, q_lanes[c][1])) for c in colours]
+    p_q = [Part(rings, ORDERS[c], d_model // n_blk, sem_q[c], y=yq, lanes=q_lanes[c]) for c in colours]
+    p_r = [Part(rings, ORDERS[c], n_cols // n_blk, sem_o[c], x=xos[c], recv=[None] + grab(2), row0=shifted(c, n_cols), lanes=(0, o_lanes[c][1])) for c in colours]
+    p_o = [Part(rings, ORDERS[c], n_cols // n_blk, sem_o[c], y=yo, lanes=o_lanes[c]) for c in colours]
+    p_t = [Part(rings, ORDERS[2], d_model // n_blk, sem_k, x=xk, recv=[None] + grab(2), row0=shifted(2, d_model), lanes=(0, head_dim))]
+    p_k = [Part(rings, ORDERS[2], d_model // n_blk, sem_k, y=yk, lanes=(0, head_dim))]
+    in_sem, out_sem, swap_s, swap_r = rest
 
     def load(blk, carry):
         for c in range(3):
@@ -591,42 +639,61 @@
         return carry
 
     lax.fori_loop(0, n_blk, load, 0)
-    for c, red in enumerate((red0, red1, red2)):
-        pltpu.make_async_copy(red, xos[c], in_sem.at[3 + c]).start()
+    loads = [pltpu.make_async_copy(src, dst, in_sem.at[3 + i]) for i, (src, dst) in enumerate(zip((red0, red1, red2, hi0, hi1, hi2), xos + hr))]
+    for copy in loads:
+        copy.start()
+    place_heads(tok_scr, dqh_ref)
+
+    def tok_cols(c):
+        return pl.ds(*q_lanes[c])
+
+    dq_sent = []
+    for c in colours:
+        ring = rings[ORDERS[c][0]]
+        dqr[c][pl.ds(pl.multiple_of(ring[0] * n_tok, n_tok), n_tok), :] = tok_scr[:, tok_cols(c)]
+        dq_sent += spread(ring, lambda pos, c=c: tok_scr.at[:, tok_cols(c)], dqr[c], n_tok, sem_g[c])
+    ring_k = rings[ORDERS[2][0]]
+    kv_sent = spread(ring_k, lambda pos: kvt_scr, kvr_scr, n_tok, sem_kr)
     enter(rings, with_partner=True)
-    for c, red in enumerate((red0, red1, red2)):
-        pltpu.make_async_copy(red, xos[c], in_sem.at[3 + c]).wait()
-    for c in range(3):
+    for copy in dq_sent:
+        copy.start()
+    for copy in loads:
+        copy.wait()
+    for c in colours:
         pltpu.make_async_copy(dkv_ref.at[pl.ds(0, n_blk * split[c][1])], xs[c], in_sem.at[c]).wait()
     half_dim = head_dim // 2
     first = tp == 0
     swap_small = pltpu.make_async_remote_copy(src_ref=give_scr, dst_ref=got_scr, send_sem=swap_s.at[0], recv_sem=swap_r.at[0], device_id=partner, device_id_type=MESH)
     swap = pltpu.make_async_remote_copy(src_ref=yk, dst_ref=yp, send_sem=swap_s.at[1], recv_sem=swap_r.at[1], device_id=partner, device_id_type=MESH)
 
-    def put(parts, which):
-        for part in parts:
-            out = gq_ref if part.y is yq else go_ref
+    def put_o(which):
+        for c, part in enumerate(p_o):
             slab, _, _, starts, *_ = part.place(0)
             for i in which:
-                src, dst = part.view(part.y, starts[i], slab), part.view(out, starts[i], slab)
-                pltpu.make_async_copy(src, dst, out_sem.at[p_qo.index(part)]).start()
+                pltpu.make_async_copy(part.view(yo, starts[i], slab), part.view(go_ref, starts[i], slab), out_sem.at[c]).start()
+
+    def turn_q(which):
+        for c, part in enumerate(p_q):
+            slab, _, _, starts, *_ = part.place(0)
+            for i in which:
+                at = pl.multiple_of(starts[i], slab)
+                for h in range(q_lanes[c][0] // head_dim, sum(q_lanes[c]) // head_dim):
+                    turn_scr[pl.ds(at * n_local + h, slab, stride=n_local), :] = yq[pl.ds(at, slab), pl.ds(h * head_dim, head_dim)]
 
     def own_block(parts, sums):
         for part, total in zip(parts, sums):
             at, lanes_y, lanes_x = part.own_rows(), pl.ds(*part.lanes), pl.ds(*total.lanes)
             part.y[pl.ds(pl.multiple_of(at, 8), part.rb), lanes_y] = total.x[pl.ds(pl.multiple_of(total.own_rows(), 8), part.rb), lanes_x]
 
+    def slab_term(dst, hid, other):
+        for at in range(0, dst.shape[0], D_TILE):
+            dst[pl.ds(at, D_TILE), :] = dot_ta(hid[:, at:at + D_TILE], other[...])
+
     def weights_q():
-        place_heads(tok_scr, dqh_ref)
-
-        def q_body(i, carry):
-            cols = pl.ds(pl.multiple_of(i * D_TILE, D_TILE), D_TILE)
-            res = dot_ta(hid_ref[:, cols], tok_scr[...])
-            for h in range(n_local):
-                xq[pl.ds(i * D_TILE * n_local + h, D_TILE, stride=n_local), :] = res[:, h * head_dim:(h + 1) * head_dim]
-            return carry
-
-        lax.fori_loop(0, d_model // D_TILE, q_body, 0)
+        for copy in dq_sent:
+            copy.wait_recv()
+        for c in colours:
+            slab_term(xqs[c], hr[c], dqr[c])
 
     def new_dkv():
         dkd_ref[...] = mine_scr[...].astype(BF16)
@@ -648,23 +715,30 @@
         swap_small.wait()
         got = got_scr[...]
         keep = jnp.where(first, dkd_ref[:, :head_dim], dkd_ref[:, head_dim:])
-        kv_tok = jnp.concatenate([jnp.where(first, keep, got), jnp.where(first, got, keep)], axis=0)
-        for i in range(d_model // D_TILE):
-            xk[pl.ds(i * D_TILE, D_TILE), :] = dot_ta(hid_ref[:, i * D_TILE:(i + 1) * D_TILE], kv_tok)
-
-    groups = {"d": p_d, "q": p_q, "r": p_r, "o": p_o, "k": [p_k]}
+        kvt_scr[...] = jnp.concatenate([jnp.where(first, keep, got), jnp.where(first, got, keep)], axis=0)
+        kvr_scr[pl.ds(pl.multiple_of(ring_k[0] * n_tok, n_tok), n_tok), :] = kvt_scr[...]
+        for copy in kv_sent:
+            copy.start()
+
+    def weights_slab():
+        for copy in kv_sent:
+            copy.wait_recv()
+        slab_term(xk, hr[2], kvr_scr)
+
+    groups = {"d": p_d, "s": p_s, "q": p_q, "r": p_r, "o": p_o, "t": p_t, "k": p_k}
     after = {
         "weights.q": weights_q,
         "weights.prep": weights_prep,
         "weights.kv": weights_kv,
+        "weights.slab": weights_slab,
         "r.rs_end2": lambda: own_block(p_o, p_r),
-        "q.rs_end2": lambda: own_block(p_q, p_q),
-        "k.rs_end2": lambda: own_block([p_k], [p_k]),
-        "o.ag_mid0": lambda: put(p_o, (0, 1, 3)),
-        "o.ag_end0": lambda: put(p_o, (2,)),
-        "q.ag_start0": lambda: put(p_q, (0,)),
-        "q.ag_mid0": lambda: put(p_q, (1, 3)),
-        "q.ag_end0": lambda: put(p_q, (2,)),
+        "s.rs_end2": lambda: own_block(p_q, p_s),
+        "t.rs_end2": lambda: own_block(p_k, p_t),
+        "o.ag_mid0": lambda: put_o((0, 1, 3)),
+        "o.ag_end0": lambda: put_o((2,)),
+        "q.ag_start0": lambda: turn_q((0,)),
+        "q.ag_mid0": lambda: turn_q((1, 3)),
+        "q.ag_end0": lambda: turn_q((2,)),
         "k.ag_end0": swap.start,
     }
     for step in GRAD_PLAN:
@@ -673,10 +747,12 @@
             stage(groups[who], what)
         if step in after:
             after[step]()
+    out_q = pltpu.make_async_copy(turn_scr, gq_ref, out_sem.at[3])
+    out_q.start()
     swap.wait()
 
     def put_kv(k_src, v_src):
-        outs = [pltpu.make_async_copy(k_src, gk_ref, out_sem.at[6]), pltpu.make_async_copy(v_src, gv_ref, out_sem.at[7])]
+        outs = [pltpu.make_async_copy(k_src, gk_ref, out_sem.at[4]), pltpu.make_async_copy(v_src, gv_ref, out_sem.at[5])]
         for copy in outs:
             copy.start()
         for copy in outs:
@@ -690,59 +766,68 @@
     def _():
         put_kv(yp, yk)
 
-    for i, part in enumerate(p_qo):
-        out = gq_ref if part.y is yq else go_ref
-        span = n_blk * part.rb
-        pltpu.make_async_copy(part.view(part.y, part.row0, span), part.view(out, part.row0, span), out_sem.at[i]).wait()
+    out_q.wait()
+    for c, part in enumerate(p_o):
+        pltpu.make_async_copy(part.view(yo, 0, n_cols), part.view(go_ref, 0, n_cols), out_sem.at[c]).wait()
     for part in p_d:
         part.drain(rs=range(3))
-    for part in p_q + [p_k]:
-        part.drain(rs=range(3), ag=range(3))
-    for part, red in zip(p_o, p_r):
-        red.drain(rs=(1, 2))
+    for part in p_s + p_r + p_t:
+        part.drain(rs=(1, 2))
+    for part in p_q + p_o + p_k:
         part.drain(ag=range(3))
-
-
-def grad_sums(dkv, hid, dq_home, reds, cos_tab, sin_tab):
-    n_tok, d_model = hid.shape
-    n_batch, _, head_dim = dq_home.shape
-    block_len = n_tok // n_batch
-    n_local = dq_home.shape[1] // block_len
-    n_cols = n_local * head_dim
+    for copy in dq_sent + kv_sent:
+        copy.wait_send()
+
+
+def grad_sums(dkv, dq_home, reds, h_rings, cos_tab, sin_tab, d_model):
+    n_batch, n_rows, head_dim = dq_home.shape
+    rows = cos_tab.shape[0]
+    n_tok, n_cols = n_batch * rows, n_rows // rows * head_dim
     n_blk = RING ** 3
     lanes = 2 * head_dim
-    q_rows, _, o_lanes = grad_layout(d_model, n_local)
-    split = by_rows(block_len, 8)
-    recv = [pltpu.VMEM((n, lanes), F32) for _, rb in split for n in slab_rows(rb)]
-    recv += [pltpu.VMEM((n, 128), F32) for rb in q_rows for n in slab_rows(rb)]
-    recv += [pltpu.VMEM((n, 128), F32) for n in slab_rows(d_model // n_blk)]
-    recv += [pltpu.VMEM((n, w), F32) for _, w in o_lanes for n in slab_rows(n_cols // n_blk)[1:]]
+    q_lanes, o_lanes = thirds(n_cols // head_dim, head_dim), wide_lanes(d_model)
+    split = by_rows(rows, 8)
     vmem, anyspace = pl.BlockSpec(memory_space=pltpu.VMEM), pl.BlockSpec(memory_space=pl.ANY)
-    xq, xo, xk = (pltpu.VMEM(s, F32) for s in ((d_model * n_local, 128), (n_cols, d_model), (d_model, 128)))
-    small = pltpu.VMEM((block_len, head_dim), BF16)
+
+    def full(*shape):
+        return pltpu.VMEM(shape, F32)
+
+    def half(*shape):
+        return pltpu.VMEM(shape, BF16)
+
+    def later(rb, width):
+        return [full(n, width) for n in slab_rows(rb)[1:]]
+
+    slab, ring_tok = d_model // RING, RING * n_tok
+    scratch = [full(d_model, n_cols), full(n_cols, d_model), full(d_model, head_dim), full(d_model, head_dim), full(d_model * n_cols // head_dim, head_dim)]
+    scratch += [half(n_tok, n_cols), half(n_tok, head_dim), half(ring_tok, head_dim), full(rows, lanes), half(rows, head_dim), half(rows, head_dim), full(slab, head_dim)]
+    scratch += [full(n_blk * rb, lanes) for _, rb in split]
+    scratch += [full(n_cols // RING, w) for _, w in o_lanes] + [full(slab, w) for _, w in q_lanes]
+    scratch += [half(ring_tok, slab)] * 3 + [half(ring_tok, w) for _, w in q_lanes]
+    scratch += pair(30) * 9 + pair(3) * 3 + pair(30) + pair(3)
+    scratch += [full(n, lanes) for _, rb in split for n in slab_rows(rb)]
+    for _, w in q_lanes:
+        scratch += later(d_model // n_blk, w)
+    for _, w in o_lanes:
+        scratch += later(n_cols // n_blk, w)
+    scratch += later(d_model // n_blk, head_dim)
+    scratch += [pltpu.SemaphoreType.DMA((9,)), pltpu.SemaphoreType.DMA((6,))] + pair(2)
     return pl.pallas_call(
         grad_kernel,
         out_shape=(
-            jax.ShapeDtypeStruct((d_model * n_local, 128), F32),
+            jax.ShapeDtypeStruct((d_model * n_cols // head_dim, head_dim), F32),
             jax.ShapeDtypeStruct((n_cols, d_model), F32),
-            jax.ShapeDtypeStruct((d_model, 128), F32),
-            jax.ShapeDtypeStruct((d_model, 128), F32),
-            jax.ShapeDtypeStruct((block_len, lanes), BF16),
+            jax.ShapeDtypeStruct((d_model, head_dim), F32),
+            jax.ShapeDtypeStruct((d_model, head_dim), F32),
+            jax.ShapeDtypeStruct((rows, lanes), BF16),
         ),
-        in_specs=[anyspace] + [vmem] * 2 + [anyspace] * 3 + [vmem] * 2,
+        in_specs=[anyspace, vmem] + [anyspace] * 6 + [vmem] * 2,
         out_specs=(anyspace,) * 4 + (vmem,),
-        scratch_shapes=[pltpu.VMEM((n_blk * rb, lanes), F32) for _, rb in split]
-        + [xq, xk, xq, xo, xk, xk]
-        + [pltpu.VMEM((n_cols // RING, w), F32) for _, w in o_lanes]
-        + [pltpu.VMEM((n_tok, n_cols), BF16), pltpu.VMEM((block_len, lanes), F32), small, small]
-        + recv
-        + pair(30) * 10
-        + [pltpu.SemaphoreType.DMA((6,)), pltpu.SemaphoreType.DMA((8,))]
-        + pair(2),
+        scratch_shapes=scratch,
         compiler_params=pltpu.CompilerParams(collective_id=3, has_side_effects=True, vmem_limit_bytes=67000000),
-        cost_estimate=pl.CostEstimate(flops=2 * n_tok * d_model * n_cols * 80, bytes_accessed=40 << 20, transcendentals=0),
+        cost_estimate=pl.CostEstimate(flops=n_tok * d_model * n_cols * 160, bytes_accessed=40 << 20, transcendentals=0),
         name="grad_sums",
-    )(dkv, hid, dq_home, *reds, cos_tab, sin_tab)
+    )(dkv, dq_home, *reds, *h_rings, cos_tab, sin_tab)
 
 
 def solution(mesh):
@@ -775,18 +860,17 @@
         hid_b = pick(hidden, tp_idx)
         key_loc = rotate(dot(hid_b, w_key), cos_tab, sin_tab).astype(BF16)
         val_loc = dot(hid_b, w_value).astype(BF16)
-        own_kv = jnp.concatenate([key_loc, val_loc], axis=1)
-
         q_pre = jnp.einsum("bsd,dhe->bhse", hidden, w_query, preferred_element_type=F32)
         queries = (rotate(q_pre, cos_tab, sin_tab) * q_scale).astype(BF16)
-        d_out = jnp.einsum("bsd,hed->bhse", grad_out, w_out, preferred_element_type=F32).astype(BF16)
-        qd_home = jnp.stack([queries, d_out], axis=1).reshape(2, 2, n_local * block_len, head_dim)
+        q_home = queries.reshape(2, n_local * block_len, head_dim)
+        d_model = hidden.shape[-1]
+        hid, grad = hidden.reshape(-1, d_model), grad_out.reshape(-1, d_model)
         tabs_t = [jnp.stack(pair_t) for pair_t in ((cos_tab.T, cos_mir.T), (sin_tab.T, sin_mir.T))]
-        o_home, dq_home, dkv, *reds = attention(own_kv, qd_home, grad_out.reshape(-1, grad_out.shape[-1]), *tabs_t)
+        o_home, dq_home, dkv, *more = attention(key_loc, val_loc, q_home, hid, grad, w_out.reshape(-1, d_model), *tabs_t)
         attn_heads = o_home.reshape(2, n_local, block_len, head_dim)
         dq_pre = dq_home.reshape(2, n_local, block_len, head_dim)
         attn_out = sum_over_tp(jnp.einsum("cirf,ife->cre", attn_heads, w_out, preferred_element_type=F32))
-        grad_q, grad_o, d_w_key, d_w_value, dkv_new = grad_sums(dkv, hidden.reshape(-1, hidden.shape[-1]), dq_home, reds, cos_tab, sin_tab)
+        grad_q, grad_o, d_w_key, d_w_value, dkv_new = grad_sums(dkv, dq_home, more[:3], more[3:], cos_tab, sin_tab, d_model)
         d_w_query = grad_q.reshape(w_query.shape)
         d_w_out = grad_o.reshape(w_out.shape)
         dk_pre, dv_pre = dkv_new[:, :head_dim], dkv_new[:, head_dim:]

time: 340 us -> 327 us (0.962)
  Pallas kernels: 291 us -> 280 us
    pallas_call x1, Pallas kernels: 161 us -> 145 us  [grad_sums(): pl.pallas_call(grad_kernel, out_shape=(jax.ShapeDtypeStruct((d_model * n_...]
    pallas_call x1, Pallas kernels: 130 us -> 136 us  [attention(): pl.pallas_call(attn_kernel, out_shape=(jax.ShapeDtypeStruct(heads, BF16),...]
    dot_general x1 -> x0, matrix products: 3.88 us -> none  [local_program(): jnp.einsum('bsd,hed->bhse', grad_out, w_out, preferred_element_type=F32)]
    unnamed x28 -> x26, local copies, waits for them, and re-layouts: 14.3 us -> 14.3 us
  transfers between devices with their start and end apart: 4 -> 4, of which waited for: 2 -> 2; matrix products, arithmetic and copies ran while one was open for 3% -> 3% of each run, Pallas kernels for 47% -> 44%
where the time goes in v4:
time: 327 us
  Pallas kernels  280 us (86%)
  matrix products  18 us (6%)
  local copies, waits for them, and re-layouts  17.3 us (5%)
  other arithmetic  6.88 us (2%)
    pallas_call x1, Pallas kernels, grad_sums(): pl.pallas_call(grad_kernel, out_shape=(jax.ShapeDtypeStruct((d_model * n_...  145 us
    pallas_call x1, Pallas kernels, attention(): pl.pallas_call(attn_kernel, out_shape=(jax.ShapeDtypeStruct(heads, BF16),...  136 us
    unnamed x26, local copies, waits for them, and re-layouts  14.3 us
    dot_general x4, matrix products, dot(): return jnp.dot(a, b, preferred_element_type=F32)  7.03 us
  transfers between devices with their start and end apart: 4, of which 2 were waited for; matrix products, arithmetic and copies ran while one was open for 3% of the time, Pallas kernels for 44%

profile of v4, /device:TPU:1, one launch (start us, length us, event | category | flops | bytes accessed | tf_op | source)
XLA Modules:
  0.0 327.0 jit_solution(8017986067881797224)
XLA Ops:
  0.7 1.5 fusion.22
  2.2 0.3 multiply_cosine_fusion
  2.5 0.0 copy-start.7
  2.5 0.0 copy-start.8
  2.5 0.1 copy.24
  2.6 0.1 copy.25
  2.7 3.9 %fusion.13 = f32[2,8,128,128]{2,3,0,1:T(8,128)S(1)} fusion(bf16[2048,8,128,1]{2,1,0,3:T(8,128)(2,1)} %bitcast.73, bf16[2,128,2048]{2,1,0:T(8,128)(2,1)} %param.6), kind=kOutput, calls=%fused_computation.10 | convolution fusion | flops 1073741824 | bytes 6291456 | tf_op jit(solution)/shard_map/bsd,dhe->bhse/dot_general | solution.py:863
  6.5 0.0 copy-done.7
  6.5 0.0 copy-done.8
  6.5 0.0 copy-start.3
  6.6 0.1 multiply_subtract_fusion
  6.7 0.3 copy.26
  7.0 0.3 copy.27
  7.4 0.3 multiply_sine_fusion.2
  7.7 0.0 copy-done.3
  7.7 2.0 convolution_convert_fusion.v_ref
  9.7 1.1 fusion.16.q_ref
  10.8 0.7 pad_maximum_fusion.4.k_ref
  11.5 0.7 pad_maximum_fusion.2
  12.2 135.7 %attention.1 = (bf16[2,1024,128]{2,1,0:T(8,128)(2,1)}, bf16[2,1024,128]{2,1,0:T(8,128)(2,1)}, f32[8192,256]{1,0:T(8,128)}, f32[256,640]{1,0:T(8,128)}, f32[256,7...) custom-call(bf16[128,128]{1,0:T(8,128)(2,1)} %pad_maximum_fusion.4.k, ...), custom_call_target="tpu_custom_call" | custom-call | flops 15032385536 | bytes 12582912 | tf_op jit(solution)/shard_map/attention/pallas_call | solution.py:554
  147.9 0.0 copy-start.6
  147.9 3.7 %fusion.10 = f32[2,128,2048]{2,1,0:T(8,128)S(1)} fusion(bf16[2,8,128,128]{3,2,1,0:T(8,128)(2,1)} %bitcast.75, bf16[2048,8,128]{2,1,0:T(8,128)(2,1)} %param.8), kind=kOutput, calls=%fused_computation.8 | convolution fusion | flops 1073741824 | bytes 6815744 | tf_op jit(solution)/shard_map/cirf,eif->cre/dot_general | solution.py:878
  151.6 0.0 copy-start.2
  151.6 1.1 dynamic-slice_bitcast_fusion
  152.8 0.4 collective-permute-start.2
  153.2 0.0 copy-done.6
  153.2 3.4 %fusion.7 = f32[2,128,2048]{2,1,0:T(8,128)S(1)} fusion(bf16[2,8,128,128]{3,2,1,0:T(8,128)(2,1)S(1)} %bitcast.72, bf16[8,128,2048]{2,1,0:T(8,128)(2,1)} %param.11), kind=kOutput, calls=%fused_computation.7 | convolution fusion | flops 1073741824 | bytes 6815744 | tf_op jit(solution)/shard_map/cirf,ife->cre/dot_general | solution.py:872
  156.6 0.0 copy-done.2
  156.6 0.0 copy-start
  156.6 1.3 copy-done
  157.9 1.0 dynamic-slice_bitcast_fusion.1
  159.0 0.1 collective-permute-start
  159.1 144.6 %grad_sums.1 = (f32[16384,128]{1,0:T(8,128)}, f32[1024,2048]{1,0:T(8,128)}, f32[2048,128]{1,0:T(8,128)}, f32[2048,128]{1,0:T(8,128)}, bf16[128,256]{1,0:T(8,128)(2,1)}) custom-call(f32[8192,256]{1,0:T(8,128)} %get-tuple-element.22.dkv_ref, bf16[2,1024,128]{2,1,0:T(8,128)(2,1)} %get-tuple-element.21.dqh_ref, f32[256,640]{1,0:T(8,128)} %get-tuple-element.23.red0, ...), custom_call_target="tpu_custom_call" | custom-call | flops 85899345920 | bytes 41943040 | tf_op jit(solution)/shard_map/grad_sums/pallas_call | solution.py:815
  303.7 0.0 copy-start.1
  303.7 1.5 fusion.29
  305.2 0.0 collective-permute-done.2
  305.2 2.1 fusion.18
  307.3 2.3 collective-permute-start.3
  309.6 0.0 collective-permute-done
  309.6 0.0 copy-done.1
  309.6 1.3 fusion.19
  311.0 0.1 collective-permute-start.1
  311.1 0.1 collective-permute-done.3
  311.1 0.1 select_bitcast_fusion.1
  311.2 1.1 pad_maximum_fusion.1
  312.3 0.7 collective-permute-done.1
  312.9 0.1 select_bitcast_fusion.3
  313.0 0.0 slice-start
  313.0 1.1 pad_maximum_fusion
  314.1 0.0 copy-start.5
  314.1 0.0 copy-start.4
  314.1 0.0 slice-start.1
  314.1 7.6 %copy.49 = f32[2048,8,128]{2,1,0:T(8,128)} copy(f32[2048,8,128]{2,1,0:T(8,128)} %bitcast.67) | data formatting | bytes 16777216
  321.7 0.0 copy-done.5
  321.7 1.0 copy.50
  322.6 0.0 copy-done.4
  322.6 1.0 copy.51
  323.6 0.0 slice-done
  323.6 0.0 slice-done.1
  323.6 3.4 %copy.52 = f32[8,128,2048]{2,1,0:T(8,128)} copy(f32[8,128,2048]{2,1,0:T(8,128)S(1)} %bitcast.66) | data formatting | bytes 16777216
  (4 shorter events, 0.0 us)
Async XLA Ops:
  2.5 4.0 %copy-start.7 = (f32[128,64]{1,0:T(8,128)}, f32[128,64]{1,0:T(8,128)S(1)}, u32[]{:S(2)}) copy-start(f32[128,64]{1,0:T(8,128)S(1)} %get-tuple-element.46.cos_ref) | copy-start | bytes 98308
  2.5 4.0 %copy-start.8 = (f32[128,64]{1,0:T(8,128)}, f32[128,64]{1,0:T(8,128)S(1)}, u32[]{:S(2)}) copy-start(f32[128,64]{1,0:T(8,128)S(1)} %get-tuple-element.47.sin_ref) | copy-start | bytes 98308
  6.5 1.2 copy-start.3
  147.9 5.2 %copy-start.6 = (bf16[2,1024,128]{2,1,0:T(8,128)(2,1)S(1)}, bf16[2,1024,128]{2,1,0:T(8,128)(2,1)}, u32[]{:S(2)}) copy-start(bf16[2,1024,128]{2,1,0:T(8,128)(2,1)} %get-tuple-element.20) | copy-start | bytes 1572868
  151.6 5.0 %copy-start.2 = (f32[2,128,2048]{2,1,0:T(8,128)}, f32[2,128,2048]{2,1,0:T(8,128)S(1)}, u32[]{:S(2)}) copy-start(f32[2,128,2048]{2,1,0:T(8,128)S(1)} %fusion.10) | copy-start | bytes 6291460
  152.8 152.4 %collective-permute-start.2 = (f32[128,2048]{1,0:T(8,128)}, f32[128,2048]{1,0:T(8,128)}, u32[]{:S(2)}, u32[]{:S(2)}) collective-permute-start(f32[128,2048]{1,0:T(8,128)} %dynamic-slice_bitcast_fusion), channel_id=1, source_target_pairs={{0,64},{64,0},{1,65},{65,1},{2,66},{66,2},{3,67},{67,3},{4,68},{68... | collective-permute-start | bytes 3145736 | tf_op jit(solution)/shard_map/ppermute | solution.py:852
  156.6 1.3 copy-start
  159.0 150.6 %collective-permute-start = (f32[128,2048]{1,0:T(8,128)}, f32[128,2048]{1,0:T(8,128)}, u32[]{:S(2)}, u32[]{:S(2)}) collective-permute-start(f32[128,2048]{1,0:T(8,128)} %dynamic-slice_bitcast_fusion.1), channel_id=1, source_target_pairs={{0,64},{64,0},{1,65},{65,1},{2,66},{66,2},{3,67},{67,3},{4,68},{68... | collective-permute-start | bytes 3145736 | tf_op jit(solution)/shard_map/ppermute | solution.py:852
  303.7 5.9 %copy-start.1 = (f32[2,128,2048]{2,1,0:T(8,128)S(1)}, f32[2,128,2048]{2,1,0:T(8,128)}, u32[]{:S(2)}) copy-start(f32[2,128,2048]{2,1,0:T(8,128)} %copy-done) | copy-start | bytes 6291460
  307.3 3.8 %collective-permute-start.3 = (bf16[128,2048]{1,0:T(8,128)(2,1)S(1)}, bf16[128,2048]{1,0:T(8,128)(2,1)S(1)}, u32[]{:S(2)}, u32[]{:S(2)}) collective-permute-start(bf16[128,2048]{1,0:T(8,128)(2,1)S(1)} %fusion.18), channel_id=1, source_target_pairs={{0,64},{64,0},{1,65},{65,1},{2,66},{66,2},{3,67},{67,3},{4,68},{68... | collective-permute-start | bytes 1572872 | tf_op jit(solution)/shard_map/ppermute | solution.py:856
  311.0 2.0 collective-permute-start.1
  313.0 10.6 %slice-start = ((s8[8388608]{0:T(1024)(128)(4,1)}), s8[4194304]{0:T(1024)(128)(4,1)S(1)}, s32[]{:S(2)}) async-start(s8[8388608]{0:T(1024)(128)(4,1)} %bitcast.64), calls=%async_computation | async-start | bytes 8388608
  314.1 7.6 %copy-start.5 = (f32[2048,128]{1,0:T(8,128)S(1)}, f32[2048,128]{1,0:T(8,128)}, u32[]{:S(2)}) copy-start(f32[2048,128]{1,0:T(8,128)} %get-tuple-element.63) | copy-start | bytes 3145732
  314.1 8.5 %copy-start.4 = (f32[2048,128]{1,0:T(8,128)S(1)}, f32[2048,128]{1,0:T(8,128)}, u32[]{:S(2)}) copy-start(f32[2048,128]{1,0:T(8,128)} %get-tuple-element.64) | copy-start | bytes 3145732
  314.1 9.5 %slice-start.1 = ((s8[8388608]{0:T(1024)(128)(4,1)}), s8[4194304]{0:T(1024)(128)(4,1)S(1)}, s32[]{:S(2)}) async-start(s8[8388608]{0:T(1024)(128)(4,1)} %bitcast.64), calls=%async_computation.1 | async-start | bytes 8388608

commit v5 on v4

--- a/solution.py
+++ b/solution.py
@@ -8,6 +8,8 @@
 ROPE_BASE = 10000.0
 BLK = 128
 TILE = 512
+COLOURS = range(3)
+VMEM_LIMIT = 67000000
 COLS = 256
 F32 = jnp.float32
 BF16 = jnp.bfloat16
@@ -103,7 +105,7 @@
         self.row0, self.lanes, self.align = row0, lanes, align
         self.places = []
         base = row0
-        for phase in range(3):
+        for phase in COLOURS:
             slab = rb * RING ** (2 - phase)
             h0 = -(-slab // (2 * align)) * align
             pos, right, left, across = rings[order[phase]]
@@ -207,7 +209,7 @@
 
 
 def slab_rows(rb):
-    return [3 * rb * RING ** (2 - phase) for phase in range(3)]
+    return [3 * rb * RING ** (2 - phase) for phase in COLOURS]
 
 
 def place_in_order(block, order):
@@ -217,9 +219,9 @@
 
 def by_rows(n_rows, align):
     unit = n_rows // align
-    counts = [(unit + 2 - c) // 3 for c in range(3)]
-    starts = [sum(counts[:c]) * align for c in range(3)]
-    return [(starts[c], counts[c] * align) for c in range(3)]
+    counts = [(unit + 2 - c) // 3 for c in COLOURS]
+    starts = [sum(counts[:c]) * align for c in COLOURS]
+    return [(starts[c], counts[c] * align) for c in COLOURS]
 
 
 def pair(n):
@@ -344,15 +346,15 @@
 D_TILE = 256
 
 
-def attn_kernel(k_ref, v_ref, q_ref, hid_ref, grad_ref, wo_ref, cos_ref, sin_ref, oh_ref, dqh_ref, dkv_ref, red0, red1, red2, ho0, ho1, ho2, y0, y1, y2, kv_scr, qd_scr, o_scr, qt_scr, dot_scr, dqt_scr, m_scr, l_scr, delta_scr, p_scr, ds_scr, xo, tok_scr, rot_scr, oh_scr, dqh_scr, do_home, *rest):
+def attn_kernel(k_ref, v_ref, q_ref, hid_ref, grad_ref, wo_ref, cos_ref, sin_ref, dqh_ref, out_ref, sl0, sl1, sl2, red0, red1, red2, ho0, ho1, ho2, y0, y1, y2, kv_scr, qd_scr, o_scr, qt_scr, dot_scr, dqt_scr, m_scr, l_scr, delta_scr, p_scr, ds_scr, dkv_scr, tok_scr, part_scr, got_scr, out_scr, rot_scr, oh_scr, dqh_scr, do_home, *rest):
     rest = list(rest)
 
     def grab(n):
         return [rest.pop(0) for _ in range(n)]
 
-    recv, hr = grab(3), grab(3)
-    k_sems, o_sems, h_sems = ([grab(2) for _ in range(3)] for _ in range(3))
-    hand_sems, oh_sems, dqh_sems, (h_out,) = grab(2), grab(2), grab(2), rest
+    hr, gr, orr, xs = (grab(3) for _ in range(4))
+    k_sems, d_sems, h_sems, g_sems, or_sems = ([grab(2) for _ in COLOURS] for _ in range(5))
+    hand_sems, oh_sems, dqh_sems, swap_sems = (grab(2) for _ in range(4))
     n_groups, _, n_cols, e_dim = qd_scr.shape
     rows = k_ref.shape[0]
     per_tile = TILE // BLK
@@ -360,17 +362,19 @@
     d_model = grad_ref.shape[1]
     cp = lax.axis_index("cp")
     mirror = n_blk - 1 - cp
-    rings = [ring_of(axis) for axis in range(3)]
+    rings = [ring_of(axis) for axis in COLOURS]
     o_lanes = wide_lanes(d_model)
     ys = (y0, y1, y2)
     split = by_rows(rows, 16)
-    p_kv = [Part(rings, ORDERS[c], split[c][1], k_sems[c], y=ys[c], lanes=(0, 2 * e_dim), align=16, direct=1) for c in range(3)]
-    p_o = [Part(rings, ORDERS[c], n_cols // n_blk, o_sems[c], x=xo, recv=[recv[c]], lanes=o_lanes[c]) for c in range(3)]
+    p_kv = [Part(rings, ORDERS[c], split[c][1], k_sems[c], y=ys[c], lanes=(0, 2 * e_dim), align=16, direct=1) for c in COLOURS]
+    rows_d = by_rows(rows, 8)
+    p_d = [Part(rings, ORDERS[c], rows_d[c][1], d_sems[c], x=xs[c], recv=grab(1), lanes=(0, 2 * e_dim)) for c in COLOURS]
+    h_out, = rest
     hand = Handout((q_ref, do_home), qd_scr, hand_sems)
     o_back = Return(o_scr, oh_scr, oh_sems)
     dq_back = Return(rot_scr, dqh_scr, dqh_sems)
 
-    for c in range(3):
+    for c in COLOURS:
         own = pl.ds(pl.multiple_of(p_kv[c].own_rows(), 16), split[c][1])
         ys[c][own, :e_dim] = k_ref[pl.ds(*split[c]), :]
         ys[c][own, e_dim:] = v_ref[pl.ds(*split[c]), :]
@@ -387,7 +391,7 @@
             for h in range(COLS // e_dim):
                 do_home[b, pl.ds(cols + h * rows, rows), :] = res[b * rows:(b + 1) * rows, h * e_dim:(h + 1) * e_dim]
     dqt_scr[...] = jnp.zeros_like(dqt_scr)
-    dkv_ref[...] = jnp.zeros_like(dkv_ref)
+    dkv_scr[...] = jnp.zeros_like(dkv_scr)
     m_scr[...] = jnp.full_like(m_scr, -jnp.inf)
     l_scr[...] = jnp.zeros_like(l_scr)
     hand.wait(0)
@@ -398,7 +402,7 @@
     stage(p_kv, "ag_end0")
 
     def place_kv(blk, carry):
-        for c in range(3):
+        for c in COLOURS:
             at, rb = split[c]
             src = pl.ds(pl.multiple_of(place_in_order(blk, ORDERS[c]) * rb, 16), rb)
             kv_scr[pl.ds(pl.multiple_of(blk * rows + at, 16), rb), :] = ys[c][src, :]
@@ -410,11 +414,19 @@
     def hid_cols(pos):
         return hid_ref.at[:, pl.ds(pl.multiple_of(pos * h_slab, h_slab), h_slab)]
 
-    h_sent = []
-    for c in range(3):
+    def grad_cols(c):
+        return grad_ref.at[:, pl.ds(*o_lanes[c])]
+
+    h_sent, g_sent = [], []
+    for c in COLOURS:
         ring = rings[ORDERS[c][0]]
+        here = pl.ds(pl.multiple_of(ring[0] * n_tok, n_tok), n_tok)
         h_sent += spread(ring, hid_cols, hr[c], n_tok, h_sems[c])
-        hr[c][pl.ds(pl.multiple_of(ring[0] * n_tok, n_tok), n_tok), :] = hid_cols(ring[0])[...]
+        g_sent += spread(ring, lambda pos, c=c: grad_cols(c), gr[c], n_tok, g_sems[c])
+        hr[c][here, :] = hid_cols(ring[0])[...]
+        gr[c][here, :] = grad_cols(c)[...]
+    for copy in g_sent:
+        copy.start()
     for copy in h_sent:
         copy.start()
     lax.fori_loop(0, n_blk, place_kv, 0)
@@ -485,23 +497,45 @@
             p_scr[:, cs] = p.astype(BF16)
             ds_scr[:, cs] = (p * (d_p - delta_scr[grp, :, cs])).astype(BF16)
         at = pl.ds(row0, TILE)
-        dkv_ref[at, :e_dim] += dot(ds_scr[...], qd_scr[grp, 0])
-        dkv_ref[at, e_dim:] += dot(p_scr[...], qd_scr[grp, 1])
+        dkv_scr[at, :e_dim] += dot(ds_scr[...], qd_scr[grp, 0])
+        dkv_scr[at, e_dim:] += dot(p_scr[...], qd_scr[grp, 1])
         dqt_scr[grp] += dot_ta(k_t, ds_scr[...])
 
-    def sum_wo_start():
+    o_slab = n_cols // RING
+
+    def o_cols(pos):
+        return tok_scr.at[:, pl.ds(pl.multiple_of(pos * o_slab, o_slab), o_slab)]
+
+    def o_spread():
+        return [copy for c in COLOURS for copy in spread(rings[ORDERS[c][0]], o_cols, orr[c], n_tok, or_sems[c])]
+
+    def send_o():
         o_back.wait()
         place_heads(tok_scr, oh_scr)
-
-        def o_body(i, carry):
-            cols = pl.ds(pl.multiple_of(i * D_TILE, D_TILE), D_TILE)
-            xo[:, cols] = dot_ta(tok_scr[...], grad_ref[:, cols])
-            return carry
-
-        lax.fori_loop(0, d_model // D_TILE, o_body, 0)
-        stage(p_o, "rs_start0")
-
-    over_tiles(bwd_step, ((3, sum_wo_start), (9, lambda: stage(p_o, "rs_mid0"))))
+        for c in COLOURS:
+            pos = rings[ORDERS[c][0]][0]
+            orr[c][pl.ds(pl.multiple_of(pos * n_tok, n_tok), n_tok), :] = o_cols(pos)[...]
+        for copy in o_spread():
+            copy.start()
+
+    def slab_wo():
+        for copy in o_spread() + g_sent:
+            copy.wait_recv()
+        for c, red in enumerate((red0, red1, red2)):
+            for at in range(0, red.shape[1], 128):
+                red[:, at:at + 128] = dot_ta(orr[c][...], gr[c][:, at:at + 128])
+
+    over_tiles(bwd_step, ((3, send_o), (8, slab_wo)))
+
+    def place_dkv(blk, carry):
+        for c in COLOURS:
+            at, rb = rows_d[c]
+            dst = pl.ds(pl.multiple_of(place_in_order(blk, ORDERS[c]) * rb, 8), rb)
+            xs[c][dst, :] = dkv_scr[pl.ds(pl.multiple_of(blk * rows + at, 8), rb), :]
+        return carry
+
+    lax.fori_loop(0, n_blk, place_dkv, 0)
+    stage(p_d, "rs_start0")
 
     scale = e_dim ** -0.5
     half_dim = e_dim // 2
@@ -518,20 +552,46 @@
     h_outs = [pltpu.make_async_copy(hr[c], out, h_out.at[c]) for c, out in enumerate((ho0, ho1, ho2))]
     for copy in h_outs:
         copy.start()
-    oh_ref[...] = oh_scr[...]
-    stage(p_o, "rs_end0")
-    for part, out, lanes in zip(p_o, (red0, red1, red2), o_lanes):
+
+    tp = lax.axis_index("tp")
+    partner = (1 - tp, cp)
+    for at in range(0, d_model, D_TILE):
+        cols = slice(at, at + D_TILE)
+        res = dot(tok_scr[...], wo_ref[:, cols])
+        for b in range(n_groups):
+            part_scr[b, :, cols] = res[b * rows:(b + 1) * rows]
+
+    def swap(src, dst, i):
+        return pltpu.make_async_remote_copy(src_ref=src, dst_ref=dst, send_sem=swap_sems[0].at[i], recv_sem=swap_sems[1].at[i], device_id=partner, device_id_type=MESH)
+
+    swap_part = swap(part_scr.at[1 - tp], got_scr, 0)
+    swap_part.start()
+    stage(p_d, "rs_mid0")
+    swap_part.wait()
+    out_scr[tp] = (part_scr[tp] + got_scr[...]).astype(BF16)
+    swap_out = swap(out_scr.at[tp], out_scr.at[tp], 1)
+    swap_out.start()
+    dq_back.wait()
+
+    def put(src, dst):
+        copy = pltpu.make_async_copy(src, dst, h_out.at[len(h_outs)])
+        copy.start()
+        h_outs.append(copy)
+
+    put(dqh_scr, dqh_ref)
+    swap_out.wait()
+    put(out_scr, out_ref)
+    stage(p_d, "rs_end0")
+    for part, out in zip(p_d, (sl0, sl1, sl2)):
         slab, _, _, starts, *_ = part.place(0)
-        out[...] = xo[pl.ds(pl.multiple_of(starts[0], 8), slab), pl.ds(*lanes)]
-    dq_back.wait()
-    dqh_ref[...] = dqh_scr[...]
+        put(part.view(part.x, starts[0], slab), out)
     for part in p_kv:
-        part.drain(ag=range(3))
-    for part in p_o:
+        part.drain(ag=COLOURS)
+    for part in p_d:
         part.drain(rs=(0,))
     for kind in range(2):
         hand.drain(kind)
-    for copy in h_sent:
+    for copy in h_sent + g_sent + o_spread():
         copy.wait_send()
     for copy in h_outs:
         copy.wait()
@@ -547,15 +607,15 @@
     seq = n_blk * rows
     o_lanes = wide_lanes(d_model)
     slab = n_cols // RING
-    vmem = pl.BlockSpec(memory_space=pltpu.VMEM)
+    vmem, anyspace = pl.BlockSpec(memory_space=pltpu.VMEM), pl.BlockSpec(memory_space=pl.ANY)
     heads = (2, n_cols, e_dim)
     h_ring = (RING * n_tok, d_model // RING)
     work = n_cols * seq
     return pl.pallas_call(
         attn_kernel,
-        out_shape=(jax.ShapeDtypeStruct(heads, BF16), jax.ShapeDtypeStruct(heads, BF16), jax.ShapeDtypeStruct((seq, 2 * e_dim), F32)) + tuple(jax.ShapeDtypeStruct((slab, n), F32) for _, n in o_lanes) + (jax.ShapeDtypeStruct(h_ring, BF16),) * 3,
+        out_shape=(jax.ShapeDtypeStruct(heads, BF16), jax.ShapeDtypeStruct((2, rows, d_model), BF16)) + tuple(jax.ShapeDtypeStruct((n_blk // RING * rb, 2 * e_dim), F32) for _, rb in by_rows(rows, 8)) + tuple(jax.ShapeDtypeStruct((slab, n), F32) for _, n in o_lanes) + (jax.ShapeDtypeStruct(h_ring, BF16),) * 3,
         in_specs=[vmem] * 8,
-        out_specs=(vmem,) * 6 + (pl.BlockSpec(memory_space=pl.ANY),) * 3,
+        out_specs=(anyspace,) * 5 + (vmem,) * 3 + (anyspace,) * 3,
         scratch_shapes=[pltpu.VMEM((n_blk * rb, 2 * e_dim), BF16) for _, rb in by_rows(rows, 16)]
         + [
             pltpu.VMEM((seq, 2 * e_dim), BF16),
@@ -569,35 +629,41 @@
             pltpu.VMEM((2, 1, n_cols), F32),
             pltpu.VMEM((TILE, n_cols), BF16),
             pltpu.VMEM((TILE, n_cols), BF16),
-            pltpu.VMEM((n_cols, d_model), F32),
+            pltpu.VMEM((seq, 2 * e_dim), F32),
             pltpu.VMEM((n_tok, n_cols), BF16),
+            pltpu.VMEM((2, rows, d_model), F32),
+            pltpu.VMEM((rows, d_model), F32),
+            pltpu.VMEM((2, rows, d_model), BF16),
         ]
         + [pltpu.VMEM(heads, BF16)] * 4
-        + [pltpu.VMEM((3 * slab, lanes), F32) for _, lanes in o_lanes]
         + [pltpu.VMEM(h_ring, BF16)] * 3
+        + [pltpu.VMEM((RING * n_tok, lanes), BF16) for _, lanes in o_lanes]
+        + [pltpu.VMEM((RING * n_tok, slab), BF16)] * 3
+        + [pltpu.VMEM((n_blk * rb, 2 * e_dim), F32) for _, rb in by_rows(rows, 8)]
         + pair(30) * 6
-        + pair(3) * 3
+        + pair(3) * 9
         + pair(4)
-        + pair(2) * 2
-        + [pltpu.SemaphoreType.DMA((3,))],
-        compiler_params=pltpu.CompilerParams(collective_id=2, has_side_effects=True, vmem_limit_bytes=64000000),
+        + pair(2) * 3
+        + [pltpu.VMEM((slab_rows(rb)[0], 2 * e_dim), F32) for _, rb in by_rows(rows, 8)]
+        + [pltpu.SemaphoreType.DMA((8,))],
+        compiler_params=pltpu.CompilerParams(collective_id=2, has_side_effects=True, vmem_limit_bytes=VMEM_LIMIT),
         cost_estimate=pl.CostEstimate(flops=14 * work * e_dim, bytes_accessed=seq * e_dim * 12, transcendentals=2 * work),
         name="attention",
     )(key_loc, val_loc, q_home, hid, grad, w_out, cos_t, sin_t)
 
 
 GRAD_PLAN = (
-    "r.rs_start1", "d.rs_start0", "weights.q", "d.rs_mid0", "r.rs_mid1", "s.rs_start1", "d.rs_end0", "d.rs_start1",
-    "r.rs_end1", "s.rs_mid1", "d.rs_mid1", "r.rs_start2", "s.rs_end1", "d.rs_end1", "d.rs_start2", "s.rs_start2",
-    "r.rs_end2", "o.ag_start2", "d.rs_end2", "weights.prep", "weights.kv", "s.rs_end2", "q.ag_start2", "o.ag_end2",
-    "o.ag_start1", "weights.slab", "t.rs_start1", "q.ag_end2", "q.ag_start1", "t.rs_mid1", "o.ag_mid1", "t.rs_end1",
-    "t.rs_start2", "q.ag_mid1", "t.rs_end2", "k.ag_start2", "o.ag_end1", "o.ag_start0", "k.ag_end2", "q.ag_end1",
-    "k.ag_start1", "k.ag_mid1", "q.ag_start0", "k.ag_end1", "k.ag_start0", "o.ag_mid0", "k.ag_mid0", "q.ag_mid0",
-    "k.ag_end0", "o.ag_end0", "q.ag_end0",
+    "r.rs_start1", "d.rs_start1", "weights.q", "s.rs_start1", "d.rs_mid1", "r.rs_mid1", "s.rs_mid1", "d.rs_end1",
+    "d.rs_start2", "r.rs_end1", "r.rs_start2", "s.rs_end1", "s.rs_start2", "d.rs_end2", "weights.prep", "weights.kv",
+    "r.rs_end2", "s.rs_end2", "o.ag_start2", "q.ag_start2", "weights.slab", "t.rs_start1", "o.ag_end2",
+    "o.ag_start1", "t.rs_mid1", "q.ag_end2", "q.ag_start1", "t.rs_end1", "t.rs_start2", "o.ag_mid1", "q.ag_mid1",
+    "t.rs_end2", "k.ag_start2", "o.ag_end1", "o.ag_start0", "k.ag_end2", "k.ag_start1", "q.ag_end1", "q.ag_start0",
+    "k.ag_mid1", "o.ag_mid0", "k.ag_end1", "k.ag_start0", "q.ag_mid0", "k.ag_mid0", "k.ag_end0", "o.ag_end0",
+    "q.ag_end0",
 )
 
 
-def grad_kernel(dkv_ref, dqh_ref, red0, red1, red2, hi0, hi1, hi2, cos_ref, sin_ref, gq_ref, go_ref, gk_ref, gv_ref, dkd_ref, yq, yo, yk, yp, turn_scr, tok_scr, kvt_scr, kvr_scr, mine_scr, give_scr, got_scr, xk, *rest):
+def grad_kernel(sl0, sl1, sl2, dqh_ref, red0, red1, red2, hi0, hi1, hi2, cos_ref, sin_ref, gq_ref, go_ref, gk_ref, gv_ref, dkd_ref, yq, yo, yk, yp, turn_scr, tok_scr, kvt_scr, kvr_scr, mine_scr, give_scr, got_scr, xk, *rest):
     rest = list(rest)
 
     def grab(n):
@@ -613,33 +679,24 @@
     split = by_rows(rows, 8)
     tp, cp = lax.axis_index("tp"), lax.axis_index("cp")
     partner = (1 - tp, cp)
-    rings = [ring_of(axis) for axis in range(3)]
-    colours = range(3)
+    rings = [ring_of(axis) for axis in COLOURS]
 
     def shifted(c, n_rows):
         return 0 - rings[ORDERS[c][0]][0] * (n_rows // RING)
 
     xs, xos, xqs, hr, dqr = (grab(3) for _ in range(5))
-    sem_d, sem_q, sem_o, sem_g = ([grab(2) for _ in colours] for _ in range(4))
+    sem_d, sem_q, sem_o, sem_g = ([grab(2) for _ in COLOURS] for _ in range(4))
     sem_k, sem_kr = grab(2), grab(2)
-    p_d = [Part(rings, ORDERS[c], split[c][1], sem_d[c], x=xs[c], recv=grab(3), lanes=(0, lanes)) for c in colours]
-    p_s = [Part(rings, ORDERS[c], d_model // n_blk, sem_q[c], x=xqs[c], recv=[None] + grab(2), row0=shifted(c, d_model), lanes=(0, q_lanes[c][1])) for c in colours]
-    p_q = [Part(rings, ORDERS[c], d_model // n_blk, sem_q[c], y=yq, lanes=q_lanes[c]) for c in colours]
-    p_r = [Part(rings, ORDERS[c], n_cols // n_blk, sem_o[c], x=xos[c], recv=[None] + grab(2), row0=shifted(c, n_cols), lanes=(0, o_lanes[c][1])) for c in colours]
-    p_o = [Part(rings, ORDERS[c], n_cols // n_blk, sem_o[c], y=yo, lanes=o_lanes[c]) for c in colours]
+    p_d = [Part(rings, ORDERS[c], split[c][1], sem_d[c], x=xs[c], recv=[None] + grab(2), row0=shifted(c, n_blk * split[c][1]), lanes=(0, lanes)) for c in COLOURS]
+    p_s = [Part(rings, ORDERS[c], d_model // n_blk, sem_q[c], x=xqs[c], recv=[None] + grab(2), row0=shifted(c, d_model), lanes=(0, q_lanes[c][1])) for c in COLOURS]
+    p_q = [Part(rings, ORDERS[c], d_model // n_blk, sem_q[c], y=yq, lanes=q_lanes[c]) for c in COLOURS]
+    p_r = [Part(rings, ORDERS[c], n_cols // n_blk, sem_o[c], x=xos[c], recv=[None] + grab(2), row0=shifted(c, n_cols), lanes=(0, o_lanes[c][1])) for c in COLOURS]
+    p_o = [Part(rings, ORDERS[c], n_cols // n_blk, sem_o[c], y=yo, lanes=o_lanes[c]) for c in COLOURS]
     p_t = [Part(rings, ORDERS[2], d_model // n_blk, sem_k, x=xk, recv=[None] + grab(2), row0=shifted(2, d_model), lanes=(0, head_dim))]
     p_k = [Part(rings, ORDERS[2], d_model // n_blk, sem_k, y=yk, lanes=(0, head_dim))]
     in_sem, out_sem, swap_s, swap_r = rest
 
-    def load(blk, carry):
-        for c in range(3):
-            at, rb = split[c]
-            dst = xs[c].at[pl.ds(pl.multiple_of(place_in_order(blk, ORDERS[c]) * rb, 8), rb)]
-            pltpu.make_async_copy(dkv_ref.at[pl.ds(pl.multiple_of(blk * rows + at, 8), rb)], dst, in_sem.at[c]).start()
-        return carry
-
-    lax.fori_loop(0, n_blk, load, 0)
-    loads = [pltpu.make_async_copy(src, dst, in_sem.at[3 + i]) for i, (src, dst) in enumerate(zip((red0, red1, red2, hi0, hi1, hi2), xos + hr))]
+    loads = [pltpu.make_async_copy(src, dst, in_sem.at[i]) for i, (src, dst) in enumerate(zip((sl0, sl1, sl2, red0, red1, red2, hi0, hi1, hi2), xs + xos + hr))]
     for copy in loads:
         copy.start()
     place_heads(tok_scr, dqh_ref)
@@ -648,7 +705,7 @@
         return pl.ds(*q_lanes[c])
 
     dq_sent = []
-    for c in colours:
+    for c in COLOURS:
         ring = rings[ORDERS[c][0]]
         dqr[c][pl.ds(pl.multiple_of(ring[0] * n_tok, n_tok), n_tok), :] = tok_scr[:, tok_cols(c)]
         dq_sent += spread(ring, lambda pos, c=c: tok_scr.at[:, tok_cols(c)], dqr[c], n_tok, sem_g[c])
@@ -659,8 +716,6 @@
         copy.start()
     for copy in loads:
         copy.wait()
-    for c in colours:
-        pltpu.make_async_copy(dkv_ref.at[pl.ds(0, n_blk * split[c][1])], xs[c], in_sem.at[c]).wait()
     half_dim = head_dim // 2
     first = tp == 0
     swap_small = pltpu.make_async_remote_copy(src_ref=give_scr, dst_ref=got_scr, send_sem=swap_s.at[0], recv_sem=swap_r.at[0], device_id=partner, device_id_type=MESH)
@@ -692,7 +747,7 @@
     def weights_q():
         for copy in dq_sent:
             copy.wait_recv()
-        for c in colours:
+        for c in COLOURS:
             slab_term(xqs[c], hr[c], dqr[c])
 
     def new_dkv():
@@ -700,7 +755,7 @@
         return dkd_ref[:, :head_dim], dkd_ref[:, head_dim:]
 
     def weights_prep():
-        for c in range(3):
+        for c in COLOURS:
             at, rb = split[c]
             own = xs[c][pl.ds(pl.multiple_of(p_d[c].own_rows(), 8), rb), :]
             cos_tab, sin_tab = cos_ref[pl.ds(at, rb), :], sin_ref[pl.ds(at, rb), :]
@@ -769,17 +824,15 @@
     out_q.wait()
     for c, part in enumerate(p_o):
         pltpu.make_async_copy(part.view(yo, 0, n_cols), part.view(go_ref, 0, n_cols), out_sem.at[c]).wait()
-    for part in p_d:
-        part.drain(rs=range(3))
-    for part in p_s + p_r + p_t:
+    for part in p_d + p_s + p_r + p_t:
         part.drain(rs=(1, 2))
     for part in p_q + p_o + p_k:
-        part.drain(ag=range(3))
+        part.drain(ag=COLOURS)
     for copy in dq_sent + kv_sent:
         copy.wait_send()
 
 
-def grad_sums(dkv, dq_home, reds, h_rings, cos_tab, sin_tab, d_model):
+def grad_sums(slabs, dq_home, reds, h_rings, cos_tab, sin_tab, d_model):
     n_batch, n_rows, head_dim = dq_home.shape
     rows = cos_tab.shape[0]
     n_tok, n_cols = n_batch * rows, n_rows // rows * head_dim
@@ -801,11 +854,12 @@
     slab, ring_tok = d_model // RING, RING * n_tok
     scratch = [full(d_model, n_cols), full(n_cols, d_model), full(d_model, head_dim), full(d_model, head_dim), full(d_model * n_cols // head_dim, head_dim)]
     scratch += [half(n_tok, n_cols), half(n_tok, head_dim), half(ring_tok, head_dim), full(rows, lanes), half(rows, head_dim), half(rows, head_dim), full(slab, head_dim)]
-    scratch += [full(n_blk * rb, lanes) for _, rb in split]
+    scratch += [full(n_blk // RING * rb, lanes) for _, rb in split]
     scratch += [full(n_cols // RING, w) for _, w in o_lanes] + [full(slab, w) for _, w in q_lanes]
     scratch += [half(ring_tok, slab)] * 3 + [half(ring_tok, w) for _, w in q_lanes]
     scratch += pair(30) * 9 + pair(3) * 3 + pair(30) + pair(3)
-    scratch += [full(n, lanes) for _, rb in split for n in slab_rows(rb)]
+    for _, rb in split:
+        scratch += later(rb, lanes)
     for _, w in q_lanes:
         scratch += later(d_model // n_blk, w)
     for _, w in o_lanes:
@@ -821,13 +875,13 @@
             jax.ShapeDtypeStruct((d_model, head_dim), F32),
             jax.ShapeDtypeStruct((rows, lanes), BF16),
         ),
-        in_specs=[anyspace, vmem] + [anyspace] * 6 + [vmem] * 2,
+        in_specs=[anyspace] * 3 + [vmem] + [anyspace] * 6 + [vmem] * 2,
         out_specs=(anyspace,) * 4 + (vmem,),
         scratch_shapes=scratch,
-        compiler_params=pltpu.CompilerParams(collective_id=3, has_side_effects=True, vmem_limit_bytes=67000000),
+        compiler_params=pltpu.CompilerParams(collective_id=3, has_side_effects=True, vmem_limit_bytes=VMEM_LIMIT),
         cost_estimate=pl.CostEstimate(flops=n_tok * d_model * n_cols * 160, bytes_accessed=40 << 20, transcendentals=0),
         name="grad_sums",
-    )(dkv, dq_home, *reds, *h_rings, cos_tab, sin_tab)
+    )(*slabs, dq_home, *reds, *h_rings, cos_tab, sin_tab)
 
 
 def solution(mesh):
@@ -866,11 +920,9 @@
         d_model = hidden.shape[-1]
         hid, grad = hidden.reshape(-1, d_model), grad_out.reshape(-1, d_model)
         tabs_t = [jnp.stack(pair_t) for pair_t in ((cos_tab.T, cos_mir.T), (sin_tab.T, sin_mir.T))]
-        o_home, dq_home, dkv, *more = attention(key_loc, val_loc, q_home, hid, grad, w_out.reshape(-1, d_model), *tabs_t)
-        attn_heads = o_home.reshape(2, n_local, block_len, head_dim)
+        dq_home, attn_out, *more = attention(key_loc, val_loc, q_home, hid, grad, w_out.reshape(-1, d_model), *tabs_t)
         dq_pre = dq_home.reshape(2, n_local, block_len, head_dim)
-        attn_out = sum_over_tp(jnp.einsum("cirf,ife->cre", attn_heads, w_out, preferred_element_type=F32))
-        grad_q, grad_o, d_w_key, d_w_value, dkv_new = grad_sums(dkv, dq_home, more[:3], more[3:], cos_tab, sin_tab, d_model)
+        grad_q, grad_o, d_w_key, d_w_value, dkv_new = grad_sums(more[:3], dq_home, more[3:6], more[6:], cos_tab, sin_tab, d_model)
         d_w_query = grad_q.reshape(w_query.shape)
         d_w_out = grad_o.reshape(w_out.shape)
         dk_pre, dv_pre = dkv_new[:, :head_dim], dkv_new[:, head_dim:]

time: 327 us -> 319 us (0.976)
  matrix products: 18 us -> 14.5 us
    pallas_call x1, Pallas kernels: 145 us -> 122 us  [grad_sums(): pl.pallas_call(grad_kernel, out_shape=(jax.ShapeDtypeStruct((d_model * n_...]
    pallas_call x1, Pallas kernels: 136 us -> 155 us  [attention(): pl.pallas_call(attn_kernel, out_shape=(jax.ShapeDtypeStruct(heads, BF16),...]
    dot_general x1 -> x0, matrix products: 3.43 us -> none  [local_program(): jnp.einsum('cirf,ife->cre', attn_heads, w_out, preferred_element_type=F32)]
    unnamed x26 -> x23, local copies, waits for them, and re-layouts: 14.3 us -> 15.4 us
  transfers between devices with their start and end apart: 4 -> 2, of which waited for: 2 -> 1; matrix products, arithmetic and copies ran while one was open for 3% -> 0% of each run, Pallas kernels for 44% -> 38%
where the time goes in v5:
time: 319 us
  Pallas kernels  278 us (87%)
  local copies, waits for them, and re-layouts  17.3 us (5%)
  matrix products  14.5 us (5%)
  other arithmetic  4.41 us (1%)
    pallas_call x1, Pallas kernels, attention(): pl.pallas_call(attn_kernel, out_shape=(jax.ShapeDtypeStruct(heads, BF16),...  155 us
    pallas_call x1, Pallas kernels, grad_sums(): pl.pallas_call(grad_kernel, out_shape=(jax.ShapeDtypeStruct((d_model * n_...  122 us
    unnamed x23, local copies, waits for them, and re-layouts  15.4 us
    dot_general x4, matrix products, dot(): return jnp.dot(a, b, preferred_element_type=F32)  6.95 us
  transfers between devices with their start and end apart: 2, of which 1 were waited for; matrix products, arithmetic and copies ran while one was open for 0% of the time, Pallas kernels for 38%

profile of v5, /device:TPU:1, one launch (start us, length us, event | category | flops | bytes accessed | tf_op | source)
XLA Modules:
  0.0 319.1 jit_solution(13537030288557212191)
XLA Ops:
  0.7 1.5 fusion.16
  2.2 0.3 multiply_cosine_fusion
  2.5 0.0 copy-start.5
  2.5 0.0 copy-start.6
  2.5 0.1 copy.24
  2.6 0.1 copy.25
  2.7 3.9 %fusion.8 = f32[2,8,128,128]{2,3,0,1:T(8,128)S(1)} fusion(bf16[2048,8,128,1]{2,1,0,3:T(8,128)(2,1)} %bitcast.52, bf16[2,128,2048]{2,1,0:T(8,128)(2,1)} %param.6), kind=kOutput, calls=%fused_computation.7 | convolution fusion | flops 1073741824 | bytes 6291456 | tf_op jit(solution)/shard_map/bsd,dhe->bhse/dot_general | solution.py:917
  6.5 0.0 copy-done.5
  6.5 0.0 copy-done.6
  6.5 0.0 copy-start.1
  6.6 0.1 multiply_subtract_fusion
  6.7 0.3 copy.26
  7.1 0.3 copy.27
  7.4 0.3 multiply_sine_fusion.2
  7.7 0.0 copy-done.1
  7.7 1.9 convolution_convert_fusion.v_ref
  9.7 1.1 fusion.11.q_ref
  10.8 0.7 pad_maximum_fusion.3.k_ref
  11.5 0.7 pad_maximum_fusion.1
  12.2 155.1 %attention.1 = (bf16[2,1024,128]{2,1,0:T(8,128)(2,1)}, bf16[2,128,2048]{2,1,0:T(8,128)(2,1)}, f32[768,256]{1,0:T(8,128)}, f32[640,256]{1,0:T(8,128)}, f32[640,25...) custom-call(bf16[128,128]{1,0:T(8,128)(2,1)} %pad_maximum_fusion.3.k, ...), custom_call_target="tpu_custom_call" | custom-call | flops 15032385536 | bytes 12582912 | tf_op jit(solution)/shard_map/attention/pallas_call | solution.py:614
  167.3 3.7 %fusion.5 = f32[2,128,2048]{2,1,0:T(8,128)S(1)} fusion(bf16[2,8,128,128]{3,2,1,0:T(8,128)(2,1)} %bitcast.54, bf16[2048,8,128]{2,1,0:T(8,128)(2,1)} %param.8), kind=kOutput, calls=%fused_computation.5 | convolution fusion | flops 1073741824 | bytes 6815744 | tf_op jit(solution)/shard_map/cirf,eif->cre/dot_general | solution.py:930
  171.0 0.0 copy-start
  171.0 1.3 copy-done
  172.3 1.0 dynamic-slice_bitcast_fusion
  173.3 1.0 collective-permute-start
  174.3 122.5 %grad_sums.1 = (f32[16384,128]{1,0:T(8,128)}, f32[1024,2048]{1,0:T(8,128)}, f32[2048,128]{1,0:T(8,128)}, f32[2048,128]{1,0:T(8,128)}, bf16[128,256]{1,0:T(8,128)(2,1)}) custom-call(f32[768,256]{1,0:T(8,128)} %get-tuple-element.24.sl0, f32[640,256]{1,0:T(8,128)} %get-tuple-element.25.sl1, f32[640,256]{1,0:T(8,128)} %get-tuple-element.26.sl2, ...), custom_call_target="tpu_custom_call" | custom-call | flops 85899345920 | bytes 41943040 | tf_op jit(solution)/shard_map/grad_sums/pallas_call | solution.py:869
  296.8 1.4 fusion.23
  298.2 0.0 copy-start.2
  298.2 0.0 collective-permute-done
  298.2 2.2 fusion.13
  300.4 2.0 collective-permute-start.1
  302.3 1.5 collective-permute-done.1
  303.9 0.1 select_bitcast_fusion.1
  303.9 1.1 pad_maximum_fusion
  305.0 0.0 copy-done.2
  305.0 0.0 slice-start
  305.0 1.0 copy.49
  306.0 0.0 copy-start.4
  306.0 0.0 copy-start.3
  306.0 0.0 slice-start.1
  306.0 7.8 %copy.50 = f32[2048,8,128]{2,1,0:T(8,128)} copy(f32[2048,8,128]{2,1,0:T(8,128)} %bitcast.47) | data formatting | bytes 16777216
  313.7 0.0 copy-done.4
  313.7 1.0 copy.51
  314.7 0.0 copy-done.3
  314.7 1.0 copy.52
  315.7 0.0 slice-done
  315.7 0.0 slice-done.1
  315.7 3.4 %copy.53 = f32[8,128,2048]{2,1,0:T(8,128)} copy(f32[8,128,2048]{2,1,0:T(8,128)S(1)} %bitcast.46) | data formatting | bytes 16777216
  (4 shorter events, 0.0 us)
Async XLA Ops:
  2.5 4.0 %copy-start.5 = (f32[128,64]{1,0:T(8,128)}, f32[128,64]{1,0:T(8,128)S(1)}, u32[]{:S(2)}) copy-start(f32[128,64]{1,0:T(8,128)S(1)} %get-tuple-element.48.cos_ref) | copy-start | bytes 98308
  2.5 4.0 %copy-start.6 = (f32[128,64]{1,0:T(8,128)}, f32[128,64]{1,0:T(8,128)S(1)}, u32[]{:S(2)}) copy-start(f32[128,64]{1,0:T(8,128)S(1)} %get-tuple-element.49.sin_ref) | copy-start | bytes 98308
  6.5 1.2 copy-start.1
  171.0 1.3 copy-start
  173.3 124.8 %collective-permute-start = (f32[128,2048]{1,0:T(8,128)}, f32[128,2048]{1,0:T(8,128)}, u32[]{:S(2)}, u32[]{:S(2)}) collective-permute-start(f32[128,2048]{1,0:T(8,128)} %dynamic-slice_bitcast_fusion), channel_id=1, source_target_pairs={{0,64},{64,0},{1,65},{65,1},{2,66},{66,2},{3,67},{67,3},{4,68},{68... | collective-permute-start | bytes 3145736 | tf_op jit(solution)/shard_map/ppermute | solution.py:906
  298.2 6.8 %copy-start.2 = (bf16[2,128,2048]{2,1,0:T(8,128)(2,1)S(1)}, bf16[2,128,2048]{2,1,0:T(8,128)(2,1)}, u32[]{:S(2)}) copy-start(bf16[2,128,2048]{2,1,0:T(8,128)(2,1)} %get-tuple-element.62) | copy-start | bytes 3145732
  300.4 3.5 %collective-permute-start.1 = (bf16[128,2048]{1,0:T(8,128)(2,1)S(1)}, bf16[128,2048]{1,0:T(8,128)(2,1)S(1)}, u32[]{:S(2)}, u32[]{:S(2)}) collective-permute-start(bf16[128,2048]{1,0:T(8,128)(2,1)S(1)} %fusion.13), channel_id=1, source_target_pairs={{0,64},{64,0},{1,65},{65,1},{2,66},{66,2},{3,67},{67,3},{4,68},{68... | collective-permute-start | bytes 1572872 | tf_op jit(solution)/shard_map/ppermute | solution.py:910
  305.0 10.7 %slice-start = ((s8[8388608]{0:T(1024)(128)(4,1)}), s8[4194304]{0:T(1024)(128)(4,1)S(1)}, s32[]{:S(2)}) async-start(s8[8388608]{0:T(1024)(128)(4,1)} %bitcast.44), calls=%async_computation | async-start | bytes 8388608
  306.0 7.8 %copy-start.4 = (f32[2048,128]{1,0:T(8,128)S(1)}, f32[2048,128]{1,0:T(8,128)}, u32[]{:S(2)}) copy-start(f32[2048,128]{1,0:T(8,128)} %get-tuple-element.65) | copy-start | bytes 3145732
  306.0 8.7 %copy-start.3 = (f32[2048,128]{1,0:T(8,128)S(1)}, f32[2048,128]{1,0:T(8,128)}, u32[]{:S(2)}) copy-start(f32[2048,128]{1,0:T(8,128)} %get-tuple-element.66) | copy-start | bytes 3145732
  306.0 9.7 %slice-start.1 = ((s8[8388608]{0:T(1024)(128)(4,1)}), s8[4194304]{0:T(1024)(128)(4,1)S(1)}, s32[]{:S(2)}) async-start(s8[8388608]{0:T(1024)(128)(4,1)} %bitcast.44), calls=%async_computation.1 | async-start | bytes 8388608

commit v6 on v5

--- a/solution.py
+++ b/solution.py
@@ -51,6 +51,7 @@
 AXIS_STRIDE = (RING * RING, RING, 1)
 ORDERS = ((0, 1, 2), (1, 2, 0), (2, 0, 1))
 MESH = pl.DeviceIdType.MESH
+HOPS = 12
 
 
 def ring_of(axis):
@@ -138,16 +139,18 @@
                 (lft, h0, 2 * slab, left),
                 (rgt, h0, slab, right),
                 (lft + h0, h1, 2 * slab + h0, left),
-                (own, slab, 0, right),
-                (own, slab, 0, left),
+                (own, h0, 0, right),
+                (own + h0, h1, 0, left),
                 (lft, h0, 0, right),
                 (rgt + h0, h1, 0, left),
+                (own + h0, h1, 0, right),
+                (own, h0, 0, left),
             )[i]
         if i < 6:
             src, dst = self.view(self.x, start, n_rows), self.recv[phase].at[pl.ds(at, n_rows)]
         else:
             src = dst = self.view(self.y, start, n_rows)
-        return remote(src, dst, self.sems, 10 * phase + i, device)
+        return remote(src, dst, self.sems, HOPS * phase + i, device)
 
     def rs_start(self, phase):
         for i in (0, 2, 3) if phase >= self.direct else range(4):
@@ -176,7 +179,7 @@
         add_rows(self.x, own, terms, slab, self.lanes)
 
     def ag_start(self, phase):
-        for i in (6, 7, 8) if phase >= self.direct else (6, 7):
+        for i in (6, 7, 8) if phase >= self.direct else (6, 7, 10, 11):
             self.hop(phase, i).start()
 
     def ag_mid(self, phase):
@@ -186,6 +189,8 @@
         self.hop(phase, 8).start()
         self.hop(phase, 7).wait_recv()
         self.hop(phase, 9).start()
+        self.hop(phase, 10).wait_recv()
+        self.hop(phase, 11).wait_recv()
 
     def ag_end(self, phase):
         for i in (6, 7, 8) if phase >= self.direct else (8, 9):
@@ -199,7 +204,7 @@
             for i in (0, 2, 3) if phase >= self.direct else range(6):
                 self.hop(phase, i).wait_send()
         for phase in ag:
-            for i in (6, 7, 8) if phase >= self.direct else range(6, 10):
+            for i in (6, 7, 8) if phase >= self.direct else range(6, HOPS):
                 self.hop(phase, i).wait_send()
 
 
@@ -353,7 +358,8 @@
         return [rest.pop(0) for _ in range(n)]
 
     hr, gr, orr, xs = (grab(3) for _ in range(4))
-    k_sems, d_sems, h_sems, g_sems, or_sems = ([grab(2) for _ in COLOURS] for _ in range(5))
+    k_sems, d_sems, r_sems, h_sems, g_sems, or_sems = ([grab(2) for _ in COLOURS] for _ in range(6))
+    red_scr = grab(3)
     hand_sems, oh_sems, dqh_sems, swap_sems = (grab(2) for _ in range(4))
     n_groups, _, n_cols, e_dim = qd_scr.shape
     rows = k_ref.shape[0]
@@ -369,6 +375,8 @@
     p_kv = [Part(rings, ORDERS[c], split[c][1], k_sems[c], y=ys[c], lanes=(0, 2 * e_dim), align=16, direct=1) for c in COLOURS]
     rows_d = by_rows(rows, 8)
     p_d = [Part(rings, ORDERS[c], rows_d[c][1], d_sems[c], x=xs[c], recv=grab(1), lanes=(0, 2 * e_dim)) for c in COLOURS]
+    first_rows = [0 - rings[order[0]][0] * (n_cols // RING) for order in ORDERS]
+    p_r = [Part(rings, ORDERS[c], n_cols // n_blk, r_sems[c], x=red_scr[c], recv=[None] + grab(2), row0=first_rows[c], lanes=(0, o_lanes[c][1])) for c in COLOURS]
     h_out, = rest
     hand = Handout((q_ref, do_home), qd_scr, hand_sems)
     o_back = Return(o_scr, oh_scr, oh_sems)
@@ -521,11 +529,16 @@
     def slab_wo():
         for copy in o_spread() + g_sent:
             copy.wait_recv()
-        for c, red in enumerate((red0, red1, red2)):
+        for c, red in enumerate(red_scr):
             for at in range(0, red.shape[1], 128):
                 red[:, at:at + 128] = dot_ta(orr[c][...], gr[c][:, at:at + 128])
-
-    over_tiles(bwd_step, ((3, send_o), (8, slab_wo)))
+        stage(p_r, "rs_start1")
+
+    def step_wo():
+        stage(p_r, "rs_end1")
+        stage(p_r, "rs_start2")
+
+    over_tiles(bwd_step, ((3, send_o), (7, slab_wo), (10, lambda: stage(p_r, "rs_mid1")), (13, step_wo)))
 
     def place_dkv(blk, carry):
         for c in COLOURS:
@@ -536,6 +549,9 @@
 
     lax.fori_loop(0, n_blk, place_dkv, 0)
     stage(p_d, "rs_start0")
+    stage(p_r, "rs_end2")
+    for part, out in zip(p_r, (red0, red1, red2)):
+        out[...] = part.x[pl.ds(pl.multiple_of(part.own_rows(), 8), part.rb), :]
 
     scale = e_dim ** -0.5
     half_dim = e_dim // 2
@@ -589,6 +605,8 @@
         part.drain(ag=COLOURS)
     for part in p_d:
         part.drain(rs=(0,))
+    for part in p_r:
+        part.drain(rs=(1, 2))
     for kind in range(2):
         hand.drain(kind)
     for copy in h_sent + g_sent + o_spread():
@@ -613,7 +631,7 @@
     work = n_cols * seq
     return pl.pallas_call(
         attn_kernel,
-        out_shape=(jax.ShapeDtypeStruct(heads, BF16), jax.ShapeDtypeStruct((2, rows, d_model), BF16)) + tuple(jax.ShapeDtypeStruct((n_blk // RING * rb, 2 * e_dim), F32) for _, rb in by_rows(rows, 8)) + tuple(jax.ShapeDtypeStruct((slab, n), F32) for _, n in o_lanes) + (jax.ShapeDtypeStruct(h_ring, BF16),) * 3,
+        out_shape=(jax.ShapeDtypeStruct(heads, BF16), jax.ShapeDtypeStruct((2, rows, d_model), BF16)) + tuple(jax.ShapeDtypeStruct((n_blk // RING * rb, 2 * e_dim), F32) for _, rb in by_rows(rows, 8)) + tuple(jax.ShapeDtypeStruct((n_cols // n_blk, n), F32) for _, n in o_lanes) + (jax.ShapeDtypeStruct(h_ring, BF16),) * 3,
         in_specs=[vmem] * 8,
         out_specs=(anyspace,) * 5 + (vmem,) * 3 + (anyspace,) * 3,
         scratch_shapes=[pltpu.VMEM((n_blk * rb, 2 * e_dim), BF16) for _, rb in by_rows(rows, 16)]
@@ -640,11 +658,13 @@
         + [pltpu.VMEM((RING * n_tok, lanes), BF16) for _, lanes in o_lanes]
         + [pltpu.VMEM((RING * n_tok, slab), BF16)] * 3
         + [pltpu.VMEM((n_blk * rb, 2 * e_dim), F32) for _, rb in by_rows(rows, 8)]
-        + pair(30) * 6
+        + pair(3 * HOPS) * 9
         + pair(3) * 9
+        + [pltpu.VMEM((slab, lanes), F32) for _, lanes in o_lanes]
         + pair(4)
         + pair(2) * 3
         + [pltpu.VMEM((slab_rows(rb)[0], 2 * e_dim), F32) for _, rb in by_rows(rows, 8)]
+        + [pltpu.VMEM((n, lanes), F32) for _, lanes in o_lanes for n in slab_rows(n_cols // n_blk)[1:]]
         + [pltpu.SemaphoreType.DMA((8,))],
         compiler_params=pltpu.CompilerParams(collective_id=2, has_side_effects=True, vmem_limit_bytes=VMEM_LIMIT),
         cost_estimate=pl.CostEstimate(flops=14 * work * e_dim, bytes_accessed=seq * e_dim * 12, transcendentals=2 * work),
@@ -653,13 +673,12 @@
 
 
 GRAD_PLAN = (
-    "r.rs_start1", "d.rs_start1", "weights.q", "s.rs_start1", "d.rs_mid1", "r.rs_mid1", "s.rs_mid1", "d.rs_end1",
-    "d.rs_start2", "r.rs_end1", "r.rs_start2", "s.rs_end1", "s.rs_start2", "d.rs_end2", "weights.prep", "weights.kv",
-    "r.rs_end2", "s.rs_end2", "o.ag_start2", "q.ag_start2", "weights.slab", "t.rs_start1", "o.ag_end2",
-    "o.ag_start1", "t.rs_mid1", "q.ag_end2", "q.ag_start1", "t.rs_end1", "t.rs_start2", "o.ag_mid1", "q.ag_mid1",
-    "t.rs_end2", "k.ag_start2", "o.ag_end1", "o.ag_start0", "k.ag_end2", "k.ag_start1", "q.ag_end1", "q.ag_start0",
-    "k.ag_mid1", "o.ag_mid0", "k.ag_end1", "k.ag_start0", "q.ag_mid0", "k.ag_mid0", "k.ag_end0", "o.ag_end0",
-    "q.ag_end0",
+    "o.ag_start2", "d.rs_start1", "o.ag_end2", "o.ag_start1", "weights.q", "d.rs_mid1", "o.ag_mid1", "d.rs_end1",
+    "d.rs_start2", "s.rs_start1", "d.rs_end2", "o.ag_end1", "weights.prep", "s.rs_mid1", "weights.kv", "o.ag_start0",
+    "weights.slab", "t.rs_start1", "s.rs_end1", "t.rs_mid1", "s.rs_start2", "o.ag_mid0", "s.rs_end2", "t.rs_end1",
+    "q.ag_start2", "t.rs_start2", "t.rs_end2", "k.ag_start2", "q.ag_end2", "q.ag_start1", "k.ag_end2", "k.ag_start1",
+    "q.ag_mid1", "k.ag_mid1", "q.ag_end1", "q.ag_start0", "k.ag_end1", "k.ag_start0", "o.ag_end0", "k.ag_mid0",
+    "q.ag_mid0", "k.ag_end0", "q.ag_end0",
 )
 
 
@@ -684,19 +703,18 @@
     def shifted(c, n_rows):
         return 0 - rings[ORDERS[c][0]][0] * (n_rows // RING)
 
-    xs, xos, xqs, hr, dqr = (grab(3) for _ in range(5))
+    xs, xqs, hr, dqr = (grab(3) for _ in range(4))
     sem_d, sem_q, sem_o, sem_g = ([grab(2) for _ in COLOURS] for _ in range(4))
     sem_k, sem_kr = grab(2), grab(2)
     p_d = [Part(rings, ORDERS[c], split[c][1], sem_d[c], x=xs[c], recv=[None] + grab(2), row0=shifted(c, n_blk * split[c][1]), lanes=(0, lanes)) for c in COLOURS]
     p_s = [Part(rings, ORDERS[c], d_model // n_blk, sem_q[c], x=xqs[c], recv=[None] + grab(2), row0=shifted(c, d_model), lanes=(0, q_lanes[c][1])) for c in COLOURS]
     p_q = [Part(rings, ORDERS[c], d_model // n_blk, sem_q[c], y=yq, lanes=q_lanes[c]) for c in COLOURS]
-    p_r = [Part(rings, ORDERS[c], n_cols // n_blk, sem_o[c], x=xos[c], recv=[None] + grab(2), row0=shifted(c, n_cols), lanes=(0, o_lanes[c][1])) for c in COLOURS]
     p_o = [Part(rings, ORDERS[c], n_cols // n_blk, sem_o[c], y=yo, lanes=o_lanes[c]) for c in COLOURS]
     p_t = [Part(rings, ORDERS[2], d_model // n_blk, sem_k, x=xk, recv=[None] + grab(2), row0=shifted(2, d_model), lanes=(0, head_dim))]
     p_k = [Part(rings, ORDERS[2], d_model // n_blk, sem_k, y=yk, lanes=(0, head_dim))]
     in_sem, out_sem, swap_s, swap_r = rest
 
-    loads = [pltpu.make_async_copy(src, dst, in_sem.at[i]) for i, (src, dst) in enumerate(zip((sl0, sl1, sl2, red0, red1, red2, hi0, hi1, hi2), xs + xos + hr))]
+    loads = [pltpu.make_async_copy(src, dst, in_sem.at[i]) for i, (src, dst) in enumerate(zip((sl0, sl1, sl2, hi0, hi1, hi2), xs + hr))]
     for copy in loads:
         copy.start()
     place_heads(tok_scr, dqh_ref)
@@ -704,6 +722,8 @@
     def tok_cols(c):
         return pl.ds(*q_lanes[c])
 
+    for part, red in zip(p_o, (red0, red1, red2)):
+        part.y[pl.ds(pl.multiple_of(part.own_rows(), 8), part.rb), pl.ds(*part.lanes)] = red[...]
     dq_sent = []
     for c in COLOURS:
         ring = rings[ORDERS[c][0]]
@@ -780,13 +800,12 @@
             copy.wait_recv()
         slab_term(xk, hr[2], kvr_scr)
 
-    groups = {"d": p_d, "s": p_s, "q": p_q, "r": p_r, "o": p_o, "t": p_t, "k": p_k}
+    groups = {"d": p_d, "s": p_s, "q": p_q, "o": p_o, "t": p_t, "k": p_k}
     after = {
         "weights.q": weights_q,
         "weights.prep": weights_prep,
         "weights.kv": weights_kv,
         "weights.slab": weights_slab,
-        "r.rs_end2": lambda: own_block(p_o, p_r),
         "s.rs_end2": lambda: own_block(p_q, p_s),
         "t.rs_end2": lambda: own_block(p_k, p_t),
         "o.ag_mid0": lambda: put_o((0, 1, 3)),
@@ -824,7 +843,7 @@
     out_q.wait()
     for c, part in enumerate(p_o):
         pltpu.make_async_copy(part.view(yo, 0, n_cols), part.view(go_ref, 0, n_cols), out_sem.at[c]).wait()
-    for part in p_d + p_s + p_r + p_t:
+    for part in p_d + p_s + p_t:
         part.drain(rs=(1, 2))
     for part in p_q + p_o + p_k:
         part.drain(ag=COLOURS)
@@ -838,7 +857,7 @@
     n_tok, n_cols = n_batch * rows, n_rows // rows * head_dim
     n_blk = RING ** 3
     lanes = 2 * head_dim
-    q_lanes, o_lanes = thirds(n_cols // head_dim, head_dim), wide_lanes(d_model)
+    q_lanes = thirds(n_cols // head_dim, head_dim)
     split = by_rows(rows, 8)
     vmem, anyspace = pl.BlockSpec(memory_space=pltpu.VMEM), pl.BlockSpec(memory_space=pl.ANY)
 
@@ -855,17 +874,15 @@
     scratch = [full(d_model, n_cols), full(n_cols, d_model), full(d_model, head_dim), full(d_model, head_dim), full(d_model * n_cols // head_dim, head_dim)]
     scratch += [half(n_tok, n_cols), half(n_tok, head_dim), half(ring_tok, head_dim), full(rows, lanes), half(rows, head_dim), half(rows, head_dim), full(slab, head_dim)]
     scratch += [full(n_blk // RING * rb, lanes) for _, rb in split]
-    scratch += [full(n_cols // RING, w) for _, w in o_lanes] + [full(slab, w) for _, w in q_lanes]
+    scratch += [full(slab, w) for _, w in q_lanes]
     scratch += [half(ring_tok, slab)] * 3 + [half(ring_tok, w) for _, w in q_lanes]
-    scratch += pair(30) * 9 + pair(3) * 3 + pair(30) + pair(3)
+    scratch += pair(3 * HOPS) * 9 + pair(3) * 3 + pair(3 * HOPS) + pair(3)
     for _, rb in split:
         scratch += later(rb, lanes)
     for _, w in q_lanes:
         scratch += later(d_model // n_blk, w)
-    for _, w in o_lanes:
-        scratch += later(n_cols // n_blk, w)
     scratch += later(d_model // n_blk, head_dim)
-    scratch += [pltpu.SemaphoreType.DMA((9,)), pltpu.SemaphoreType.DMA((6,))] + pair(2)
+    scratch += [pltpu.SemaphoreType.DMA((6,)), pltpu.SemaphoreType.DMA((6,))] + pair(2)
     return pl.pallas_call(
         grad_kernel,
         out_shape=(
@@ -875,7 +892,7 @@
             jax.ShapeDtypeStruct((d_model, head_dim), F32),
             jax.ShapeDtypeStruct((rows, lanes), BF16),
         ),
-        in_specs=[anyspace] * 3 + [vmem] + [anyspace] * 6 + [vmem] * 2,
+        in_specs=[anyspace] * 3 + [vmem] * 4 + [anyspace] * 3 + [vmem] * 2,
         out_specs=(anyspace,) * 4 + (vmem,),
         scratch_shapes=scratch,
         compiler_params=pltpu.CompilerParams(collective_id=3, has_side_effects=True, vmem_limit_bytes=VMEM_LIMIT),

time: 319 us -> 320 us (level)
  starting transfers between devices: 2.94 us -> 6.9 us
    pallas_call x1, Pallas kernels: 122 us -> 110 us  [grad_sums(): pl.pallas_call(grad_kernel, out_shape=(jax.ShapeDtypeStruct((d_model * n_...]
    pallas_call x1, Pallas kernels: 155 us -> 164 us  [attention(): pl.pallas_call(attn_kernel, out_shape=(jax.ShapeDtypeStruct(heads, BF16),...]
    ppermute x1, starting transfers between devices: 1.97 us -> 6.89 us  [sum_over_tp(): other = lax.ppermute(mine, 'tp', partner)]
  transfers between devices with their start and end apart: 2 -> 2, of which waited for: 1 -> 1; matrix products, arithmetic and copies ran while one was open for 0% -> 0% of each run, Pallas kernels for 38% -> 34%
where the time goes in v6:
time: 320 us
  Pallas kernels  275 us (86%)
  local copies, waits for them, and re-layouts  17.3 us (5%)
  matrix products  14.5 us (5%)
  starting transfers between devices  6.9 us (2%)
  other arithmetic  4.41 us (1%)
    pallas_call x1, Pallas kernels, attention(): pl.pallas_call(attn_kernel, out_shape=(jax.ShapeDtypeStruct(heads, BF16),...  164 us
    pallas_call x1, Pallas kernels, grad_sums(): pl.pallas_call(grad_kernel, out_shape=(jax.ShapeDtypeStruct((d_model * n_...  110 us
    unnamed x23, local copies, waits for them, and re-layouts  15.4 us
    dot_general x4, matrix products, dot(): return jnp.dot(a, b, preferred_element_type=F32)  6.96 us
    ppermute x1, starting transfers between devices, sum_over_tp(): other = lax.ppermute(mine, 'tp', partner)  6.89 us
  transfers between devices with their start and end apart: 2, of which 1 were waited for; matrix products, arithmetic and copies ran while one was open for 0% of the time, Pallas kernels for 34%

profile of v6, /device:TPU:1, one launch (start us, length us, event | category | flops | bytes accessed | tf_op | source)
XLA Modules:
  0.0 320.0 jit_solution(4436830048603139575)
XLA Ops:
  0.7 1.5 fusion.16
  2.2 0.3 multiply_cosine_fusion
  2.5 0.0 copy-start.5
  2.5 0.0 copy-start.6
  2.5 0.1 copy.24
  2.6 0.1 copy.25
  2.7 3.9 %fusion.8 = f32[2,8,128,128]{2,3,0,1:T(8,128)S(1)} fusion(bf16[2048,8,128,1]{2,1,0,3:T(8,128)(2,1)} %bitcast.52, bf16[2,128,2048]{2,1,0:T(8,128)(2,1)} %param.6), kind=kOutput, calls=%fused_computation.7 | convolution fusion | flops 1073741824 | bytes 6291456 | tf_op jit(solution)/shard_map/bsd,dhe->bhse/dot_general | solution.py:934
  6.5 0.0 copy-done.5
  6.5 0.0 copy-done.6
  6.5 0.0 copy-start.1
  6.6 0.1 multiply_subtract_fusion
  6.7 0.3 copy.26
  7.1 0.3 copy.27
  7.4 0.3 multiply_sine_fusion.2
  7.7 0.0 copy-done.1
  7.7 1.9 convolution_convert_fusion.v_ref
  9.7 1.1 fusion.11.q_ref
  10.8 0.7 pad_maximum_fusion.3.k_ref
  11.5 0.7 pad_maximum_fusion.1
  12.2 164.2 %attention.1 = (bf16[2,1024,128]{2,1,0:T(8,128)(2,1)}, bf16[2,128,2048]{2,1,0:T(8,128)(2,1)}, f32[768,256]{1,0:T(8,128)}, f32[640,256]{1,0:T(8,128)}, f32[640,25...) custom-call(bf16[128,128]{1,0:T(8,128)(2,1)} %pad_maximum_fusion.3.k, ...), custom_call_target="tpu_custom_call" | custom-call | flops 15032385536 | bytes 12582912 | tf_op jit(solution)/shard_map/attention/pallas_call | solution.py:632
  176.4 3.6 %fusion.5 = f32[2,128,2048]{2,1,0:T(8,128)S(1)} fusion(bf16[2,8,128,128]{3,2,1,0:T(8,128)(2,1)} %bitcast.54, bf16[2048,8,128]{2,1,0:T(8,128)(2,1)} %param.8), kind=kOutput, calls=%fused_computation.5 | convolution fusion | flops 1073741824 | bytes 6815744 | tf_op jit(solution)/shard_map/cirf,eif->cre/dot_general | solution.py:947
  180.1 0.0 copy-start
  180.1 1.3 copy-done
  181.4 1.0 dynamic-slice_bitcast_fusion
  182.4 0.0 collective-permute-start
  182.5 110.4 %grad_sums.1 = (f32[16384,128]{1,0:T(8,128)}, f32[1024,2048]{1,0:T(8,128)}, f32[2048,128]{1,0:T(8,128)}, f32[2048,128]{1,0:T(8,128)}, bf16[128,256]{1,0:T(8,128)(2,1)}) custom-call(f32[768,256]{1,0:T(8,128)} %get-tuple-element.24.sl0, f32[640,256]{1,0:T(8,128)} %get-tuple-element.25.sl1, f32[640,256]{1,0:T(8,128)} %get-tuple-element.26.sl2, ...), custom_call_target="tpu_custom_call" | custom-call | flops 85899345920 | bytes 41943040 | tf_op jit(solution)/shard_map/grad_sums/pallas_call | solution.py:886
  292.8 1.4 fusion.23
  294.2 0.0 copy-start.2
  294.2 0.0 collective-permute-done
  294.2 2.2 fusion.13
  296.4 6.9 %collective-permute-start.1 = (bf16[128,2048]{1,0:T(8,128)(2,1)S(1)}, bf16[128,2048]{1,0:T(8,128)(2,1)S(1)}, u32[]{:S(2)}, u32[]{:S(2)}) collective-permute-start(bf16[128,2048]{1,0:T(8,128)(2,1)S(1)} %fusion.13), channel_id=1, source_target_pairs={{0,64},{64,0},{1,65},{65,1},{2,66},{66,2},{3,67},{67,3},{4,68},{68... | collective-permute-start | bytes 1572872 | tf_op jit(solution)/shard_map/ppermute | solution.py:927
  303.3 1.5 collective-permute-done.1
  304.8 0.1 select_bitcast_fusion.1
  304.9 1.1 pad_maximum_fusion
  305.9 0.0 copy-done.2
  305.9 0.0 slice-start
  305.9 1.0 copy.49
  306.9 0.0 copy-start.4
  306.9 0.0 copy-start.3
  306.9 0.0 slice-start.1
  306.9 7.8 %copy.50 = f32[2048,8,128]{2,1,0:T(8,128)} copy(f32[2048,8,128]{2,1,0:T(8,128)} %bitcast.47) | data formatting | bytes 16777216
  314.7 0.0 copy-done.4
  314.7 1.0 copy.51
  315.7 0.0 copy-done.3
  315.7 1.0 copy.52
  316.6 0.0 slice-done
  316.6 0.0 slice-done.1
  316.6 3.4 %copy.53 = f32[8,128,2048]{2,1,0:T(8,128)} copy(f32[8,128,2048]{2,1,0:T(8,128)S(1)} %bitcast.46) | data formatting | bytes 16777216
  (4 shorter events, 0.0 us)
Async XLA Ops:
  2.5 4.0 %copy-start.5 = (f32[128,64]{1,0:T(8,128)}, f32[128,64]{1,0:T(8,128)S(1)}, u32[]{:S(2)}) copy-start(f32[128,64]{1,0:T(8,128)S(1)} %get-tuple-element.48.cos_ref) | copy-start | bytes 98308
  2.5 4.0 %copy-start.6 = (f32[128,64]{1,0:T(8,128)}, f32[128,64]{1,0:T(8,128)S(1)}, u32[]{:S(2)}) copy-start(f32[128,64]{1,0:T(8,128)S(1)} %get-tuple-element.49.sin_ref) | copy-start | bytes 98308
  6.5 1.2 copy-start.1
  180.1 1.3 copy-start
  182.4 111.7 %collective-permute-start = (f32[128,2048]{1,0:T(8,128)}, f32[128,2048]{1,0:T(8,128)}, u32[]{:S(2)}, u32[]{:S(2)}) collective-permute-start(f32[128,2048]{1,0:T(8,128)} %dynamic-slice_bitcast_fusion), channel_id=1, source_target_pairs={{0,64},{64,0},{1,65},{65,1},{2,66},{66,2},{3,67},{67,3},{4,68},{68... | collective-permute-start | bytes 3145736 | tf_op jit(solution)/shard_map/ppermute | solution.py:923
  294.2 11.8 %copy-start.2 = (bf16[2,128,2048]{2,1,0:T(8,128)(2,1)S(1)}, bf16[2,128,2048]{2,1,0:T(8,128)(2,1)}, u32[]{:S(2)}) copy-start(bf16[2,128,2048]{2,1,0:T(8,128)(2,1)} %get-tuple-element.62) | copy-start | bytes 3145732
  296.4 8.4 %collective-permute-start.1 = (bf16[128,2048]{1,0:T(8,128)(2,1)S(1)}, bf16[128,2048]{1,0:T(8,128)(2,1)S(1)}, u32[]{:S(2)}, u32[]{:S(2)}) collective-permute-start(bf16[128,2048]{1,0:T(8,128)(2,1)S(1)} %fusion.13), channel_id=1, source_target_pairs={{0,64},{64,0},{1,65},{65,1},{2,66},{66,2},{3,67},{67,3},{4,68},{68... | collective-permute-start | bytes 1572872 | tf_op jit(solution)/shard_map/ppermute | solution.py:927
  305.9 10.7 %slice-start = ((s8[8388608]{0:T(1024)(128)(4,1)}), s8[4194304]{0:T(1024)(128)(4,1)S(1)}, s32[]{:S(2)}) async-start(s8[8388608]{0:T(1024)(128)(4,1)} %bitcast.44), calls=%async_computation | async-start | bytes 8388608
  306.9 7.8 %copy-start.4 = (f32[2048,128]{1,0:T(8,128)S(1)}, f32[2048,128]{1,0:T(8,128)}, u32[]{:S(2)}) copy-start(f32[2048,128]{1,0:T(8,128)} %get-tuple-element.65) | copy-start | bytes 3145732
  306.9 8.7 %copy-start.3 = (f32[2048,128]{1,0:T(8,128)S(1)}, f32[2048,128]{1,0:T(8,128)}, u32[]{:S(2)}) copy-start(f32[2048,128]{1,0:T(8,128)} %get-tuple-element.66) | copy-start | bytes 3145732
  306.9 9.7 %slice-start.1 = ((s8[8388608]{0:T(1024)(128)(4,1)}), s8[4194304]{0:T(1024)(128)(4,1)S(1)}, s32[]{:S(2)}) async-start(s8[8388608]{0:T(1024)(128)(4,1)} %bitcast.44), calls=%async_computation.1 | async-start | bytes 8388608

commit v7 on v6

--- a/solution.py
+++ b/solution.py
@@ -435,8 +435,6 @@
         gr[c][here, :] = grad_cols(c)[...]
     for copy in g_sent:
         copy.start()
-    for copy in h_sent:
-        copy.start()
     lax.fori_loop(0, n_blk, place_kv, 0)
 
     n_first = cp // per_tile + 1
@@ -533,12 +531,10 @@
             for at in range(0, red.shape[1], 128):
                 red[:, at:at + 128] = dot_ta(orr[c][...], gr[c][:, at:at + 128])
         stage(p_r, "rs_start1")
-
-    def step_wo():
-        stage(p_r, "rs_end1")
-        stage(p_r, "rs_start2")
-
-    over_tiles(bwd_step, ((3, send_o), (7, slab_wo), (10, lambda: stage(p_r, "rs_mid1")), (13, step_wo)))
+        for copy in h_sent:
+            copy.start()
+
+    over_tiles(bwd_step, ((3, send_o), (8, slab_wo), (11, lambda: stage(p_r, "rs_mid1"))))
 
     def place_dkv(blk, carry):
         for c in COLOURS:
@@ -549,9 +545,6 @@
 
     lax.fori_loop(0, n_blk, place_dkv, 0)
     stage(p_d, "rs_start0")
-    stage(p_r, "rs_end2")
-    for part, out in zip(p_r, (red0, red1, red2)):
-        out[...] = part.x[pl.ds(pl.multiple_of(part.own_rows(), 8), part.rb), :]
 
     scale = e_dim ** -0.5
     half_dim = e_dim // 2
@@ -563,12 +556,6 @@
             turned = jnp.concatenate([low * cos_t + high * sin_t, high * cos_t - low * sin_t], axis=0) * scale
             rot_scr[grp, cols, :] = turned.T.astype(BF16)
     dq_back.start()
-    for copy in h_sent:
-        copy.wait_recv()
-    h_outs = [pltpu.make_async_copy(hr[c], out, h_out.at[c]) for c, out in enumerate((ho0, ho1, ho2))]
-    for copy in h_outs:
-        copy.start()
-
     tp = lax.axis_index("tp")
     partner = (1 - tp, cp)
     for at in range(0, d_model, D_TILE):
@@ -582,7 +569,14 @@
 
     swap_part = swap(part_scr.at[1 - tp], got_scr, 0)
     swap_part.start()
+    stage(p_r, "rs_end1")
+    stage(p_r, "rs_start2")
     stage(p_d, "rs_mid0")
+    for copy in h_sent:
+        copy.wait_recv()
+    h_outs = [pltpu.make_async_copy(hr[c], out, h_out.at[c]) for c, out in enumerate((ho0, ho1, ho2))]
+    for copy in h_outs:
+        copy.start()
     swap_part.wait()
     out_scr[tp] = (part_scr[tp] + got_scr[...]).astype(BF16)
     swap_out = swap(out_scr.at[tp], out_scr.at[tp], 1)
@@ -597,6 +591,9 @@
     put(dqh_scr, dqh_ref)
     swap_out.wait()
     put(out_scr, out_ref)
+    stage(p_r, "rs_end2")
+    for part, out in zip(p_r, (red0, red1, red2)):
+        out[...] = part.x[pl.ds(pl.multiple_of(part.own_rows(), 8), part.rb), :]
     stage(p_d, "rs_end0")
     for part, out in zip(p_d, (sl0, sl1, sl2)):
         slab, _, _, starts, *_ = part.place(0)

time: 320 us -> 325 us (1.016)
    pallas_call x1, Pallas kernels: 164 us -> 168 us  [attention(): pl.pallas_call(attn_kernel, out_shape=(jax.ShapeDtypeStruct(heads, BF16),...]
where the time goes in v7:
time: 325 us; the launch traced here: 324 us
  Pallas kernels  278 us (86%)
  local copies, waits for them, and re-layouts  17.3 us (5%)
  matrix products  14.5 us (4%)
  starting transfers between devices  7.36 us (2%)
  other arithmetic  4.41 us (1%)
    pallas_call x1, Pallas kernels, attention(): pl.pallas_call(attn_kernel, out_shape=(jax.ShapeDtypeStruct(heads, BF16),...  168 us
    pallas_call x1, Pallas kernels, grad_sums(): pl.pallas_call(grad_kernel, out_shape=(jax.ShapeDtypeStruct((d_model * n_...  110 us
    unnamed x23, local copies, waits for them, and re-layouts  15.4 us
    ppermute x1, starting transfers between devices, sum_over_tp(): other = lax.ppermute(mine, 'tp', partner)  7.35 us
    dot_general x4, matrix products, dot(): return jnp.dot(a, b, preferred_element_type=F32)  6.96 us
  transfers between devices with their start and end apart: 2, of which 1 were waited for; matrix products, arithmetic and copies ran while one was open for 0% of the time, Pallas kernels for 34%

profile of v7, /device:TPU:1, one launch (start us, length us, event | category | flops | bytes accessed | tf_op | source)
XLA Modules:
  0.0 324.4 jit_solution(9005925381438969435)
XLA Ops:
  0.7 1.5 fusion.16
  2.2 0.3 multiply_cosine_fusion
  2.5 0.0 copy-start.5
  2.5 0.0 copy-start.6
  2.5 0.1 copy.24
  2.6 0.1 copy.25
  2.7 3.9 %fusion.8 = f32[2,8,128,128]{2,3,0,1:T(8,128)S(1)} fusion(bf16[2048,8,128,1]{2,1,0,3:T(8,128)(2,1)} %bitcast.52, bf16[2,128,2048]{2,1,0:T(8,128)(2,1)} %param.6), kind=kOutput, calls=%fused_computation.7 | convolution fusion | flops 1073741824 | bytes 6291456 | tf_op jit(solution)/shard_map/bsd,dhe->bhse/dot_general | solution.py:931
  6.5 0.0 copy-done.5
  6.5 0.0 copy-done.6
  6.5 0.0 copy-start.1
  6.6 0.1 multiply_subtract_fusion
  6.7 0.3 copy.26
  7.1 0.3 copy.27
  7.4 0.3 multiply_sine_fusion.2
  7.7 0.0 copy-done.1
  7.7 1.9 convolution_convert_fusion.v_ref
  9.7 1.1 fusion.11.q_ref
  10.8 0.7 pad_maximum_fusion.3.k_ref
  11.5 0.7 pad_maximum_fusion.1
  12.2 168.3 %attention.1 = (bf16[2,1024,128]{2,1,0:T(8,128)(2,1)}, bf16[2,128,2048]{2,1,0:T(8,128)(2,1)}, f32[768,256]{1,0:T(8,128)}, f32[640,256]{1,0:T(8,128)}, f32[640,25...) custom-call(bf16[128,128]{1,0:T(8,128)(2,1)} %pad_maximum_fusion.3.k, ...), custom_call_target="tpu_custom_call" | custom-call | flops 15032385536 | bytes 12582912 | tf_op jit(solution)/shard_map/attention/pallas_call | solution.py:629
  180.5 3.6 %fusion.5 = f32[2,128,2048]{2,1,0:T(8,128)S(1)} fusion(bf16[2,8,128,128]{3,2,1,0:T(8,128)(2,1)} %bitcast.54, bf16[2048,8,128]{2,1,0:T(8,128)(2,1)} %param.8), kind=kOutput, calls=%fused_computation.5 | convolution fusion | flops 1073741824 | bytes 6815744 | tf_op jit(solution)/shard_map/cirf,eif->cre/dot_general | solution.py:944
  184.1 0.0 copy-start
  184.2 1.3 copy-done
  185.5 1.0 dynamic-slice_bitcast_fusion
  186.5 0.0 collective-permute-start
  186.5 110.2 %grad_sums.1 = (f32[16384,128]{1,0:T(8,128)}, f32[1024,2048]{1,0:T(8,128)}, f32[2048,128]{1,0:T(8,128)}, f32[2048,128]{1,0:T(8,128)}, bf16[128,256]{1,0:T(8,128)(2,1)}) custom-call(f32[768,256]{1,0:T(8,128)} %get-tuple-element.24.sl0, f32[640,256]{1,0:T(8,128)} %get-tuple-element.25.sl1, f32[640,256]{1,0:T(8,128)} %get-tuple-element.26.sl2, ...), custom_call_target="tpu_custom_call" | custom-call | flops 85899345920 | bytes 41943040 | tf_op jit(solution)/shard_map/grad_sums/pallas_call | solution.py:883
  296.7 1.4 fusion.23
  298.0 0.0 copy-start.2
  298.1 0.0 collective-permute-done
  298.1 2.2 fusion.13
  300.2 7.4 %collective-permute-start.1 = (bf16[128,2048]{1,0:T(8,128)(2,1)S(1)}, bf16[128,2048]{1,0:T(8,128)(2,1)S(1)}, u32[]{:S(2)}, u32[]{:S(2)}) collective-permute-start(bf16[128,2048]{1,0:T(8,128)(2,1)S(1)} %fusion.13), channel_id=1, source_target_pairs={{0,64},{64,0},{1,65},{65,1},{2,66},{66,2},{3,67},{67,3},{4,68},{68... | collective-permute-start | bytes 1572872 | tf_op jit(solution)/shard_map/ppermute | solution.py:924
  307.6 1.5 collective-permute-done.1
  309.1 0.1 select_bitcast_fusion.1
  309.2 1.1 pad_maximum_fusion
  310.3 0.0 copy-done.2
  310.3 0.0 slice-start
  310.3 1.0 copy.49
  311.2 0.0 copy-start.4
  311.2 0.0 copy-start.3
  311.2 0.0 slice-start.1
  311.3 7.8 %copy.50 = f32[2048,8,128]{2,1,0:T(8,128)} copy(f32[2048,8,128]{2,1,0:T(8,128)} %bitcast.47) | data formatting | bytes 16777216
  319.0 0.0 copy-done.4
  319.0 1.0 copy.51
  320.0 0.0 copy-done.3
  320.0 1.0 copy.52
  321.0 0.0 slice-done
  321.0 0.0 slice-done.1
  321.0 3.4 %copy.53 = f32[8,128,2048]{2,1,0:T(8,128)} copy(f32[8,128,2048]{2,1,0:T(8,128)S(1)} %bitcast.46) | data formatting | bytes 16777216
  (4 shorter events, 0.0 us)
Async XLA Ops:
  2.5 4.0 %copy-start.5 = (f32[128,64]{1,0:T(8,128)}, f32[128,64]{1,0:T(8,128)S(1)}, u32[]{:S(2)}) copy-start(f32[128,64]{1,0:T(8,128)S(1)} %get-tuple-element.48.cos_ref) | copy-start | bytes 98308
  2.5 4.0 %copy-start.6 = (f32[128,64]{1,0:T(8,128)}, f32[128,64]{1,0:T(8,128)S(1)}, u32[]{:S(2)}) copy-start(f32[128,64]{1,0:T(8,128)S(1)} %get-tuple-element.49.sin_ref) | copy-start | bytes 98308
  6.5 1.2 copy-start.1
  184.1 1.3 copy-start
  186.5 111.6 %collective-permute-start = (f32[128,2048]{1,0:T(8,128)}, f32[128,2048]{1,0:T(8,128)}, u32[]{:S(2)}, u32[]{:S(2)}) collective-permute-start(f32[128,2048]{1,0:T(8,128)} %dynamic-slice_bitcast_fusion), channel_id=1, source_target_pairs={{0,64},{64,0},{1,65},{65,1},{2,66},{66,2},{3,67},{67,3},{4,68},{68... | collective-permute-start | bytes 3145736 | tf_op jit(solution)/shard_map/ppermute | solution.py:920
  298.0 12.2 %copy-start.2 = (bf16[2,128,2048]{2,1,0:T(8,128)(2,1)S(1)}, bf16[2,128,2048]{2,1,0:T(8,128)(2,1)}, u32[]{:S(2)}) copy-start(bf16[2,128,2048]{2,1,0:T(8,128)(2,1)} %get-tuple-element.62) | copy-start | bytes 3145732
  300.2 8.9 %collective-permute-start.1 = (bf16[128,2048]{1,0:T(8,128)(2,1)S(1)}, bf16[128,2048]{1,0:T(8,128)(2,1)S(1)}, u32[]{:S(2)}, u32[]{:S(2)}) collective-permute-start(bf16[128,2048]{1,0:T(8,128)(2,1)S(1)} %fusion.13), channel_id=1, source_target_pairs={{0,64},{64,0},{1,65},{65,1},{2,66},{66,2},{3,67},{67,3},{4,68},{68... | collective-permute-start | bytes 1572872 | tf_op jit(solution)/shard_map/ppermute | solution.py:924
  310.3 10.7 %slice-start = ((s8[8388608]{0:T(1024)(128)(4,1)}), s8[4194304]{0:T(1024)(128)(4,1)S(1)}, s32[]{:S(2)}) async-start(s8[8388608]{0:T(1024)(128)(4,1)} %bitcast.44), calls=%async_computation | async-start | bytes 8388608
  311.2 7.8 %copy-start.4 = (f32[2048,128]{1,0:T(8,128)S(1)}, f32[2048,128]{1,0:T(8,128)}, u32[]{:S(2)}) copy-start(f32[2048,128]{1,0:T(8,128)} %get-tuple-element.65) | copy-start | bytes 3145732
  311.2 8.7 %copy-start.3 = (f32[2048,128]{1,0:T(8,128)S(1)}, f32[2048,128]{1,0:T(8,128)}, u32[]{:S(2)}) copy-start(f32[2048,128]{1,0:T(8,128)} %get-tuple-element.66) | copy-start | bytes 3145732
  311.2 9.7 %slice-start.1 = ((s8[8388608]{0:T(1024)(128)(4,1)}), s8[4194304]{0:T(1024)(128)(4,1)S(1)}, s32[]{:S(2)}) async-start(s8[8388608]{0:T(1024)(128)(4,1)} %bitcast.44), calls=%async_computation.1 | async-start | bytes 8388608
